TPU v7x, 256 devices: a whole 4x4x8 slice. The times are simulated.
256 devices in a mesh: gx: 4 (over z_lo), gy: 16 (over z_hi, y, core), gz: 4 (over x).
Axes of the slice: x: 4, y: 4, z: 8 (z_hi: 2, z_lo: 4; z = z_hi * 4 + z_lo), core: 2. Of those that a mesh axis runs over, the one named last changes fastest.
Arguments:
- positions: float32 [3, 1048576], P(None, ('gx', 'gy', 'gz'))
- velocities: float32 [3, 1048576], P(None, ('gx', 'gy', 'gz')), may hold values from -6 to 6
- forces_old: float32 [3, 1048576], P(None, ('gx', 'gy', 'gz')), may hold values from -6 to 6
- inv_mass: float32 [1048576], P(('gx', 'gy', 'gz')), may hold values from 0.25 to 4
- charges: float32 [1048576], P(('gx', 'gy', 'gz')), may hold values from -3 to 3
- block_species: int32 [8192], P(('gx', 'gy', 'gz')), may hold values from 0 to 3
- sigma_table: float32 [4], replicated, may hold values from 0.25 to 0.5
- epsilon_table: float32 [4], replicated, may hold values from 0.02 to 0.2
- tower_index: int32 [256, 64], P(('gx', 'gy', 'gz')), may hold values from 0 to 127
- plate_index: int32 [256, 64], P(('gx', 'gy', 'gz')), may hold values from 0 to 287
- tile_counts: int32 [256], P(('gx', 'gy', 'gz')), may hold values from 1 to 64, as said below
- exclusions: int32 [256, 64, 16, 128], P(('gx', 'gy', 'gz')), may hold values from 0 to 255, as said below
- mig_block: int32 [256, 4], P(('gx', 'gy', 'gz')), may hold values from 0 to 31, as said below
- mig_dest: int32 [256, 4], P(('gx', 'gy', 'gz')), may hold values from 0 to 8, as said below
Outputs:
- positions_new: float32 [3, 1048576], P(None, ('gx', 'gy', 'gz'))
- velocities_new: float32 [3, 1048576], P(None, ('gx', 'gy', 'gz'))
- forces_new: float32 [3, 1048576], P(None, ('gx', 'gy', 'gz'))
- arrivals: float32 [6, 256, 8, 512], P(None, ('gx', 'gy', 'gz'))
Inputs may be any that keep to these rules, and one draw needn't show every extreme that they name: `tile_counts`: at most 64 for every box, and exactly 64 for some box; slots at or after a box's count carry no weight. `exclusions`: each of the low eight bits marks one excluded atom pair. `mig_block`: the 4 entries of one box are distinct. `mig_dest`: never 4.
All inputs are finite; a program needn't handle non-finite values.
Results may differ from a plain program's by a relative error of at most 0.0003.
Values sent between devices are 32-bit elements; how exact they have to be, the bound alone decides.
No kernel may reach another device: no remote copies, remote signals or barrier semaphores. Data moves between devices by JAX's collectives and lax.ppermute only.
A program may use at most 64 MiB of HBM per device.

v0:
```python
import functools

import jax
import jax.numpy as jnp
from jax import lax
from jax.experimental import pallas as pl
from jax.experimental.pallas import tpu as pltpu
from jax.sharding import PartitionSpec as P


time_step = 0.2
soft_core = 0.09
cutoff_sq = 1.44
coulomb_k = 0.5
lanes = 128
sources = ((0, 0), (0, 1), (0, 2), (1, 0), (1, 2), (2, 0), (2, 1), (2, 2))
group = 4
VMEM_LIMIT = 24 * 1024 * 1024


def pairs_first(count):
    return [(i, i + 1) for i in range(0, count, 2)]


def pairs_second(count):
    return [(i, (i + 1) % count) for i in range(1, count, 2)]


def far_pairs(count):
    return [(count // 2 - 1, count // 2), (count - 1, 0)]


def swap(value, axis, pairs):
    return lax.ppermute(value, axis, [*pairs, *((j, i) for i, j in pairs)])


def swap_in_far_rows(value, pairs):
    count = lax.axis_size("gy")
    rows = sorted(y for pair in far_pairs(count) for y in pair)
    return swap(
        value, ("gx", "gy"), [(i * count + y, j * count + y) for i, j in pairs for y in rows]
    )


def halo(value):
    count_x, count_y = lax.axis_size("gx"), lax.axis_size("gy")
    first_x, second_x = pairs_first(count_x), pairs_second(count_x)
    far_y = far_pairs(count_y)
    near_y = [pair for pair in pairs_second(count_y) if pair not in far_y]
    across = swap(value, "gy", far_y)
    own = jnp.stack([swap(value, "gx", first_x), value, swap(value, "gx", second_x)])
    first = swap(own, "gy", pairs_first(count_y))
    second = swap(own, "gy", near_y)
    far = (swap_in_far_rows(across, first_x),
        across,
        swap_in_far_rows(across, second_x),
    )
    return (first, own, second), far


def sent_home(first, own, second):
    count_x, count_y = lax.axis_size("gx"), lax.axis_size("gy")
    first_x, second_x = pairs_first(count_x), pairs_second(count_x)
    far_y = far_pairs(count_y)
    near_y = [pair for pair in pairs_second(count_y) if pair not in far_y]
    side_one = swap_in_far_rows(second[0], first_x)
    side_two = swap_in_far_rows(second[2], second_x)
    across = swap(second[1] + side_one + side_two, "gy", far_y)
    row = own + swap(first, "gy", pairs_first(count_y)) + swap(second, "gy", near_y)
    return row[1] + swap(row[0], "gx", first_x) + swap(row[2], "gx", second_x) + across


def piece_of(offset, odd):
    return jnp.where(offset == 1, 1, jnp.where(offset == 2 * odd, 2, 0))


def vmem():
    return pl.BlockSpec(memory_space=pltpu.VMEM)


def smem():
    return pl.BlockSpec(memory_space=pltpu.SMEM)


def exact_parts(value):
    high = value.astype(jnp.bfloat16).astype(jnp.float32)
    rest = value - high
    middle = rest.astype(jnp.bfloat16).astype(jnp.float32)
    return high, middle, rest - middle


def pair_kernel(
    length_x,
    length_y,
    unroll,
    tower_list,
    plate_list,
    count,
    spot,
    *refs,
):
    tower_refs, (first_row, own_row, second_row), far_refs = refs[0:4], refs[4:7], refs[7:10]
    masks, tower_outs, row_outs, held = refs[10], refs[11:15], refs[15:18], refs[18:]
    blocks = tower_outs[0].shape[0]
    for ref in (*tower_outs, *row_outs):
        ref[...] = jnp.zeros_like(ref)
    odd_x, odd_y, far, me_z = (spot[n] for n in range(4))
    f32 = jnp.float32
    row4 = lax.broadcasted_iota(jnp.int32, (4, lanes), 0)
    lane4 = lax.broadcasted_iota(jnp.int32, (4, lanes), 1)
    sub = lax.broadcasted_iota(jnp.int32, (8, lanes), 0)
    lane = lax.broadcasted_iota(jnp.int32, (8, lanes), 1)
    lane_group = lane // 8
    on_diagonal = sub == lane % 8
    bit = jnp.left_shift(jnp.int32(1), sub)
    scale = jnp.where(
        row4 == 0,
        1.0 / length_x,
        jnp.where(row4 == 1, 1.0 / length_y, jnp.where(row4 == 2, 1.0 / length_x, 1.0)),
    ).astype(f32)
    ratio = (length_y / length_x) ** 2
    unit_sq = length_x * length_x
    soft = soft_core / unit_sq
    fall = unit_sq / cutoff_sq
    tower_scale = jnp.where(row4 == 3, coulomb_k / length_x, scale).astype(f32)
    back = jnp.where(
        row4 == 0,
        length_x / unit_sq,
        jnp.where(row4 == 1, length_y / unit_sq, length_x / unit_sq),
    ).astype(f32)
    pick = jnp.concatenate(
        [
            jnp.where(
                jnp.logical_and(
                    lax.broadcasted_iota(jnp.int32, (16, lanes), 0) % 4 == c,
                    lax.broadcasted_iota(jnp.int32, (16, lanes), 0) < 12,
                ),
                1.0,
                0.0,
            ).astype(f32)
            for c in range(4)
        ],
        axis=1,
    ).astype(jnp.bfloat16)
    total = count[0]

    def place(slot):
        tower, plate = tower_list[0, slot], plate_list[0, slot]
        cell = plate // blocks
        return (
            jnp.bitwise_xor(tower // blocks, me_z),
            tower % blocks,
            piece_of(cell // 3, odd_x),
            piece_of(cell % 3, odd_y),
            plate % blocks,
        )

    def tower_tile(layer, row):
        near = jnp.where(layer == 0, tower_refs[0][row], tower_refs[1][row])
        return jnp.where(
            layer < 2, near, jnp.where(layer == 2, tower_refs[2][row], tower_refs[3][row])
        )

    last = tower_list.shape[1] - 1

    def prepare(slot, buffer, u):
        spread_ref, terms_ref = buffer
        layer, tower_block, cell_x, cell_y, plate_block = place(jnp.minimum(slot, last))
        tower_kind = tower_tile(layer, blocks)

        def chosen(row):
            from_far = jnp.where(
                cell_x == 0,
                far_refs[0][row],
                jnp.where(cell_x == 1, far_refs[1][row], far_refs[2][row]),
            )
            second = jnp.where(far == 1, from_far, second_row[cell_x, row])
            return jnp.where(
                cell_y == 0,
                first_row[cell_x, row],
                jnp.where(cell_y == 1, own_row[cell_x, row], second),
            )

        plate_rows = chosen(plate_block) * scale
        plate_kind = chosen(blocks)
        of_tower = jnp.sum(
            jnp.where(lane4 == tower_block, tower_kind, 0.0), axis=1, keepdims=True
        )
        of_plate = jnp.sum(
            jnp.where(lane4 == plate_block, plate_kind, 0.0), axis=1, keepdims=True
        )
        sigma = 0.5 * (of_tower[0:1] + of_plate[0:1])
        depth = of_tower[1:2] * of_plate[1:2]
        sigma_sq = sigma * sigma * (1.0 / unit_sq)
        sigma_six = sigma_sq * sigma_sq * sigma_sq
        low = jnp.broadcast_to(6.0 * depth * sigma_six, (8, lanes))
        high = jnp.broadcast_to(12.0 * depth * sigma_six * sigma_six, (8, lanes))
        parts = jnp.concatenate([*exact_parts(plate_rows), jnp.zeros_like(plate_rows)], axis=0)
        spread_ref[u] = lax.dot_general(
            parts.astype(jnp.bfloat16),
            pick,
            (((0,), (0,)), ((), ())),
            preferred_element_type=f32,
        )
        terms_ref[u, 0] = low
        terms_ref[u, 1] = high

    def evaluate(slot, buffer, u):
        spread_ref, terms_ref = buffer
        layer, tower_block, cell_x, cell_y, plate_block = place(slot)
        tower_rows = tower_tile(layer, tower_block) * tower_scale
        low, high = terms_ref[u, 0], terms_ref[u, 1]
        rows = [jnp.broadcast_to(tower_rows[c : c + 1], (8, lanes)) for c in range(4)]
        words = masks[slot]
        on_tower = [jnp.zeros((8, lanes), f32) for _ in range(3)]
        on_plate = [jnp.zeros((8, lanes), f32) for _ in range(3)]
        for w in range(lanes // 8):
            piece = [
                spread_ref[u, 8 * w : 8 * w + 8, lanes * c : lanes * c + lanes]
                for c in range(4)
            ]
            raw_x, raw_y, dz = (rows[c] - piece[c] for c in range(3))
            dx = raw_x - jnp.round(raw_x)
            dy = raw_y - jnp.round(raw_y)
            dist = dx * dx + ratio * (dy * dy) + dz * dz
            root = lax.rsqrt(dist + soft)
            inverse = root * root
            cube = inverse * inverse * inverse
            falloff = 1.0 - fall * dist
            word = jnp.broadcast_to(words[w : w + 1], (8, lanes))
            falloff = jnp.where(jnp.bitwise_and(word, bit) == 0, falloff, 0.0)
            falloff = jnp.maximum(falloff, 0.0) * root
            energy = cube * (high * cube - low) + rows[3] * piece[3] * root
            strength = energy * (falloff * falloff)
            for c, offset in enumerate((dx, dy, dz)):
                weighted = strength * offset
                on_tower[c] += weighted
                on_plate[c] = jnp.where(
                    lane_group == w, jnp.sum(weighted, axis=1, keepdims=True), on_plate[c]
                )
        listed = jnp.where(slot < total, 1.0, 0.0).astype(f32)
        zero = jnp.zeros((1, lanes), f32)
        tower_sum = jnp.concatenate(
            [*(jnp.sum(v, axis=0, keepdims=True) for v in on_tower), zero], axis=0
        )
        plate_sum = jnp.concatenate(
            [
                *(
                    jnp.sum(jnp.where(on_diagonal, v, 0.0), axis=0, keepdims=True)
                    for v in on_plate
                ),
                zero,
            ],
            axis=0,
        )
        factor = back * listed
        return (
            (layer, tower_block, tower_sum * factor),
            (cell_x, cell_y, plate_block, plate_sum * -factor),
        )

    def finish(done):
        for (layer, tower_block, on_tower), (cell_x, cell_y, plate_block, on_plate) in done:
            for z, ref in enumerate(tower_outs):
                ref[tower_block] += jnp.where(layer == z, on_tower, 0.0)
            for y, ref in enumerate(row_outs):
                ref[cell_x, plate_block] += jnp.where(cell_y == y, on_plate, 0.0)

    buffers = (held[0:2], held[2:4])

    def step(index, carry):
        done = []
        for half in range(2):
            first = (2 * index + half) * unroll
            for u in range(unroll):
                prepare(first + unroll + u, buffers[1 - half], u)
            done += [evaluate(first + u, buffers[half], u) for u in range(unroll)]
        finish(done)
        return carry

    for u in range(unroll):
        prepare(u, buffers[0], u)
    lax.fori_loop(0, (total + 2 * unroll - 1) // (2 * unroll), step, 0)


def pair_forces(tower_list, plate_list, count, spot, towers, rows, far, masks, lengths):
    blocks = towers[0].shape[0] - 1
    shape_one = jax.ShapeDtypeStruct((blocks, 4, lanes), jnp.float32)
    shape_row = jax.ShapeDtypeStruct((3, blocks, 4, lanes), jnp.float32)
    return pl.pallas_call(
        functools.partial(pair_kernel, *lengths, group),
        out_shape=[shape_one] * 4 + [shape_row] * 3,
        in_specs=[smem()] * 4 + [vmem()] * 11,
        out_specs=[vmem()] * 7,
        scratch_shapes=[
            pltpu.VMEM((group, lanes, 4 * lanes), jnp.float32),
            pltpu.VMEM((group, 2, 8, lanes), jnp.float32),
        ]
        * 2,
        compiler_params=pltpu.CompilerParams(vmem_limit_bytes=VMEM_LIMIT),
        cost_estimate=pl.CostEstimate(
            flops=40 * 64 * lanes * lanes, bytes_accessed=2**21, transcendentals=64 * lanes * lanes
        ),
        name="pair_forces",
    )(tower_list, plate_list, count, spot, *towers, *rows, *far, masks)


def arrival_kernel(spot, *refs):
    (first_row, own_row, second_row), far_refs, out = refs[0:3], refs[3:6], refs[6]
    odd_x, odd_y, far = spot[0], spot[1], spot[2]
    for q in range(own_row.shape[1]):
        second = [jnp.where(far == 1, far_refs[k][q], second_row[k, q]) for k in range(3)]
        first = [first_row[k, q] for k in range(3)]
        own = [own_row[k, q] for k in range(3)]
        for number, (x, y) in enumerate(sources):
            wanted = float((2 - x) * 3 + (2 - y))
            by_y = own
            if y != 1:
                flip = odd_y == (1 if y == 0 else 0)
                by_y = [jnp.where(flip, first[k], second[k]) for k in range(3)]
            state = by_y[1]
            if x != 1:
                flip = odd_x == (1 if x == 0 else 0)
                state = jnp.where(flip, by_y[0], by_y[2])
            kept = jnp.where(state[6:7] == wanted, state, 0.0)
            for c in range(6):
                out[c, number : number + 1, lanes * q : lanes * q + lanes] = kept[c : c + 1]


def arrivals_of(spot, rows, far):
    leaving = rows[0].shape[1]
    return pl.pallas_call(
        arrival_kernel,
        out_shape=jax.ShapeDtypeStruct((6, 8, leaving * lanes), jnp.float32),
        in_specs=[smem()] + [vmem()] * 6,
        out_specs=vmem(),
        compiler_params=pltpu.CompilerParams(vmem_limit_bytes=VMEM_LIMIT),
        name="arrivals",
    )(spot, *rows, *far)


def by_block(rows):
    return rows.reshape(rows.shape[0], -1, lanes).transpose(1, 0, 2)


def by_atom(tiles):
    return tiles.transpose(1, 0, 2).reshape(tiles.shape[1], -1)


def local(
    positions,
    velocities,
    forces_old,
    inv_mass,
    charges,
    block_species,
    sigma_table,
    epsilon_table,
    tower_index,
    plate_index,
    tile_counts,
    exclusions,
    mig_block,
    mig_dest,
):
    block_count = block_species.shape[0]
    layers = lax.axis_size("gz")
    length_x = float(lax.axis_size("gx"))
    length_y = float(lax.axis_size("gy"))
    half_kick = velocities + 0.5 * time_step * forces_old * inv_mass[None, :]
    moved = positions + time_step * half_kick
    kinds = jnp.stack([sigma_table, jnp.sqrt(epsilon_table)])
    per_block = jnp.zeros((2, block_count), jnp.float32)
    for kind in range(sigma_table.shape[0]):
        per_block = jnp.where(block_species[None, :] == kind, kinds[:, kind : kind + 1], per_block)
    kind_tile = jnp.pad(per_block, ((0, 2), (0, lanes - block_count)))
    features = jnp.concatenate(
        [by_block(jnp.concatenate([moved, charges[None, :]])), kind_tile[None]]
    )
    count_y = lax.axis_size("gy")
    me_x, me_y, me_z = (lax.axis_index(axis) for axis in ("gx", "gy", "gz"))
    is_far = functools.reduce(
        jnp.logical_or, [me_y == y for pair in far_pairs(count_y) for y in pair]
    )
    spot = jnp.stack([me_x % 2, me_y % 2, is_far.astype(jnp.int32), me_z]).astype(jnp.int32)
    rows, far = halo(features)

    def from_layer(value, step):
        return lax.ppermute(value, "gz", [(i, i ^ step) for i in range(layers)])

    towers = [features] + [from_layer(features, step) for step in range(1, layers)]
    sums = pair_forces(
        tower_index,
        plate_index,
        tile_counts,
        spot,
        towers,
        rows,
        far,
        exclusions[0],
        (length_x, length_y),
    )
    tower_back = sums[0] + sum(from_layer(sums[step], step) for step in range(1, layers))
    total = tower_back + sent_home(*sums[layers:])
    forces_new = by_atom(total[:, 0:3])
    velocity_full = half_kick + 0.5 * time_step * forces_new * inv_mass[None, :]
    leaving = mig_block[0]
    block_slots = jnp.arange(block_count, dtype=jnp.int32)
    departed = jnp.any(leaving[:, None] == block_slots[None, :], axis=0)
    staying = jnp.repeat(1.0 - departed.astype(jnp.float32), lanes)[None, :]
    positions_new = moved * staying
    velocities_new = velocity_full * staying
    tags = jnp.broadcast_to(
        mig_dest[0].astype(jnp.float32)[:, None, None], (leaving.shape[0], 2, lanes)
    )
    state = by_block(jnp.concatenate([moved, velocity_full]))
    state = jnp.concatenate([jnp.take(state, leaving, axis=0), tags], axis=1)
    arrivals = arrivals_of(spot, *halo(state))[:, None]
    return (positions_new, velocities_new, forces_new, arrivals)


def solution(mesh):
    everywhere = ("gx", "gy", "gz")
    in_specs = (
        P(None, everywhere),
        P(None, everywhere),
        P(None, everywhere),
        P(everywhere),
        P(everywhere),
        P(everywhere),
        P(),
        P(),
        P(everywhere, None),
        P(everywhere, None),
        P(everywhere),
        P(everywhere, None, None, None),
        P(everywhere, None),
        P(everywhere, None),
    )
    out_specs = (
        P(None, everywhere),
        P(None, everywhere),
        P(None, everywhere),
        P(None, everywhere, None, None),
    )
    return jax.shard_map(local, mesh=mesh, in_specs=in_specs, out_specs=out_specs, check_vma=False)
```

profile of v0, /device:TPU:2, one launch (start us, length us, event | category | flops | bytes accessed | tf_op | source)
XLA Modules:
  0.0 97.6 jit_solution(801490284548775943)
XLA Ops:
  0.7 0.6 copy-done.7
  1.3 0.1 fusion.3
  1.4 0.1 broadcast_bitcast_fusion
  1.5 0.7 broadcast_compare_fusion.3
  2.1 0.7 sqrt_bitcast_fusion
  2.8 0.7 pad_maximum_fusion.4
  3.5 0.2 slice_reduce_fusion
  3.7 0.1 select_select_fusion
  3.8 1.6 %broadcast_multiply_fusion.1 = (f32[3,4096]{1,0:T(4,128)}, f32[3,4096]{1,0:T(4,128)S(1)}) fusion(f32[4096]{0:T(1024)S(1)} %broadcast_bitcast_fusion, f32[3,4096]{1,0:T(4,128)} %param.14, f32[3,4096]{1,0:T(4,128)S(1)} %copy-done.3, f32[3,4096]{1,0:T(4,128)} %param.16, f32[4096]{0:T(1024)S(1)} %broadcast_multiply_fusion.2), kind=kLoop, calls=%fused_computation.26 | loop fusion | flops 61440 | bytes 278528 | tf_op jit(solution)/shard_map/mul | solution.py:411
  5.5 2.3 %collective-permute-start = (f32[33,4,128]{2,1,0:T(4,128)S(1)}, f32[33,4,128]{2,1,0:T(4,128)S(1)}, u32[]{:S(2)}, u32[]{:S(2)}) collective-permute-start(f32[33,4,128]{2,1,0:T(4,128)S(1)} %get-tuple-element.45.refs_0_), channel_id=1, source_target_pairs={{0,1},{1,0},{2,3},{3,2},{4,5},{5,4},{6,7},{7,6},{8,9},{9,8},{10,11... | collective-permute-start | bytes 202760 | tf_op jit(solution)/shard_map/ppermute | solution.py:389
  7.8 0.7 collective-permute-start.1
  8.5 4.6 %collective-permute-start.4 = (f32[33,4,128]{2,1,0:T(4,128)S(1)}, f32[33,4,128]{2,1,0:T(4,128)S(1)}, u32[]{:S(2)}, u32[]{:S(2)}) collective-permute-start(f32[33,4,128]{2,1,0:T(4,128)S(1)} %get-tuple-element.45.refs_0_), channel_id=1, source_target_pairs={{64,128},{192,0},{128,64},{0,192},{65,129},{193,1},{129,65},{1,193... | collective-permute-start | bytes 202760 | tf_op jit(solution)/shard_map/ppermute | solution.py:34
  13.1 7.4 %collective-permute-start.7 = (f32[33,4,128]{2,1,0:T(4,128)S(1)}, f32[33,4,128]{2,1,0:T(4,128)S(1)}, u32[]{:S(2)}, u32[]{:S(2)}) collective-permute-start(f32[33,4,128]{2,1,0:T(4,128)S(1)} %get-tuple-element.45.refs_0_), channel_id=1, source_target_pairs={{28,32},{60,0},{32,28},{0,60},{29,33},{61,1},{33,29},{1,61},{30,34... | collective-permute-start | bytes 202760 | tf_op jit(solution)/shard_map/ppermute | solution.py:34
  20.7 0.1 collective-permute-start.5
  20.8 0.7 collective-permute-start.6
  22.1 0.6 collective-permute-start.2
  22.8 2.0 %collective-permute-done.7.refs_8_ = f32[33,4,128]{2,1,0:T(4,128)S(1)} collective-permute-done((f32[33,4,128]{2,1,0:T(4,128)S(1)}, f32[33,4,128]{2,1,0:T(4,128)S(1)}, u32[]{:S(2)}, u32[]{:S(2)}) %collective-permute-start.7) | collective-permute-done | bytes 67616 | tf_op jit(solution)/shard_map/ppermute | solution.py:34
  24.7 3.9 %collective-permute-start.8 = (f32[33,4,128]{2,1,0:T(4,128)S(1)}, f32[33,4,128]{2,1,0:T(4,128)S(1)}, u32[]{:S(2)}, u32[]{:S(2)}) collective-permute-start(f32[33,4,128]{2,1,0:T(4,128)S(1)} %collective-permute-done.7.refs_8_), channel_id=1, source_target_pairs={{0,64},{28,92},{32,96},{60,124},{128,192},{156,220},{160,224},{188... | collective-permute-start | bytes 202760 | tf_op jit(solution)/shard_map/ppermute | solution.py:34
  28.7 2.9 %collective-permute-start.9 = (f32[33,4,128]{2,1,0:T(4,128)S(1)}, f32[33,4,128]{2,1,0:T(4,128)S(1)}, u32[]{:S(2)}, u32[]{:S(2)}) collective-permute-start(f32[33,4,128]{2,1,0:T(4,128)S(1)} %collective-permute-done.7.refs_8_), channel_id=1, source_target_pairs={{64,128},{92,156},{96,160},{124,188},{192,0},{220,28},{224,32},{25... | collective-permute-start | bytes 202760 | tf_op jit(solution)/shard_map/ppermute | solution.py:34
  31.5 0.1 pad_add_fusion.spot
  31.6 5.0 %collective-permute-done.9.refs_9_ = f32[33,4,128]{2,1,0:T(4,128)S(1)} collective-permute-done((f32[33,4,128]{2,1,0:T(4,128)S(1)}, f32[33,4,128]{2,1,0:T(4,128)S(1)}, u32[]{:S(2)}, u32[]{:S(2)}) %collective-permute-start.9) | collective-permute-done | bytes 67616 | tf_op jit(solution)/shard_map/ppermute | solution.py:34
  36.7 3.5 %pair_forces.1 = (f32[32,4,128]{2,1,0:T(4,128)S(1)}, f32[32,4,128]{2,1,0:T(4,128)S(1)}, f32[32,4,128]{2,1,0:T(4,128)S(1)}, f32[32,4,128]{2,1,0:T(4,128)S(1)}, f3...) custom-call(s32[1,64]{1,0:T(1,128)S(1)} %copy-done.1, ...), custom_call_target="tpu_custom_call" | custom-call | flops 41943040 | bytes 2097152 | tf_op jit(solution)/shard_map/pair_forces/pallas_call | solution.py:290
  40.2 1.9 %collective-permute-start.18 = (f32[32,4,128]{2,1,0:T(4,128)S(1)}, f32[32,4,128]{2,1,0:T(4,128)S(1)}, u32[]{:S(2)}, u32[]{:S(2)}) collective-permute-start(f32[32,4,128]{2,1,0:T(4,128)S(1)} %get-tuple-element.43), channel_id=1, source_target_pairs={{64,128},{92,156},{96,160},{124,188},{192,0},{220,28},{224,32},{25... | collective-permute-start | bytes 196616 | tf_op jit(solution)/shard_map/ppermute | solution.py:34
  42.2 1.9 %collective-permute-start.17 = (f32[32,4,128]{2,1,0:T(4,128)S(1)}, f32[32,4,128]{2,1,0:T(4,128)S(1)}, u32[]{:S(2)}, u32[]{:S(2)}) collective-permute-start(f32[32,4,128]{2,1,0:T(4,128)S(1)} %get-tuple-element.42), channel_id=1, source_target_pairs={{0,64},{28,92},{32,96},{60,124},{128,192},{156,220},{160,224},{188... | collective-permute-start | bytes 196616 | tf_op jit(solution)/shard_map/ppermute | solution.py:34
  44.1 0.7 collective-permute-start.14
  44.8 0.1 collective-permute-start.13
  44.9 4.1 %collective-permute-start.12 = (f32[32,4,128]{2,1,0:T(4,128)S(1)}, f32[32,4,128]{2,1,0:T(4,128)S(1)}, u32[]{:S(2)}, u32[]{:S(2)}) collective-permute-start(f32[32,4,128]{2,1,0:T(4,128)S(1)} %get-tuple-element.14), channel_id=1, source_target_pairs={{0,3},{1,2},{2,1},{3,0},{4,7},{5,6},{6,5},{7,4},{8,11},{9,10},{10,... | collective-permute-start | bytes 196616 | tf_op jit(solution)/shard_map/ppermute | solution.py:389
  49.0 5.4 %collective-permute-start.11 = (f32[32,4,128]{2,1,0:T(4,128)S(1)}, f32[32,4,128]{2,1,0:T(4,128)S(1)}, u32[]{:S(2)}, u32[]{:S(2)}) collective-permute-start(f32[32,4,128]{2,1,0:T(4,128)S(1)} %get-tuple-element.13), channel_id=1, source_target_pairs={{0,2},{1,3},{2,0},{3,1},{4,6},{5,7},{6,4},{7,5},{8,10},{9,11},{10,... | collective-permute-start | bytes 196616 | tf_op jit(solution)/shard_map/ppermute | solution.py:389
  54.3 1.2 %collective-permute-start.10 = (f32[32,4,128]{2,1,0:T(4,128)S(1)}, f32[32,4,128]{2,1,0:T(4,128)S(1)}, u32[]{:S(2)}, u32[]{:S(2)}) collective-permute-start(f32[32,4,128]{2,1,0:T(4,128)S(1)} %get-tuple-element.12), channel_id=1, source_target_pairs={{0,1},{1,0},{2,3},{3,2},{4,5},{5,4},{6,7},{7,6},{8,9},{9,8},{10,11... | collective-permute-start | bytes 196616 | tf_op jit(solution)/shard_map/ppermute | solution.py:389
  55.5 3.8 %collective-permute-start.19 = (f32[32,4,128]{2,1,0:T(4,128)S(1)}, f32[32,4,128]{2,1,0:T(4,128)S(1)}, u32[]{:S(2)}, u32[]{:S(2)}) collective-permute-start(f32[32,4,128]{2,1,0:T(4,128)S(1)} %fusion.2), channel_id=1, source_target_pairs={{28,32},{60,0},{32,28},{0,60},{29,33},{61,1},{33,29},{1,61},{30,34... | collective-permute-start | bytes 196616 | tf_op jit(solution)/shard_map/ppermute | solution.py:34
  59.4 0.9 collective-permute-start.16
  60.4 0.6 collective-permute-start.15
  61.0 6.1 %collective-permute-done.19 = f32[32,4,128]{2,1,0:T(4,128)S(1)} collective-permute-done((f32[32,4,128]{2,1,0:T(4,128)S(1)}, f32[32,4,128]{2,1,0:T(4,128)S(1)}, u32[]{:S(2)}, u32[]{:S(2)}) %collective-permute-start.19) | collective-permute-done | bytes 65568 | tf_op jit(solution)/shard_map/ppermute | solution.py:34
  67.1 0.8 broadcast_multiply_fusion
  67.9 0.6 gather_fusion
  68.5 0.1 broadcast_select_fusion
  68.5 0.1 broadcast_in_dim.107
  68.6 2.2 %collective-permute-start.21 = (f32[4,8,128]{2,1,0:T(8,128)S(1)}, f32[4,8,128]{2,1,0:T(8,128)S(1)}, u32[]{:S(2)}, u32[]{:S(2)}) collective-permute-start(f32[4,8,128]{2,1,0:T(8,128)S(1)} %get-tuple-element.47), channel_id=1, source_target_pairs={{64,128},{192,0},{128,64},{0,192},{65,129},{193,1},{129,65},{1,193... | collective-permute-start | bytes 49160 | tf_op jit(solution)/shard_map/ppermute | solution.py:34
  70.8 0.7 collective-permute-start.20
  71.5 2.7 %collective-permute-done.21 = f32[4,8,128]{2,1,0:T(8,128)S(1)} collective-permute-done((f32[4,8,128]{2,1,0:T(8,128)S(1)}, f32[4,8,128]{2,1,0:T(8,128)S(1)}, u32[]{:S(2)}, u32[]{:S(2)}) %collective-permute-start.21) | collective-permute-done | bytes 16416 | tf_op jit(solution)/shard_map/ppermute | solution.py:34
  74.3 0.3 collective-permute-done.20
  74.6 0.7 collective-permute-start.23
  75.3 4.6 %collective-permute-start.24 = (f32[4,8,128]{2,1,0:T(8,128)S(1)}, f32[4,8,128]{2,1,0:T(8,128)S(1)}, u32[]{:S(2)}, u32[]{:S(2)}) collective-permute-start(f32[4,8,128]{2,1,0:T(8,128)S(1)} %get-tuple-element.47), channel_id=1, source_target_pairs={{28,32},{60,0},{32,28},{0,60},{29,33},{61,1},{33,29},{1,61},{30,34... | collective-permute-start | bytes 49160 | tf_op jit(solution)/shard_map/ppermute | solution.py:34
  79.9 6.4 %collective-permute-done.24.refs_4_ = f32[4,8,128]{2,1,0:T(8,128)S(1)} collective-permute-done((f32[4,8,128]{2,1,0:T(8,128)S(1)}, f32[4,8,128]{2,1,0:T(8,128)S(1)}, u32[]{:S(2)}, u32[]{:S(2)}) %collective-permute-start.24) | collective-permute-done | bytes 16416 | tf_op jit(solution)/shard_map/ppermute | solution.py:34
  86.3 2.6 %collective-permute-start.25 = (f32[4,8,128]{2,1,0:T(8,128)S(1)}, f32[4,8,128]{2,1,0:T(8,128)S(1)}, u32[]{:S(2)}, u32[]{:S(2)}) collective-permute-start(f32[4,8,128]{2,1,0:T(8,128)S(1)} %collective-permute-done.24.refs_4_), channel_id=1, source_target_pairs={{0,64},{28,92},{32,96},{60,124},{128,192},{156,220},{160,224},{188... | collective-permute-start | bytes 49160 | tf_op jit(solution)/shard_map/ppermute | solution.py:34
  88.9 4.7 %collective-permute-start.26 = (f32[4,8,128]{2,1,0:T(8,128)S(1)}, f32[4,8,128]{2,1,0:T(8,128)S(1)}, u32[]{:S(2)}, u32[]{:S(2)}) collective-permute-start(f32[4,8,128]{2,1,0:T(8,128)S(1)} %collective-permute-done.24.refs_4_), channel_id=1, source_target_pairs={{64,128},{92,156},{96,160},{124,188},{192,0},{220,28},{224,32},{25... | collective-permute-start | bytes 49160 | tf_op jit(solution)/shard_map/ppermute | solution.py:34
  93.7 2.7 %collective-permute-done.26.refs_5_ = f32[4,8,128]{2,1,0:T(8,128)S(1)} collective-permute-done((f32[4,8,128]{2,1,0:T(8,128)S(1)}, f32[4,8,128]{2,1,0:T(8,128)S(1)}, u32[]{:S(2)}, u32[]{:S(2)}) %collective-permute-start.26) | collective-permute-done | bytes 16416 | tf_op jit(solution)/shard_map/ppermute | solution.py:34
  96.4 1.3 %arrivals.1 = f32[6,8,512]{2,1,0:T(8,128)} custom-call(s32[4]{0:T(128)S(1)} %pad_add_fusion.spot, f32[3,4,8,128]{3,2,1,0:T(8,128)S(1)} %collective-permute-done.22.refs_0_, f32[3,4,8,128]{3,2,1,0:T(8,128)S(1)} %pad_maximum_fusion.2.refs_1_, f32[3,4,8,128]{3,2,1,0:T(8,128)S(1)} %collective-permute-done.23.refs_2_, ...), custom_call_target="tpu_custom_call" | custom-call | tf_op jit(solution)/shard_map/arrivals/pallas_call | solution.py:332
  (56 shorter events, 0.4 us)
Async XLA Ops:
  0.6 0.7 copy-start.7
  0.6 0.8 copy-start.6
  0.7 3.1 %copy-start.3 = (f32[3,4096]{1,0:T(4,128)S(1)}, f32[3,4096]{1,0:T(4,128)}, u32[]{:S(2)}) copy-start(f32[3,4096]{1,0:T(4,128)} %param.15) | copy-start | bytes 147460
  3.7 1.7 %copy-start.5 = (f32[4096]{0:T(1024)S(1)}, f32[4096]{0:T(1024)}, u32[]{:S(2)}) copy-start(f32[4096]{0:T(1024)} %param.18) | copy-start | bytes 49156
  3.8 32.9 %copy-start = (s32[1,64,16,128]{3,2,1,0:T(8,128)S(1)}, s32[1,64,16,128]{3,2,1,0:T(8,128)}, u32[]{:S(2)}) copy-start(s32[1,64,16,128]{3,2,1,0:T(8,128)} %param.25) | copy-start | bytes 1572868
  5.5 16.7 %collective-permute-start = (f32[33,4,128]{2,1,0:T(4,128)S(1)}, f32[33,4,128]{2,1,0:T(4,128)S(1)}, u32[]{:S(2)}, u32[]{:S(2)}) collective-permute-start(f32[33,4,128]{2,1,0:T(4,128)S(1)} %get-tuple-element.45.refs_0_), channel_id=1, source_target_pairs={{0,1},{1,0},{2,3},{3,2},{4,5},{5,4},{6,7},{7,6},{8,9},{9,8},{10,11... | collective-permute-start | bytes 202760 | tf_op jit(solution)/shard_map/ppermute | solution.py:389
  7.8 20.9 %collective-permute-start.1 = (f32[33,4,128]{2,1,0:T(4,128)S(1)}, f32[33,4,128]{2,1,0:T(4,128)S(1)}, u32[]{:S(2)}, u32[]{:S(2)}) collective-permute-start(f32[33,4,128]{2,1,0:T(4,128)S(1)} %get-tuple-element.45.refs_0_), channel_id=1, source_target_pairs={{0,2},{1,3},{2,0},{3,1},{4,6},{5,7},{6,4},{7,5},{8,10},{9,11},{10,... | collective-permute-start | bytes 202760 | tf_op jit(solution)/shard_map/ppermute | solution.py:389
  8.5 12.1 %collective-permute-start.4 = (f32[33,4,128]{2,1,0:T(4,128)S(1)}, f32[33,4,128]{2,1,0:T(4,128)S(1)}, u32[]{:S(2)}, u32[]{:S(2)}) collective-permute-start(f32[33,4,128]{2,1,0:T(4,128)S(1)} %get-tuple-element.45.refs_0_), channel_id=1, source_target_pairs={{64,128},{192,0},{128,64},{0,192},{65,129},{193,1},{129,65},{1,193... | collective-permute-start | bytes 202760 | tf_op jit(solution)/shard_map/ppermute | solution.py:34
  13.1 7.5 %collective-permute-start.3 = (f32[33,4,128]{2,1,0:T(4,128)S(1)}, f32[33,4,128]{2,1,0:T(4,128)S(1)}, u32[]{:S(2)}, u32[]{:S(2)}) collective-permute-start(f32[33,4,128]{2,1,0:T(4,128)S(1)} %get-tuple-element.45.refs_0_), channel_id=1, source_target_pairs={{0,64},{128,192},{64,0},{192,128},{1,65},{129,193},{65,1},{193,129... | collective-permute-start | bytes 202760 | tf_op jit(solution)/shard_map/ppermute | solution.py:34
  13.1 11.6 %collective-permute-start.7 = (f32[33,4,128]{2,1,0:T(4,128)S(1)}, f32[33,4,128]{2,1,0:T(4,128)S(1)}, u32[]{:S(2)}, u32[]{:S(2)}) collective-permute-start(f32[33,4,128]{2,1,0:T(4,128)S(1)} %get-tuple-element.45.refs_0_), channel_id=1, source_target_pairs={{28,32},{60,0},{32,28},{0,60},{29,33},{61,1},{33,29},{1,61},{30,34... | collective-permute-start | bytes 202760 | tf_op jit(solution)/shard_map/ppermute | solution.py:34
  20.7 16.0 %collective-permute-start.5 = (f32[3,33,4,128]{3,2,1,0:T(4,128)S(1)}, f32[3,33,4,128]{3,2,1,0:T(4,128)S(1)}, u32[]{:S(2)}, u32[]{:S(2)}) collective-permute-start(f32[3,33,4,128]{3,2,1,0:T(4,128)S(1)} %pad_maximum_fusion.refs_5_), channel_id=1, source_target_pairs={{0,4},{8,12},{16,20},{24,28},{32,36},{40,44},{48,52},{56,60},{4,0}... | collective-permute-start | bytes 608264 | tf_op jit(solution)/shard_map/ppermute | solution.py:34
  20.8 15.9 %collective-permute-start.6 = (f32[3,33,4,128]{3,2,1,0:T(4,128)S(1)}, f32[3,33,4,128]{3,2,1,0:T(4,128)S(1)}, u32[]{:S(2)}, u32[]{:S(2)}) collective-permute-start(f32[3,33,4,128]{3,2,1,0:T(4,128)S(1)} %pad_maximum_fusion.refs_5_), channel_id=1, source_target_pairs={{4,8},{12,16},{20,24},{36,40},{44,48},{52,56},{8,4},{16,12},{24,20... | collective-permute-start | bytes 608264 | tf_op jit(solution)/shard_map/ppermute | solution.py:34
  22.1 9.5 %collective-permute-start.2 = (f32[33,4,128]{2,1,0:T(4,128)S(1)}, f32[33,4,128]{2,1,0:T(4,128)S(1)}, u32[]{:S(2)}, u32[]{:S(2)}) collective-permute-start(f32[33,4,128]{2,1,0:T(4,128)S(1)} %get-tuple-element.45.refs_0_), channel_id=1, source_target_pairs={{0,3},{1,2},{2,1},{3,0},{4,7},{5,6},{6,5},{7,4},{8,11},{9,10},{10,... | collective-permute-start | bytes 202760 | tf_op jit(solution)/shard_map/ppermute | solution.py:389
  24.7 6.9 %collective-permute-start.8 = (f32[33,4,128]{2,1,0:T(4,128)S(1)}, f32[33,4,128]{2,1,0:T(4,128)S(1)}, u32[]{:S(2)}, u32[]{:S(2)}) collective-permute-start(f32[33,4,128]{2,1,0:T(4,128)S(1)} %collective-permute-done.7.refs_8_), channel_id=1, source_target_pairs={{0,64},{28,92},{32,96},{60,124},{128,192},{156,220},{160,224},{188... | collective-permute-start | bytes 202760 | tf_op jit(solution)/shard_map/ppermute | solution.py:34
  28.7 8.0 %collective-permute-start.9 = (f32[33,4,128]{2,1,0:T(4,128)S(1)}, f32[33,4,128]{2,1,0:T(4,128)S(1)}, u32[]{:S(2)}, u32[]{:S(2)}) collective-permute-start(f32[33,4,128]{2,1,0:T(4,128)S(1)} %collective-permute-done.7.refs_8_), channel_id=1, source_target_pairs={{64,128},{92,156},{96,160},{124,188},{192,0},{220,28},{224,32},{25... | collective-permute-start | bytes 202760 | tf_op jit(solution)/shard_map/ppermute | solution.py:34
  31.6 5.1 %copy-start.1 = (s32[1,64]{1,0:T(1,128)S(1)}, s32[1,64]{1,0:T(1,128)}, u32[]{:S(2)}) copy-start(s32[1,64]{1,0:T(1,128)} %tower_list.1) | copy-start | bytes 772
  31.6 5.1 %copy-start.2 = (s32[1,64]{1,0:T(1,128)S(1)}, s32[1,64]{1,0:T(1,128)}, u32[]{:S(2)}) copy-start(s32[1,64]{1,0:T(1,128)} %plate_list.1) | copy-start | bytes 772
  40.2 3.9 %copy-start.8 = (s32[1,4]{1,0:T(1,128)S(1)}, s32[1,4]{1,0:T(1,128)}, u32[]{:S(2)}) copy-start(s32[1,4]{1,0:T(1,128)} %param.27) | copy-start | bytes 52
  40.2 8.7 %collective-permute-start.18 = (f32[32,4,128]{2,1,0:T(4,128)S(1)}, f32[32,4,128]{2,1,0:T(4,128)S(1)}, u32[]{:S(2)}, u32[]{:S(2)}) collective-permute-start(f32[32,4,128]{2,1,0:T(4,128)S(1)} %get-tuple-element.43), channel_id=1, source_target_pairs={{64,128},{92,156},{96,160},{124,188},{192,0},{220,28},{224,32},{25... | collective-permute-start | bytes 196616 | tf_op jit(solution)/shard_map/ppermute | solution.py:34
  42.2 12.2 %collective-permute-start.17 = (f32[32,4,128]{2,1,0:T(4,128)S(1)}, f32[32,4,128]{2,1,0:T(4,128)S(1)}, u32[]{:S(2)}, u32[]{:S(2)}) collective-permute-start(f32[32,4,128]{2,1,0:T(4,128)S(1)} %get-tuple-element.42), channel_id=1, source_target_pairs={{0,64},{28,92},{32,96},{60,124},{128,192},{156,220},{160,224},{188... | collective-permute-start | bytes 196616 | tf_op jit(solution)/shard_map/ppermute | solution.py:34
  44.1 11.4 %collective-permute-start.14 = (f32[3,32,4,128]{3,2,1,0:T(4,128)S(1)}, f32[3,32,4,128]{3,2,1,0:T(4,128)S(1)}, u32[]{:S(2)}, u32[]{:S(2)}) collective-permute-start(f32[3,32,4,128]{3,2,1,0:T(4,128)S(1)} %get-tuple-element.17), channel_id=1, source_target_pairs={{4,8},{12,16},{20,24},{36,40},{44,48},{52,56},{8,4},{16,12},{24,20... | collective-permute-start | bytes 589832 | tf_op jit(solution)/shard_map/ppermute | solution.py:34
  44.8 14.5 %collective-permute-start.13 = (f32[3,32,4,128]{3,2,1,0:T(4,128)S(1)}, f32[3,32,4,128]{3,2,1,0:T(4,128)S(1)}, u32[]{:S(2)}, u32[]{:S(2)}) collective-permute-start(f32[3,32,4,128]{3,2,1,0:T(4,128)S(1)} %get-tuple-element.16), channel_id=1, source_target_pairs={{0,4},{8,12},{16,20},{24,28},{32,36},{40,44},{48,52},{56,60},{4,0}... | collective-permute-start | bytes 589832 | tf_op jit(solution)/shard_map/ppermute | solution.py:34
  44.9 15.5 %collective-permute-start.12 = (f32[32,4,128]{2,1,0:T(4,128)S(1)}, f32[32,4,128]{2,1,0:T(4,128)S(1)}, u32[]{:S(2)}, u32[]{:S(2)}) collective-permute-start(f32[32,4,128]{2,1,0:T(4,128)S(1)} %get-tuple-element.14), channel_id=1, source_target_pairs={{0,3},{1,2},{2,1},{3,0},{4,7},{5,6},{6,5},{7,4},{8,11},{9,10},{10,... | collective-permute-start | bytes 196616 | tf_op jit(solution)/shard_map/ppermute | solution.py:389
  49.0 12.0 %collective-permute-start.11 = (f32[32,4,128]{2,1,0:T(4,128)S(1)}, f32[32,4,128]{2,1,0:T(4,128)S(1)}, u32[]{:S(2)}, u32[]{:S(2)}) collective-permute-start(f32[32,4,128]{2,1,0:T(4,128)S(1)} %get-tuple-element.13), channel_id=1, source_target_pairs={{0,2},{1,3},{2,0},{3,1},{4,6},{5,7},{6,4},{7,5},{8,10},{9,11},{10,... | collective-permute-start | bytes 196616 | tf_op jit(solution)/shard_map/ppermute | solution.py:389
  54.3 6.6 %collective-permute-start.10 = (f32[32,4,128]{2,1,0:T(4,128)S(1)}, f32[32,4,128]{2,1,0:T(4,128)S(1)}, u32[]{:S(2)}, u32[]{:S(2)}) collective-permute-start(f32[32,4,128]{2,1,0:T(4,128)S(1)} %get-tuple-element.12), channel_id=1, source_target_pairs={{0,1},{1,0},{2,3},{3,2},{4,5},{5,4},{6,7},{7,6},{8,9},{9,8},{10,11... | collective-permute-start | bytes 196616 | tf_op jit(solution)/shard_map/ppermute | solution.py:389
  55.5 11.6 %collective-permute-start.19 = (f32[32,4,128]{2,1,0:T(4,128)S(1)}, f32[32,4,128]{2,1,0:T(4,128)S(1)}, u32[]{:S(2)}, u32[]{:S(2)}) collective-permute-start(f32[32,4,128]{2,1,0:T(4,128)S(1)} %fusion.2), channel_id=1, source_target_pairs={{28,32},{60,0},{32,28},{0,60},{29,33},{61,1},{33,29},{1,61},{30,34... | collective-permute-start | bytes 196616 | tf_op jit(solution)/shard_map/ppermute | solution.py:34
  59.4 7.7 %copy-start.4 = (f32[3,4096]{1,0:T(4,128)S(1)}, f32[3,4096]{1,0:T(4,128)}, u32[]{:S(2)}) copy-start(f32[3,4096]{1,0:T(4,128)} %param.16) | copy-start | bytes 147460
  59.4 7.7 %collective-permute-start.16 = (f32[32,4,128]{2,1,0:T(4,128)S(1)}, f32[32,4,128]{2,1,0:T(4,128)S(1)}, u32[]{:S(2)}, u32[]{:S(2)}) collective-permute-start(f32[32,4,128]{2,1,0:T(4,128)S(1)} %get-tuple-element.40), channel_id=1, source_target_pairs={{64,128},{192,0},{128,64},{0,192},{65,129},{193,1},{129,65},{1,193... | collective-permute-start | bytes 196616 | tf_op jit(solution)/shard_map/ppermute | solution.py:34
  60.4 6.8 %collective-permute-start.15 = (f32[32,4,128]{2,1,0:T(4,128)S(1)}, f32[32,4,128]{2,1,0:T(4,128)S(1)}, u32[]{:S(2)}, u32[]{:S(2)}) collective-permute-start(f32[32,4,128]{2,1,0:T(4,128)S(1)} %get-tuple-element.41), channel_id=1, source_target_pairs={{0,64},{128,192},{64,0},{192,128},{1,65},{129,193},{65,1},{193,129... | collective-permute-start | bytes 196616 | tf_op jit(solution)/shard_map/ppermute | solution.py:34
  68.6 5.6 %collective-permute-start.21 = (f32[4,8,128]{2,1,0:T(8,128)S(1)}, f32[4,8,128]{2,1,0:T(8,128)S(1)}, u32[]{:S(2)}, u32[]{:S(2)}) collective-permute-start(f32[4,8,128]{2,1,0:T(8,128)S(1)} %get-tuple-element.47), channel_id=1, source_target_pairs={{64,128},{192,0},{128,64},{0,192},{65,129},{193,1},{129,65},{1,193... | collective-permute-start | bytes 49160 | tf_op jit(solution)/shard_map/ppermute | solution.py:34
  70.8 3.7 %collective-permute-start.20 = (f32[4,8,128]{2,1,0:T(8,128)S(1)}, f32[4,8,128]{2,1,0:T(8,128)S(1)}, u32[]{:S(2)}, u32[]{:S(2)}) collective-permute-start(f32[4,8,128]{2,1,0:T(8,128)S(1)} %get-tuple-element.47), channel_id=1, source_target_pairs={{0,64},{128,192},{64,0},{192,128},{1,65},{129,193},{65,1},{193,129... | collective-permute-start | bytes 49160 | tf_op jit(solution)/shard_map/ppermute | solution.py:34
  74.6 21.8 %collective-permute-start.22 = (f32[3,4,8,128]{3,2,1,0:T(8,128)S(1)}, f32[3,4,8,128]{3,2,1,0:T(8,128)S(1)}, u32[]{:S(2)}, u32[]{:S(2)}) collective-permute-start(f32[3,4,8,128]{3,2,1,0:T(8,128)S(1)} %pad_maximum_fusion.2.refs_1_), channel_id=1, source_target_pairs={{0,4},{8,12},{16,20},{24,28},{32,36},{40,44},{48,52},{56,60},{4,0}... | collective-permute-start | bytes 147464 | tf_op jit(solution)/shard_map/ppermute | solution.py:34
  74.6 21.8 %collective-permute-start.23 = (f32[3,4,8,128]{3,2,1,0:T(8,128)S(1)}, f32[3,4,8,128]{3,2,1,0:T(8,128)S(1)}, u32[]{:S(2)}, u32[]{:S(2)}) collective-permute-start(f32[3,4,8,128]{3,2,1,0:T(8,128)S(1)} %pad_maximum_fusion.2.refs_1_), channel_id=1, source_target_pairs={{4,8},{12,16},{20,24},{36,40},{44,48},{52,56},{8,4},{16,12},{24,20... | collective-permute-start | bytes 147464 | tf_op jit(solution)/shard_map/ppermute | solution.py:34
  75.3 11.1 %collective-permute-start.24 = (f32[4,8,128]{2,1,0:T(8,128)S(1)}, f32[4,8,128]{2,1,0:T(8,128)S(1)}, u32[]{:S(2)}, u32[]{:S(2)}) collective-permute-start(f32[4,8,128]{2,1,0:T(8,128)S(1)} %get-tuple-element.47), channel_id=1, source_target_pairs={{28,32},{60,0},{32,28},{0,60},{29,33},{61,1},{33,29},{1,61},{30,34... | collective-permute-start | bytes 49160 | tf_op jit(solution)/shard_map/ppermute | solution.py:34
  86.3 7.3 %collective-permute-start.25 = (f32[4,8,128]{2,1,0:T(8,128)S(1)}, f32[4,8,128]{2,1,0:T(8,128)S(1)}, u32[]{:S(2)}, u32[]{:S(2)}) collective-permute-start(f32[4,8,128]{2,1,0:T(8,128)S(1)} %collective-permute-done.24.refs_4_), channel_id=1, source_target_pairs={{0,64},{28,92},{32,96},{60,124},{128,192},{156,220},{160,224},{188... | collective-permute-start | bytes 49160 | tf_op jit(solution)/shard_map/ppermute | solution.py:34
  88.9 7.4 %collective-permute-start.26 = (f32[4,8,128]{2,1,0:T(8,128)S(1)}, f32[4,8,128]{2,1,0:T(8,128)S(1)}, u32[]{:S(2)}, u32[]{:S(2)}) collective-permute-start(f32[4,8,128]{2,1,0:T(8,128)S(1)} %collective-permute-done.24.refs_4_), channel_id=1, source_target_pairs={{64,128},{92,156},{96,160},{124,188},{192,0},{220,28},{224,32},{25... | collective-permute-start | bytes 49160 | tf_op jit(solution)/shard_map/ppermute | solution.py:34
where the time goes:
time: 98.4 us; the launch traced here: 97.6 us
  starting transfers between devices  59.3 us (60%)
  waiting for transfers between devices  25.3 us (26%)
  Pallas kernels  4.77 us (5%)
  other arithmetic  4.26 us (4%)
  local copies, waits for them, and re-layouts  2.27 us (2%)
  between operations  1.69 us (2%)
    ppermute x21, starting transfers between devices, swap(): return lax.ppermute(value, axis, [*pairs, *((j, i) for i, j in pairs)])  45.1 us
    ppermute x21, waiting for transfers between devices, swap(): return lax.ppermute(value, axis, [*pairs, *((j, i) for i, j in pairs)])  25.3 us
    ppermute x6, starting transfers between devices, from_layer(): return lax.ppermute(value, 'gz', [(i, i ^ step) for i in range(layers)])  14.2 us
    pallas_call x1, Pallas kernels, pair_forces(): pl.pallas_call(functools.partial(pair_kernel, *lengths, group), out_shape...  3.51 us
  transfers between devices with their start and end apart: 27, of which 7 were waited for; matrix products, arithmetic and copies ran while one was open for 0% of the time, Pallas kernels for 0%

commit v1 on v0

--- a/solution.py
+++ b/solution.py
@@ -26,48 +26,30 @@
     return [(i, (i + 1) % count) for i in range(1, count, 2)]
 
 
-def far_pairs(count):
-    return [(count // 2 - 1, count // 2), (count - 1, 0)]
-
-
 def swap(value, axis, pairs):
     return lax.ppermute(value, axis, [*pairs, *((j, i) for i, j in pairs)])
 
 
-def swap_in_far_rows(value, pairs):
-    count = lax.axis_size("gy")
-    rows = sorted(y for pair in far_pairs(count) for y in pair)
-    return swap(
-        value, ("gx", "gy"), [(i * count + y, j * count + y) for i, j in pairs for y in rows]
-    )
-
-
 def halo(value):
     count_x, count_y = lax.axis_size("gx"), lax.axis_size("gy")
-    first_x, second_x = pairs_first(count_x), pairs_second(count_x)
-    far_y = far_pairs(count_y)
-    near_y = [pair for pair in pairs_second(count_y) if pair not in far_y]
-    across = swap(value, "gy", far_y)
-    own = jnp.stack([swap(value, "gx", first_x), value, swap(value, "gx", second_x)])
-    first = swap(own, "gy", pairs_first(count_y))
-    second = swap(own, "gy", near_y)
-    far = (swap_in_far_rows(across, first_x),
-        across,
-        swap_in_far_rows(across, second_x),
-    )
-    return (first, own, second), far
+    own = jnp.stack(
+        [swap(value, "gx", pairs_first(count_x)), value, swap(value, "gx", pairs_second(count_x))]
+    )
+    return (swap(own, "gy", pairs_first(count_y)), own, swap(own, "gy", pairs_second(count_y)))
 
 
 def sent_home(first, own, second):
     count_x, count_y = lax.axis_size("gx"), lax.axis_size("gy")
-    first_x, second_x = pairs_first(count_x), pairs_second(count_x)
-    far_y = far_pairs(count_y)
-    near_y = [pair for pair in pairs_second(count_y) if pair not in far_y]
-    side_one = swap_in_far_rows(second[0], first_x)
-    side_two = swap_in_far_rows(second[2], second_x)
-    across = swap(second[1] + side_one + side_two, "gy", far_y)
-    row = own + swap(first, "gy", pairs_first(count_y)) + swap(second, "gy", near_y)
-    return row[1] + swap(row[0], "gx", first_x) + swap(row[2], "gx", second_x) + across
+    row = (
+        own
+        + swap(first, "gy", pairs_first(count_y))
+        + swap(second, "gy", pairs_second(count_y))
+    )
+    return (
+        row[1]
+        + swap(row[0], "gx", pairs_first(count_x))
+        + swap(row[2], "gx", pairs_second(count_x))
+    )
 
 
 def piece_of(offset, odd):
@@ -99,12 +81,12 @@
     spot,
     *refs,
 ):
-    tower_refs, (first_row, own_row, second_row), far_refs = refs[0:4], refs[4:7], refs[7:10]
-    masks, tower_outs, row_outs, held = refs[10], refs[11:15], refs[15:18], refs[18:]
+    tower_refs, (first_row, own_row, second_row) = refs[0:4], refs[4:7]
+    masks, tower_outs, row_outs, held = refs[7], refs[8:12], refs[12:15], refs[15:]
     blocks = tower_outs[0].shape[0]
     for ref in (*tower_outs, *row_outs):
         ref[...] = jnp.zeros_like(ref)
-    odd_x, odd_y, far, me_z = (spot[n] for n in range(4))
+    odd_x, odd_y, me_z = (spot[n] for n in range(3))
     f32 = jnp.float32
     row4 = lax.broadcasted_iota(jnp.int32, (4, lanes), 0)
     lane4 = lax.broadcasted_iota(jnp.int32, (4, lanes), 1)
@@ -169,16 +151,10 @@
         tower_kind = tower_tile(layer, blocks)
 
         def chosen(row):
-            from_far = jnp.where(
-                cell_x == 0,
-                far_refs[0][row],
-                jnp.where(cell_x == 1, far_refs[1][row], far_refs[2][row]),
-            )
-            second = jnp.where(far == 1, from_far, second_row[cell_x, row])
             return jnp.where(
                 cell_y == 0,
                 first_row[cell_x, row],
-                jnp.where(cell_y == 1, own_row[cell_x, row], second),
+                jnp.where(cell_y == 1, own_row[cell_x, row], second_row[cell_x, row]),
             )
 
         plate_rows = chosen(plate_block) * scale
@@ -283,14 +259,14 @@
     lax.fori_loop(0, (total + 2 * unroll - 1) // (2 * unroll), step, 0)
 
 
-def pair_forces(tower_list, plate_list, count, spot, towers, rows, far, masks, lengths):
+def pair_forces(tower_list, plate_list, count, spot, towers, rows, masks, lengths):
     blocks = towers[0].shape[0] - 1
     shape_one = jax.ShapeDtypeStruct((blocks, 4, lanes), jnp.float32)
     shape_row = jax.ShapeDtypeStruct((3, blocks, 4, lanes), jnp.float32)
     return pl.pallas_call(
         functools.partial(pair_kernel, *lengths, group),
         out_shape=[shape_one] * 4 + [shape_row] * 3,
-        in_specs=[smem()] * 4 + [vmem()] * 11,
+        in_specs=[smem()] * 4 + [vmem()] * 8,
         out_specs=[vmem()] * 7,
         scratch_shapes=[
             pltpu.VMEM((group, lanes, 4 * lanes), jnp.float32),
@@ -302,14 +278,14 @@
             flops=40 * 64 * lanes * lanes, bytes_accessed=2**21, transcendentals=64 * lanes * lanes
         ),
         name="pair_forces",
-    )(tower_list, plate_list, count, spot, *towers, *rows, *far, masks)
+    )(tower_list, plate_list, count, spot, *towers, *rows, masks)
 
 
 def arrival_kernel(spot, *refs):
-    (first_row, own_row, second_row), far_refs, out = refs[0:3], refs[3:6], refs[6]
-    odd_x, odd_y, far = spot[0], spot[1], spot[2]
+    first_row, own_row, second_row, out = refs
+    odd_x, odd_y = spot[0], spot[1]
     for q in range(own_row.shape[1]):
-        second = [jnp.where(far == 1, far_refs[k][q], second_row[k, q]) for k in range(3)]
+        second = [second_row[k, q] for k in range(3)]
         first = [first_row[k, q] for k in range(3)]
         own = [own_row[k, q] for k in range(3)]
         for number, (x, y) in enumerate(sources):
@@ -327,16 +303,16 @@
                 out[c, number : number + 1, lanes * q : lanes * q + lanes] = kept[c : c + 1]
 
 
-def arrivals_of(spot, rows, far):
+def arrivals_of(spot, rows):
     leaving = rows[0].shape[1]
     return pl.pallas_call(
         arrival_kernel,
         out_shape=jax.ShapeDtypeStruct((6, 8, leaving * lanes), jnp.float32),
-        in_specs=[smem()] + [vmem()] * 6,
+        in_specs=[smem()] + [vmem()] * 3,
         out_specs=vmem(),
         compiler_params=pltpu.CompilerParams(vmem_limit_bytes=VMEM_LIMIT),
         name="arrivals",
-    )(spot, *rows, *far)
+    )(spot, *rows)
 
 
 def by_block(rows):
@@ -377,13 +353,9 @@
     features = jnp.concatenate(
         [by_block(jnp.concatenate([moved, charges[None, :]])), kind_tile[None]]
     )
-    count_y = lax.axis_size("gy")
     me_x, me_y, me_z = (lax.axis_index(axis) for axis in ("gx", "gy", "gz"))
-    is_far = functools.reduce(
-        jnp.logical_or, [me_y == y for pair in far_pairs(count_y) for y in pair]
-    )
-    spot = jnp.stack([me_x % 2, me_y % 2, is_far.astype(jnp.int32), me_z]).astype(jnp.int32)
-    rows, far = halo(features)
+    spot = jnp.stack([me_x % 2, me_y % 2, me_z]).astype(jnp.int32)
+    rows = halo(features)
 
     def from_layer(value, step):
         return lax.ppermute(value, "gz", [(i, i ^ step) for i in range(layers)])
@@ -396,7 +368,6 @@
         spot,
         towers,
         rows,
-        far,
         exclusions[0],
         (length_x, length_y),
     )
@@ -415,7 +386,7 @@
     )
     state = by_block(jnp.concatenate([moved, velocity_full]))
     state = jnp.concatenate([jnp.take(state, leaving, axis=0), tags], axis=1)
-    arrivals = arrivals_of(spot, *halo(state))[:, None]
+    arrivals = arrivals_of(spot, halo(state))[:, None]
     return (positions_new, velocities_new, forces_new, arrivals)
 
 

time: 98.4 us -> 78.7 us (0.80)
  the two profiles are of different devices: /device:TPU:2 before, /device:TPU:6 now
where the time goes in v1:
time: 78.7 us; the launch traced here: 78.5 us
  starting transfers between devices  41.8 us (53%)
  waiting for transfers between devices  25.2 us (32%)
  other arithmetic  4.21 us (5%)
  Pallas kernels  3.5 us (4%)
  local copies, waits for them, and re-layouts  2.26 us (3%)
  between operations  1.5 us (2%)
    ppermute x12, starting transfers between devices, swap(): return lax.ppermute(value, axis, [*pairs, *((j, i) for i, j in pairs)])  32.9 us
    ppermute x12, waiting for transfers between devices, swap(): return lax.ppermute(value, axis, [*pairs, *((j, i) for i, j in pairs)])  25.2 us
    ppermute x6, starting transfers between devices, from_layer(): return lax.ppermute(value, 'gz', [(i, i ^ step) for i in range(layers)])  8.97 us
    pallas_call x1, Pallas kernels, pair_forces(): pl.pallas_call(functools.partial(pair_kernel, *lengths, group), out_shape...  2.25 us
    mul x1, other arithmetic, local(): positions_new = moved * staying  1.61 us
  transfers between devices with their start and end apart: 18, of which 9 were waited for; matrix products, arithmetic and copies ran while one was open for 0% of the time, Pallas kernels for 0%

profile of v1, /device:TPU:6, one launch (start us, length us, event | category | flops | bytes accessed | tf_op | source)
XLA Modules:
  0.0 78.5 jit_solution(15351752903126465400)
XLA Ops:
  0.7 0.6 copy-done.7
  1.3 0.1 fusion.2
  1.4 0.1 broadcast_bitcast_fusion
  1.5 0.7 broadcast_compare_fusion.3
  2.1 0.7 sqrt_bitcast_fusion
  2.8 0.7 pad_maximum_fusion.4
  3.5 0.2 slice_reduce_fusion
  3.7 0.0 copy-start.5
  3.7 0.1 select_select_fusion
  3.8 1.6 %broadcast_multiply_fusion.1 = (f32[3,4096]{1,0:T(4,128)}, f32[3,4096]{1,0:T(4,128)S(1)}) fusion(f32[4096]{0:T(1024)S(1)} %broadcast_bitcast_fusion, f32[3,4096]{1,0:T(4,128)} %param.14, f32[3,4096]{1,0:T(4,128)S(1)} %copy-done.3, f32[3,4096]{1,0:T(4,128)} %param.16, f32[4096]{0:T(1024)S(1)} %broadcast_multiply_fusion.2), kind=kLoop, calls=%fused_computation.21 | loop fusion | flops 61440 | bytes 278528 | tf_op jit(solution)/shard_map/mul | solution.py:382
  5.5 0.9 %collective-permute-start = (f32[33,4,128]{2,1,0:T(4,128)S(1)}, f32[33,4,128]{2,1,0:T(4,128)S(1)}, u32[]{:S(2)}, u32[]{:S(2)}) collective-permute-start(f32[33,4,128]{2,1,0:T(4,128)S(1)} %get-tuple-element.43.refs_0_), channel_id=1, source_target_pairs={{0,1},{1,0},{2,3},{3,2},{4,5},{5,4},{6,7},{7,6},{8,9},{9,8},{10,11... | collective-permute-start | bytes 202760 | tf_op jit(solution)/shard_map/ppermute | solution.py:361
  6.4 2.8 %collective-permute-start.1 = (f32[33,4,128]{2,1,0:T(4,128)S(1)}, f32[33,4,128]{2,1,0:T(4,128)S(1)}, u32[]{:S(2)}, u32[]{:S(2)}) collective-permute-start(f32[33,4,128]{2,1,0:T(4,128)S(1)} %get-tuple-element.43.refs_0_), channel_id=1, source_target_pairs={{0,2},{1,3},{2,0},{3,1},{4,6},{5,7},{6,4},{7,5},{8,10},{9,11},{10,... | collective-permute-start | bytes 202760 | tf_op jit(solution)/shard_map/ppermute | solution.py:361
  9.2 1.1 %collective-permute-start.2 = (f32[33,4,128]{2,1,0:T(4,128)S(1)}, f32[33,4,128]{2,1,0:T(4,128)S(1)}, u32[]{:S(2)}, u32[]{:S(2)}) collective-permute-start(f32[33,4,128]{2,1,0:T(4,128)S(1)} %get-tuple-element.43.refs_0_), channel_id=1, source_target_pairs={{0,3},{1,2},{2,1},{3,0},{4,7},{5,6},{6,5},{7,4},{8,11},{9,10},{10,... | collective-permute-start | bytes 202760 | tf_op jit(solution)/shard_map/ppermute | solution.py:361
  10.2 4.6 %collective-permute-start.4 = (f32[33,4,128]{2,1,0:T(4,128)S(1)}, f32[33,4,128]{2,1,0:T(4,128)S(1)}, u32[]{:S(2)}, u32[]{:S(2)}) collective-permute-start(f32[33,4,128]{2,1,0:T(4,128)S(1)} %get-tuple-element.43.refs_0_), channel_id=1, source_target_pairs={{64,128},{192,0},{128,64},{0,192},{65,129},{193,1},{129,65},{1,193... | collective-permute-start | bytes 202760 | tf_op jit(solution)/shard_map/ppermute | solution.py:30
  14.9 2.4 %collective-permute-done.4 = f32[33,4,128]{2,1,0:T(4,128)S(1)} collective-permute-done((f32[33,4,128]{2,1,0:T(4,128)S(1)}, f32[33,4,128]{2,1,0:T(4,128)S(1)}, u32[]{:S(2)}, u32[]{:S(2)}) %collective-permute-start.4) | collective-permute-done | bytes 67616 | tf_op jit(solution)/shard_map/ppermute | solution.py:30
  17.2 1.9 %collective-permute-done.3 = f32[33,4,128]{2,1,0:T(4,128)S(1)} collective-permute-done((f32[33,4,128]{2,1,0:T(4,128)S(1)}, f32[33,4,128]{2,1,0:T(4,128)S(1)}, u32[]{:S(2)}, u32[]{:S(2)}) %collective-permute-start.3) | collective-permute-done | bytes 67616 | tf_op jit(solution)/shard_map/ppermute | solution.py:30
  19.2 0.1 collective-permute-start.5
  19.3 7.6 %collective-permute-start.6 = (f32[3,33,4,128]{3,2,1,0:T(4,128)S(1)}, f32[3,33,4,128]{3,2,1,0:T(4,128)S(1)}, u32[]{:S(2)}, u32[]{:S(2)}) collective-permute-start(f32[3,33,4,128]{3,2,1,0:T(4,128)S(1)} %pad_maximum_fusion.refs_5_), channel_id=1, source_target_pairs={{4,8},{12,16},{20,24},{28,32},{36,40},{44,48},{52,56},{60,0},{8,4}... | collective-permute-start | bytes 608264 | tf_op jit(solution)/shard_map/ppermute | solution.py:30
  27.6 0.1 pad_add_fusion.spot
  27.7 0.0 collective-permute-done.refs_1_
  27.7 0.0 collective-permute-done.1.refs_2_
  27.7 0.0 collective-permute-done.2.refs_3_
  27.7 2.9 %collective-permute-done.6.refs_6_ = f32[3,33,4,128]{3,2,1,0:T(4,128)S(1)} collective-permute-done((f32[3,33,4,128]{3,2,1,0:T(4,128)S(1)}, f32[3,33,4,128]{3,2,1,0:T(4,128)S(1)}, u32[]{:S(2)}, u32[]{:S(2)}) %collective-permute-start.6) | collective-permute-done | bytes 202784 | tf_op jit(solution)/shard_map/ppermute | solution.py:30
  30.7 2.2 %pair_forces.1 = (f32[32,4,128]{2,1,0:T(4,128)S(1)}, f32[32,4,128]{2,1,0:T(4,128)S(1)}, f32[32,4,128]{2,1,0:T(4,128)S(1)}, f32[32,4,128]{2,1,0:T(4,128)S(1)}, f3...) custom-call(s32[1,64]{1,0:T(1,128)S(1)} %copy-done.1, ...), custom_call_target="tpu_custom_call" | custom-call | flops 41943040 | bytes 2097152 | tf_op jit(solution)/shard_map/pair_forces/pallas_call | solution.py:266
  32.9 0.0 copy-start.8
  33.0 7.6 %collective-permute-start.11 = (f32[3,32,4,128]{3,2,1,0:T(4,128)S(1)}, f32[3,32,4,128]{3,2,1,0:T(4,128)S(1)}, u32[]{:S(2)}, u32[]{:S(2)}) collective-permute-start(f32[3,32,4,128]{3,2,1,0:T(4,128)S(1)} %get-tuple-element.17), channel_id=1, source_target_pairs={{4,8},{12,16},{20,24},{28,32},{36,40},{44,48},{52,56},{60,0},{8,4}... | collective-permute-start | bytes 589832 | tf_op jit(solution)/shard_map/ppermute | solution.py:30
  40.6 0.6 collective-permute-start.9
  41.2 1.2 %collective-permute-start.8 = (f32[32,4,128]{2,1,0:T(4,128)S(1)}, f32[32,4,128]{2,1,0:T(4,128)S(1)}, u32[]{:S(2)}, u32[]{:S(2)}) collective-permute-start(f32[32,4,128]{2,1,0:T(4,128)S(1)} %get-tuple-element.13), channel_id=1, source_target_pairs={{0,2},{1,3},{2,0},{3,1},{4,6},{5,7},{6,4},{7,5},{8,10},{9,11},{10,... | collective-permute-start | bytes 196616 | tf_op jit(solution)/shard_map/ppermute | solution.py:361
  42.4 2.4 %collective-permute-start.7 = (f32[32,4,128]{2,1,0:T(4,128)S(1)}, f32[32,4,128]{2,1,0:T(4,128)S(1)}, u32[]{:S(2)}, u32[]{:S(2)}) collective-permute-start(f32[32,4,128]{2,1,0:T(4,128)S(1)} %get-tuple-element.12), channel_id=1, source_target_pairs={{0,1},{1,0},{2,3},{3,2},{4,5},{5,4},{6,7},{7,6},{8,9},{9,8},{10,11... | collective-permute-start | bytes 196616 | tf_op jit(solution)/shard_map/ppermute | solution.py:361
  44.8 0.0 collective-permute-done.11
  44.8 0.0 collective-permute-done.10
  44.8 0.0 copy-start.4
  44.9 10.7 %collective-permute-start.13 = (f32[32,4,128]{2,1,0:T(4,128)S(1)}, f32[32,4,128]{2,1,0:T(4,128)S(1)}, u32[]{:S(2)}, u32[]{:S(2)}) collective-permute-start(f32[32,4,128]{2,1,0:T(4,128)S(1)} %get-tuple-element.40), channel_id=1, source_target_pairs={{64,128},{192,0},{128,64},{0,192},{65,129},{193,1},{129,65},{1,193... | collective-permute-start | bytes 196616 | tf_op jit(solution)/shard_map/ppermute | solution.py:30
  55.6 0.0 collective-permute-start.12
  55.6 0.0 collective-permute-done.9
  55.6 2.4 %collective-permute-done.13 = f32[32,4,128]{2,1,0:T(4,128)S(1)} collective-permute-done((f32[32,4,128]{2,1,0:T(4,128)S(1)}, f32[32,4,128]{2,1,0:T(4,128)S(1)}, u32[]{:S(2)}, u32[]{:S(2)}) %collective-permute-start.13) | collective-permute-done | bytes 65568 | tf_op jit(solution)/shard_map/ppermute | solution.py:30
  58.0 1.8 %collective-permute-done.12 = f32[32,4,128]{2,1,0:T(4,128)S(1)} collective-permute-done((f32[32,4,128]{2,1,0:T(4,128)S(1)}, f32[32,4,128]{2,1,0:T(4,128)S(1)}, u32[]{:S(2)}, u32[]{:S(2)}) %collective-permute-start.12) | collective-permute-done | bytes 65568 | tf_op jit(solution)/shard_map/ppermute | solution.py:30
  59.9 0.7 broadcast_multiply_fusion
  60.6 0.6 gather_fusion
  61.2 0.1 broadcast_select_fusion
  61.3 0.1 broadcast_in_dim.107
  61.3 2.1 %collective-permute-start.15 = (f32[4,8,128]{2,1,0:T(8,128)S(1)}, f32[4,8,128]{2,1,0:T(8,128)S(1)}, u32[]{:S(2)}, u32[]{:S(2)}) collective-permute-start(f32[4,8,128]{2,1,0:T(8,128)S(1)} %get-tuple-element.45), channel_id=1, source_target_pairs={{64,128},{192,0},{128,64},{0,192},{65,129},{193,1},{129,65},{1,193... | collective-permute-start | bytes 49160 | tf_op jit(solution)/shard_map/ppermute | solution.py:30
  63.4 3.6 %collective-permute-done.15 = f32[4,8,128]{2,1,0:T(8,128)S(1)} collective-permute-done((f32[4,8,128]{2,1,0:T(8,128)S(1)}, f32[4,8,128]{2,1,0:T(8,128)S(1)}, u32[]{:S(2)}, u32[]{:S(2)}) %collective-permute-start.15) | collective-permute-done | bytes 16416 | tf_op jit(solution)/shard_map/ppermute | solution.py:30
  67.0 0.2 collective-permute-done.14
  67.2 0.1 collective-permute-start.17
  67.3 1.1 %collective-permute-done.16.refs_0_ = f32[3,4,8,128]{3,2,1,0:T(8,128)S(1)} collective-permute-done((f32[3,4,8,128]{3,2,1,0:T(8,128)S(1)}, f32[3,4,8,128]{3,2,1,0:T(8,128)S(1)}, u32[]{:S(2)}, u32[]{:S(2)}) %collective-permute-start.16) | collective-permute-done | bytes 49184 | tf_op jit(solution)/shard_map/ppermute | solution.py:30
  68.4 8.9 %collective-permute-done.17.refs_2_ = f32[3,4,8,128]{3,2,1,0:T(8,128)S(1)} collective-permute-done((f32[3,4,8,128]{3,2,1,0:T(8,128)S(1)}, f32[3,4,8,128]{3,2,1,0:T(8,128)S(1)}, u32[]{:S(2)}, u32[]{:S(2)}) %collective-permute-start.17) | collective-permute-done | bytes 49184 | tf_op jit(solution)/shard_map/ppermute | solution.py:30
  77.3 1.3 %arrivals.1 = f32[6,8,512]{2,1,0:T(8,128)} custom-call(s32[3]{0:T(128)S(1)} %pad_add_fusion.spot, f32[3,4,8,128]{3,2,1,0:T(8,128)S(1)} %collective-permute-done.16.refs_0_, f32[3,4,8,128]{3,2,1,0:T(8,128)S(1)} %pad_maximum_fusion.2.refs_1_, f32[3,4,8,128]{3,2,1,0:T(8,128)S(1)} %collective-permute-done.17.refs_2_), custom_call_target="tpu_custom_call" | custom-call | tf_op jit(solution)/shard_map/arrivals/pallas_call | solution.py:308
  (36 shorter events, 0.3 us)
Async XLA Ops:
  0.6 0.7 copy-start.7
  0.6 0.8 %copy-start.6 = (f32[4096]{0:T(1024)S(1)}, f32[4096]{0:T(1024)}, u32[]{:S(2)}) copy-start(f32[4096]{0:T(1024)} %param.17) | copy-start | bytes 49156
  0.7 3.1 %copy-start.3 = (f32[3,4096]{1,0:T(4,128)S(1)}, f32[3,4096]{1,0:T(4,128)}, u32[]{:S(2)}) copy-start(f32[3,4096]{1,0:T(4,128)} %param.15) | copy-start | bytes 147460
  3.7 1.7 %copy-start.5 = (f32[4096]{0:T(1024)S(1)}, f32[4096]{0:T(1024)}, u32[]{:S(2)}) copy-start(f32[4096]{0:T(1024)} %param.18) | copy-start | bytes 49156
  3.8 26.9 %copy-start = (s32[1,64,16,128]{3,2,1,0:T(8,128)S(1)}, s32[1,64,16,128]{3,2,1,0:T(8,128)}, u32[]{:S(2)}) copy-start(s32[1,64,16,128]{3,2,1,0:T(8,128)} %param.25) | copy-start | bytes 1572868
  5.5 22.2 %collective-permute-start = (f32[33,4,128]{2,1,0:T(4,128)S(1)}, f32[33,4,128]{2,1,0:T(4,128)S(1)}, u32[]{:S(2)}, u32[]{:S(2)}) collective-permute-start(f32[33,4,128]{2,1,0:T(4,128)S(1)} %get-tuple-element.43.refs_0_), channel_id=1, source_target_pairs={{0,1},{1,0},{2,3},{3,2},{4,5},{5,4},{6,7},{7,6},{8,9},{9,8},{10,11... | collective-permute-start | bytes 202760 | tf_op jit(solution)/shard_map/ppermute | solution.py:361
  6.4 21.3 %collective-permute-start.1 = (f32[33,4,128]{2,1,0:T(4,128)S(1)}, f32[33,4,128]{2,1,0:T(4,128)S(1)}, u32[]{:S(2)}, u32[]{:S(2)}) collective-permute-start(f32[33,4,128]{2,1,0:T(4,128)S(1)} %get-tuple-element.43.refs_0_), channel_id=1, source_target_pairs={{0,2},{1,3},{2,0},{3,1},{4,6},{5,7},{6,4},{7,5},{8,10},{9,11},{10,... | collective-permute-start | bytes 202760 | tf_op jit(solution)/shard_map/ppermute | solution.py:361
  9.2 18.5 %collective-permute-start.2 = (f32[33,4,128]{2,1,0:T(4,128)S(1)}, f32[33,4,128]{2,1,0:T(4,128)S(1)}, u32[]{:S(2)}, u32[]{:S(2)}) collective-permute-start(f32[33,4,128]{2,1,0:T(4,128)S(1)} %get-tuple-element.43.refs_0_), channel_id=1, source_target_pairs={{0,3},{1,2},{2,1},{3,0},{4,7},{5,6},{6,5},{7,4},{8,11},{9,10},{10,... | collective-permute-start | bytes 202760 | tf_op jit(solution)/shard_map/ppermute | solution.py:361
  10.2 7.0 %collective-permute-start.4 = (f32[33,4,128]{2,1,0:T(4,128)S(1)}, f32[33,4,128]{2,1,0:T(4,128)S(1)}, u32[]{:S(2)}, u32[]{:S(2)}) collective-permute-start(f32[33,4,128]{2,1,0:T(4,128)S(1)} %get-tuple-element.43.refs_0_), channel_id=1, source_target_pairs={{64,128},{192,0},{128,64},{0,192},{65,129},{193,1},{129,65},{1,193... | collective-permute-start | bytes 202760 | tf_op jit(solution)/shard_map/ppermute | solution.py:30
  14.9 4.3 %collective-permute-start.3 = (f32[33,4,128]{2,1,0:T(4,128)S(1)}, f32[33,4,128]{2,1,0:T(4,128)S(1)}, u32[]{:S(2)}, u32[]{:S(2)}) collective-permute-start(f32[33,4,128]{2,1,0:T(4,128)S(1)} %get-tuple-element.43.refs_0_), channel_id=1, source_target_pairs={{0,64},{128,192},{64,0},{192,128},{1,65},{129,193},{65,1},{193,129... | collective-permute-start | bytes 202760 | tf_op jit(solution)/shard_map/ppermute | solution.py:30
  19.2 8.5 %collective-permute-start.5 = (f32[3,33,4,128]{3,2,1,0:T(4,128)S(1)}, f32[3,33,4,128]{3,2,1,0:T(4,128)S(1)}, u32[]{:S(2)}, u32[]{:S(2)}) collective-permute-start(f32[3,33,4,128]{3,2,1,0:T(4,128)S(1)} %pad_maximum_fusion.refs_5_), channel_id=1, source_target_pairs={{0,4},{8,12},{16,20},{24,28},{32,36},{40,44},{48,52},{56,60},{4,0}... | collective-permute-start | bytes 608264 | tf_op jit(solution)/shard_map/ppermute | solution.py:30
  19.3 11.4 %collective-permute-start.6 = (f32[3,33,4,128]{3,2,1,0:T(4,128)S(1)}, f32[3,33,4,128]{3,2,1,0:T(4,128)S(1)}, u32[]{:S(2)}, u32[]{:S(2)}) collective-permute-start(f32[3,33,4,128]{3,2,1,0:T(4,128)S(1)} %pad_maximum_fusion.refs_5_), channel_id=1, source_target_pairs={{4,8},{12,16},{20,24},{28,32},{36,40},{44,48},{52,56},{60,0},{8,4}... | collective-permute-start | bytes 608264 | tf_op jit(solution)/shard_map/ppermute | solution.py:30
  27.7 3.0 %copy-start.1 = (s32[1,64]{1,0:T(1,128)S(1)}, s32[1,64]{1,0:T(1,128)}, u32[]{:S(2)}) copy-start(s32[1,64]{1,0:T(1,128)} %tower_list.1) | copy-start | bytes 772
  27.7 3.0 %copy-start.2 = (s32[1,64]{1,0:T(1,128)S(1)}, s32[1,64]{1,0:T(1,128)}, u32[]{:S(2)}) copy-start(s32[1,64]{1,0:T(1,128)} %plate_list.1) | copy-start | bytes 772
  32.9 7.7 %copy-start.8 = (s32[1,4]{1,0:T(1,128)S(1)}, s32[1,4]{1,0:T(1,128)}, u32[]{:S(2)}) copy-start(s32[1,4]{1,0:T(1,128)} %param.27) | copy-start | bytes 52
  33.0 11.8 %collective-permute-start.11 = (f32[3,32,4,128]{3,2,1,0:T(4,128)S(1)}, f32[3,32,4,128]{3,2,1,0:T(4,128)S(1)}, u32[]{:S(2)}, u32[]{:S(2)}) collective-permute-start(f32[3,32,4,128]{3,2,1,0:T(4,128)S(1)} %get-tuple-element.17), channel_id=1, source_target_pairs={{4,8},{12,16},{20,24},{28,32},{36,40},{44,48},{52,56},{60,0},{8,4}... | collective-permute-start | bytes 589832 | tf_op jit(solution)/shard_map/ppermute | solution.py:30
  40.6 4.2 %collective-permute-start.10 = (f32[3,32,4,128]{3,2,1,0:T(4,128)S(1)}, f32[3,32,4,128]{3,2,1,0:T(4,128)S(1)}, u32[]{:S(2)}, u32[]{:S(2)}) collective-permute-start(f32[3,32,4,128]{3,2,1,0:T(4,128)S(1)} %get-tuple-element.16), channel_id=1, source_target_pairs={{0,4},{8,12},{16,20},{24,28},{32,36},{40,44},{48,52},{56,60},{4,0}... | collective-permute-start | bytes 589832 | tf_op jit(solution)/shard_map/ppermute | solution.py:30
  40.6 15.0 %collective-permute-start.9 = (f32[32,4,128]{2,1,0:T(4,128)S(1)}, f32[32,4,128]{2,1,0:T(4,128)S(1)}, u32[]{:S(2)}, u32[]{:S(2)}) collective-permute-start(f32[32,4,128]{2,1,0:T(4,128)S(1)} %get-tuple-element.14), channel_id=1, source_target_pairs={{0,3},{1,2},{2,1},{3,0},{4,7},{5,6},{6,5},{7,4},{8,11},{9,10},{10,... | collective-permute-start | bytes 196616 | tf_op jit(solution)/shard_map/ppermute | solution.py:361
  41.2 14.5 %collective-permute-start.8 = (f32[32,4,128]{2,1,0:T(4,128)S(1)}, f32[32,4,128]{2,1,0:T(4,128)S(1)}, u32[]{:S(2)}, u32[]{:S(2)}) collective-permute-start(f32[32,4,128]{2,1,0:T(4,128)S(1)} %get-tuple-element.13), channel_id=1, source_target_pairs={{0,2},{1,3},{2,0},{3,1},{4,6},{5,7},{6,4},{7,5},{8,10},{9,11},{10,... | collective-permute-start | bytes 196616 | tf_op jit(solution)/shard_map/ppermute | solution.py:361
  42.4 13.3 %collective-permute-start.7 = (f32[32,4,128]{2,1,0:T(4,128)S(1)}, f32[32,4,128]{2,1,0:T(4,128)S(1)}, u32[]{:S(2)}, u32[]{:S(2)}) collective-permute-start(f32[32,4,128]{2,1,0:T(4,128)S(1)} %get-tuple-element.12), channel_id=1, source_target_pairs={{0,1},{1,0},{2,3},{3,2},{4,5},{5,4},{6,7},{7,6},{8,9},{9,8},{10,11... | collective-permute-start | bytes 196616 | tf_op jit(solution)/shard_map/ppermute | solution.py:361
  44.8 15.0 %copy-start.4 = (f32[3,4096]{1,0:T(4,128)S(1)}, f32[3,4096]{1,0:T(4,128)}, u32[]{:S(2)}) copy-start(f32[3,4096]{1,0:T(4,128)} %param.16) | copy-start | bytes 147460
  44.9 13.2 %collective-permute-start.13 = (f32[32,4,128]{2,1,0:T(4,128)S(1)}, f32[32,4,128]{2,1,0:T(4,128)S(1)}, u32[]{:S(2)}, u32[]{:S(2)}) collective-permute-start(f32[32,4,128]{2,1,0:T(4,128)S(1)} %get-tuple-element.40), channel_id=1, source_target_pairs={{64,128},{192,0},{128,64},{0,192},{65,129},{193,1},{129,65},{1,193... | collective-permute-start | bytes 196616 | tf_op jit(solution)/shard_map/ppermute | solution.py:30
  55.6 4.3 %collective-permute-start.12 = (f32[32,4,128]{2,1,0:T(4,128)S(1)}, f32[32,4,128]{2,1,0:T(4,128)S(1)}, u32[]{:S(2)}, u32[]{:S(2)}) collective-permute-start(f32[32,4,128]{2,1,0:T(4,128)S(1)} %get-tuple-element.41), channel_id=1, source_target_pairs={{0,64},{128,192},{64,0},{192,128},{1,65},{129,193},{65,1},{193,129... | collective-permute-start | bytes 196616 | tf_op jit(solution)/shard_map/ppermute | solution.py:30
  61.3 5.6 %collective-permute-start.15 = (f32[4,8,128]{2,1,0:T(8,128)S(1)}, f32[4,8,128]{2,1,0:T(8,128)S(1)}, u32[]{:S(2)}, u32[]{:S(2)}) collective-permute-start(f32[4,8,128]{2,1,0:T(8,128)S(1)} %get-tuple-element.45), channel_id=1, source_target_pairs={{64,128},{192,0},{128,64},{0,192},{65,129},{193,1},{129,65},{1,193... | collective-permute-start | bytes 49160 | tf_op jit(solution)/shard_map/ppermute | solution.py:30
  63.4 3.7 %collective-permute-start.14 = (f32[4,8,128]{2,1,0:T(8,128)S(1)}, f32[4,8,128]{2,1,0:T(8,128)S(1)}, u32[]{:S(2)}, u32[]{:S(2)}) collective-permute-start(f32[4,8,128]{2,1,0:T(8,128)S(1)} %get-tuple-element.45), channel_id=1, source_target_pairs={{0,64},{128,192},{64,0},{192,128},{1,65},{129,193},{65,1},{193,129... | collective-permute-start | bytes 49160 | tf_op jit(solution)/shard_map/ppermute | solution.py:30
  67.2 1.2 %collective-permute-start.16 = (f32[3,4,8,128]{3,2,1,0:T(8,128)S(1)}, f32[3,4,8,128]{3,2,1,0:T(8,128)S(1)}, u32[]{:S(2)}, u32[]{:S(2)}) collective-permute-start(f32[3,4,8,128]{3,2,1,0:T(8,128)S(1)} %pad_maximum_fusion.2.refs_1_), channel_id=1, source_target_pairs={{0,4},{8,12},{16,20},{24,28},{32,36},{40,44},{48,52},{56,60},{4,0}... | collective-permute-start | bytes 147464 | tf_op jit(solution)/shard_map/ppermute | solution.py:30
  67.2 10.1 %collective-permute-start.17 = (f32[3,4,8,128]{3,2,1,0:T(8,128)S(1)}, f32[3,4,8,128]{3,2,1,0:T(8,128)S(1)}, u32[]{:S(2)}, u32[]{:S(2)}) collective-permute-start(f32[3,4,8,128]{3,2,1,0:T(8,128)S(1)} %pad_maximum_fusion.2.refs_1_), channel_id=1, source_target_pairs={{4,8},{12,16},{20,24},{28,32},{36,40},{44,48},{52,56},{60,0},{8,4}... | collective-permute-start | bytes 147464 | tf_op jit(solution)/shard_map/ppermute | solution.py:30

commit v2 on v1

--- a/solution.py
+++ b/solution.py
@@ -45,11 +45,9 @@
         + swap(first, "gy", pairs_first(count_y))
         + swap(second, "gy", pairs_second(count_y))
     )
-    return (
-        row[1]
-        + swap(row[0], "gx", pairs_first(count_x))
-        + swap(row[2], "gx", pairs_second(count_x))
-    )
+    return [
+        row[1], swap(row[0], "gx", pairs_first(count_x)), swap(row[2], "gx", pairs_second(count_x))
+    ]
 
 
 def piece_of(offset, odd):
@@ -79,6 +77,8 @@
     plate_list,
     count,
     spot,
+    sigma_table,
+    epsilon_table,
     *refs,
 ):
     tower_refs, (first_row, own_row, second_row) = refs[0:4], refs[4:7]
@@ -125,16 +125,28 @@
         axis=1,
     ).astype(jnp.bfloat16)
     total = count[0]
+    sigmas = [jnp.full((1, 1), sigma_table[n]) for n in range(sigma_table.shape[0])]
+    depths = [jnp.sqrt(jnp.full((1, 1), epsilon_table[n])) for n in range(sigma_table.shape[0])]
+
+    def of_kind(table, kind):
+        value = table[0]
+        for n in range(1, len(table)):
+            value = jnp.where(kind == n, table[n], value)
+        return value
+
+
+    shift = blocks.bit_length() - 1
 
     def place(slot):
         tower, plate = tower_list[0, slot], plate_list[0, slot]
-        cell = plate // blocks
+        cell = jnp.right_shift(plate, shift)
+        cell_x = jnp.right_shift(cell * 11, 5)
         return (
-            jnp.bitwise_xor(tower // blocks, me_z),
-            tower % blocks,
-            piece_of(cell // 3, odd_x),
-            piece_of(cell % 3, odd_y),
-            plate % blocks,
+            jnp.bitwise_xor(jnp.right_shift(tower, shift), me_z),
+            jnp.bitwise_and(tower, blocks - 1),
+            piece_of(cell_x, odd_x),
+            piece_of(cell - 3 * cell_x, odd_y),
+            jnp.bitwise_and(plate, blocks - 1),
         )
 
     def tower_tile(layer, row):
@@ -165,8 +177,9 @@
         of_plate = jnp.sum(
             jnp.where(lane4 == plate_block, plate_kind, 0.0), axis=1, keepdims=True
         )
-        sigma = 0.5 * (of_tower[0:1] + of_plate[0:1])
-        depth = of_tower[1:2] * of_plate[1:2]
+        kind_one, kind_two = of_tower[0:1], of_plate[0:1]
+        sigma = 0.5 * (of_kind(sigmas, kind_one) + of_kind(sigmas, kind_two))
+        depth = of_kind(depths, kind_one) * of_kind(depths, kind_two)
         sigma_sq = sigma * sigma * (1.0 / unit_sq)
         sigma_six = sigma_sq * sigma_sq * sigma_sq
         low = jnp.broadcast_to(6.0 * depth * sigma_six, (8, lanes))
@@ -250,7 +263,7 @@
             first = (2 * index + half) * unroll
             for u in range(unroll):
                 prepare(first + unroll + u, buffers[1 - half], u)
-            done += [evaluate(first + u, buffers[half], u) for u in range(unroll)]
+                done.append(evaluate(first + u, buffers[half], u))
         finish(done)
         return carry
 
@@ -259,14 +272,14 @@
     lax.fori_loop(0, (total + 2 * unroll - 1) // (2 * unroll), step, 0)
 
 
-def pair_forces(tower_list, plate_list, count, spot, towers, rows, masks, lengths):
+def pair_forces(tower_list, plate_list, count, spot, tables, towers, rows, masks, lengths):
     blocks = towers[0].shape[0] - 1
     shape_one = jax.ShapeDtypeStruct((blocks, 4, lanes), jnp.float32)
     shape_row = jax.ShapeDtypeStruct((3, blocks, 4, lanes), jnp.float32)
     return pl.pallas_call(
         functools.partial(pair_kernel, *lengths, group),
         out_shape=[shape_one] * 4 + [shape_row] * 3,
-        in_specs=[smem()] * 4 + [vmem()] * 8,
+        in_specs=[smem()] * 6 + [vmem()] * 8,
         out_specs=[vmem()] * 7,
         scratch_shapes=[
             pltpu.VMEM((group, lanes, 4 * lanes), jnp.float32),
@@ -278,7 +291,7 @@
             flops=40 * 64 * lanes * lanes, bytes_accessed=2**21, transcendentals=64 * lanes * lanes
         ),
         name="pair_forces",
-    )(tower_list, plate_list, count, spot, *towers, *rows, masks)
+    )(tower_list, plate_list, count, spot, *tables, *towers, *rows, masks)
 
 
 def arrival_kernel(spot, *refs):
@@ -323,6 +336,42 @@
     return tiles.transpose(1, 0, 2).reshape(tiles.shape[1], -1)
 
 
+def kick_kernel(leaving, heading, features, half_kick, inv_mass, *refs):
+    parts, (positions, velocities, forces, state) = refs[:-4], refs[-4:]
+    blocks = half_kick.shape[0]
+    for b in range(blocks):
+        total = parts[0][b]
+        for part in parts[1:]:
+            total = total + part[b]
+        force = total[0:3]
+        forces[b] = force
+        velocities[b] = half_kick[b] + 0.5 * time_step * force * inv_mass[b : b + 1]
+        positions[b] = features[b, 0:3]
+    for q in range(leaving.shape[1]):
+        block = leaving[0, q]
+        state[q, 0:3] = features[block, 0:3]
+        state[q, 3:6] = velocities[block]
+        state[q, 6:8] = jnp.full((2, lanes), heading[0, q].astype(jnp.float32))
+    nothing = jnp.zeros((3, lanes), jnp.float32)
+    for q in range(leaving.shape[1]):
+        positions[leaving[0, q]] = nothing
+        velocities[leaving[0, q]] = nothing
+
+
+def kick(leaving, heading, features, half_kick, inv_mass, parts):
+    blocks = half_kick.shape[0]
+    shape = jax.ShapeDtypeStruct((blocks, 3, lanes), jnp.float32)
+    return pl.pallas_call(
+        kick_kernel,
+        out_shape=[shape] * 3
+        + [jax.ShapeDtypeStruct((leaving.shape[1], 8, lanes), jnp.float32)],
+        in_specs=[smem()] * 2 + [vmem()] * (3 + len(parts)),
+        out_specs=[vmem()] * 4,
+        compiler_params=pltpu.CompilerParams(vmem_limit_bytes=VMEM_LIMIT),
+        name="kick",
+    )(leaving, heading, features, half_kick, inv_mass.reshape(blocks, lanes), *parts)
+
+
 def local(
     positions,
     velocities,
@@ -339,17 +388,13 @@
     mig_block,
     mig_dest,
 ):
-    block_count = block_species.shape[0]
     layers = lax.axis_size("gz")
     length_x = float(lax.axis_size("gx"))
     length_y = float(lax.axis_size("gy"))
     half_kick = velocities + 0.5 * time_step * forces_old * inv_mass[None, :]
     moved = positions + time_step * half_kick
-    kinds = jnp.stack([sigma_table, jnp.sqrt(epsilon_table)])
-    per_block = jnp.zeros((2, block_count), jnp.float32)
-    for kind in range(sigma_table.shape[0]):
-        per_block = jnp.where(block_species[None, :] == kind, kinds[:, kind : kind + 1], per_block)
-    kind_tile = jnp.pad(per_block, ((0, 2), (0, lanes - block_count)))
+    kinds = block_species.astype(jnp.float32)
+    kind_tile = jnp.pad(kinds[None, :], ((0, 3), (0, lanes - kinds.shape[0])))
     features = jnp.concatenate(
         [by_block(jnp.concatenate([moved, charges[None, :]])), kind_tile[None]]
     )
@@ -366,28 +411,19 @@
         plate_index,
         tile_counts,
         spot,
+        (sigma_table, epsilon_table),
         towers,
         rows,
         exclusions[0],
         (length_x, length_y),
     )
-    tower_back = sums[0] + sum(from_layer(sums[step], step) for step in range(1, layers))
-    total = tower_back + sent_home(*sums[layers:])
-    forces_new = by_atom(total[:, 0:3])
-    velocity_full = half_kick + 0.5 * time_step * forces_new * inv_mass[None, :]
-    leaving = mig_block[0]
-    block_slots = jnp.arange(block_count, dtype=jnp.int32)
-    departed = jnp.any(leaving[:, None] == block_slots[None, :], axis=0)
-    staying = jnp.repeat(1.0 - departed.astype(jnp.float32), lanes)[None, :]
-    positions_new = moved * staying
-    velocities_new = velocity_full * staying
-    tags = jnp.broadcast_to(
-        mig_dest[0].astype(jnp.float32)[:, None, None], (leaving.shape[0], 2, lanes)
-    )
-    state = by_block(jnp.concatenate([moved, velocity_full]))
-    state = jnp.concatenate([jnp.take(state, leaving, axis=0), tags], axis=1)
+    parts = [sums[0]] + [from_layer(sums[step], step) for step in range(1, layers)]
+    parts += sent_home(*sums[layers:])
+    positions_new, velocities_new, forces_new, state = kick(
+        mig_block, mig_dest, features, by_block(half_kick), inv_mass, parts
+    )
     arrivals = arrivals_of(spot, halo(state))[:, None]
-    return (positions_new, velocities_new, forces_new, arrivals)
+    return (by_atom(positions_new), by_atom(velocities_new), by_atom(forces_new), arrivals)
 
 
 def solution(mesh):

time: 78.7 us -> 72.6 us (0.922)
  starting transfers between devices: 41.8 us -> 37.2 us
  other arithmetic: 4.21 us -> 2.61 us
  local copies, waits for them, and re-layouts: 2.26 us -> 0.72 us
  Pallas kernels: 3.5 us -> 4.69 us
    ppermute x12, starting transfers between devices: 32.9 us -> 28.4 us  [swap(): return lax.ppermute(value, axis, [*pairs, *((j, i) for i, j in pairs)])]
    ppermute x6, waiting for transfers between devices: 0.02 us -> 2.94 us  [from_layer(): return lax.ppermute(value, 'gz', [(i, i ^ step) for i in range(layers)])]
    ppermute x12, waiting for transfers between devices: 25.2 us -> 22.8 us  [swap(): return lax.ppermute(value, axis, [*pairs, *((j, i) for i, j in pairs)])]
    mul x2 -> x0, other arithmetic: 2.35 us -> none  [the longest x1 1.61 us: local(): positions_new = moved * staying]
    pallas_call x0 -> x1, Pallas kernels: none -> 1.3 us  [kick(): pl.pallas_call(kick_kernel, out_shape=[shape] * 3 + [jax.ShapeDtypeStruct...]
    transpose x2, other arithmetic: 0.06 us -> 1.04 us  [by_block(): return rows.reshape(rows.shape[0], -1, lanes).transpose(1, 0, 2)]
  transfers between devices with their start and end apart: 18 -> 18, of which waited for: 9 -> 10; matrix products, arithmetic and copies ran while one was open for 0% -> 0% of each run, Pallas kernels for 0% -> 0%
where the time goes in v2:
time: 72.6 us; the launch traced here: 72.4 us
  starting transfers between devices  37.2 us (51%)
  waiting for transfers between devices  25.8 us (36%)
  Pallas kernels  4.69 us (6%)
  other arithmetic  2.61 us (4%)
  between operations  1.43 us (2%)
    ppermute x12, starting transfers between devices, swap(): return lax.ppermute(value, axis, [*pairs, *((j, i) for i, j in pairs)])  28.4 us
    ppermute x12, waiting for transfers between devices, swap(): return lax.ppermute(value, axis, [*pairs, *((j, i) for i, j in pairs)])  22.8 us
    ppermute x6, starting transfers between devices, from_layer(): return lax.ppermute(value, 'gz', [(i, i ^ step) for i in range(layers)])  8.79 us
    ppermute x6, waiting for transfers between devices, from_layer(): return lax.ppermute(value, 'gz', [(i, i ^ step) for i in range(layers)])  2.94 us
    pallas_call x1, Pallas kernels, pair_forces(): pl.pallas_call(functools.partial(pair_kernel, *lengths, group), out_shape...  2.13 us
  transfers between devices with their start and end apart: 18, of which 10 were waited for; matrix products, arithmetic and copies ran while one was open for 0% of the time, Pallas kernels for 0%

profile of v2, /device:TPU:6, one launch (start us, length us, event | category | flops | bytes accessed | tf_op | source)
XLA Modules:
  0.0 72.4 jit_solution(3024867798283121878)
XLA Ops:
  0.6 0.7 convert_bitcast_fusion
  1.3 0.7 %broadcast_multiply_fusion = f32[4096]{0:T(1024)S(1)} fusion(f32[4096]{0:T(1024)} %param.17), kind=kLoop, calls=%fused_computation.11 | loop fusion | flops 4096 | bytes 32768 | tf_op jit(solution)/shard_map/mul | solution.py:394
  2.0 1.0 %fusion = (f32[32,3,128]{2,1,0:T(4,128)S(1)}, f32[3,32,128]{2,0,1:T(4,128)S(1)}) fusion(f32[3,4096]{1,0:T(4,128)} %param.15, f32[3,4096]{1,0:T(4,128)} %param.16, f32[4096]{0:T(1024)S(1)} %broadcast_multiply_fusion, f32[3,4096]{1,0:T(4,128)} %param.14), kind=kLoop, calls=%fused_computation.10 | loop fusion | flops 49152 | bytes 262144 | tf_op jit(solution)/shard_map/transpose | solution.py:332
  3.0 0.0 copy-done.8
  3.1 4.7 %collective-permute-start.4 = (f32[33,4,128]{2,1,0:T(4,128)S(1)}, f32[33,4,128]{2,1,0:T(4,128)S(1)}, u32[]{:S(2)}, u32[]{:S(2)}) collective-permute-start(f32[33,4,128]{2,1,0:T(4,128)S(1)} %get-tuple-element.36.refs_0_.features), channel_id=1, source_target_pairs={{64,128},{192,0},{128,64},{0,192},{65,129},{193,1},{129,65},{1,193... | collective-permute-start | bytes 202760 | tf_op jit(solution)/shard_map/ppermute | solution.py:30
  7.8 0.0 collective-permute-start.3
  7.8 3.0 %collective-permute-done.4 = f32[33,4,128]{2,1,0:T(4,128)S(1)} collective-permute-done((f32[33,4,128]{2,1,0:T(4,128)S(1)}, f32[33,4,128]{2,1,0:T(4,128)S(1)}, u32[]{:S(2)}, u32[]{:S(2)}) %collective-permute-start.4) | collective-permute-done | bytes 67616 | tf_op jit(solution)/shard_map/ppermute | solution.py:30
  10.8 1.3 %collective-permute-done.3 = f32[33,4,128]{2,1,0:T(4,128)S(1)} collective-permute-done((f32[33,4,128]{2,1,0:T(4,128)S(1)}, f32[33,4,128]{2,1,0:T(4,128)S(1)}, u32[]{:S(2)}, u32[]{:S(2)}) %collective-permute-start.3) | collective-permute-done | bytes 67616 | tf_op jit(solution)/shard_map/ppermute | solution.py:30
  12.2 6.4 %collective-permute-start.6 = (f32[3,33,4,128]{3,2,1,0:T(4,128)S(1)}, f32[3,33,4,128]{3,2,1,0:T(4,128)S(1)}, u32[]{:S(2)}, u32[]{:S(2)}) collective-permute-start(f32[3,33,4,128]{3,2,1,0:T(4,128)S(1)} %pad_maximum_fusion.refs_5_), channel_id=1, source_target_pairs={{4,8},{12,16},{20,24},{28,32},{36,40},{44,48},{52,56},{60,0},{8,4}... | collective-permute-start | bytes 608264 | tf_op jit(solution)/shard_map/ppermute | solution.py:30
  18.6 0.0 collective-permute-start.5
  18.6 0.5 collective-permute-start.2
  19.1 2.4 %collective-permute-start.1 = (f32[33,4,128]{2,1,0:T(4,128)S(1)}, f32[33,4,128]{2,1,0:T(4,128)S(1)}, u32[]{:S(2)}, u32[]{:S(2)}) collective-permute-start(f32[33,4,128]{2,1,0:T(4,128)S(1)} %get-tuple-element.36.refs_0_.features), channel_id=1, source_target_pairs={{0,2},{1,3},{2,0},{3,1},{4,6},{5,7},{6,4},{7,5},{8,10},{9,11},{10,... | collective-permute-start | bytes 202760 | tf_op jit(solution)/shard_map/ppermute | solution.py:406
  21.5 1.2 %collective-permute-start = (f32[33,4,128]{2,1,0:T(4,128)S(1)}, f32[33,4,128]{2,1,0:T(4,128)S(1)}, u32[]{:S(2)}, u32[]{:S(2)}) collective-permute-start(f32[33,4,128]{2,1,0:T(4,128)S(1)} %get-tuple-element.36.refs_0_.features), channel_id=1, source_target_pairs={{0,1},{1,0},{2,3},{3,2},{4,5},{5,4},{6,7},{7,6},{8,9},{9,8},{10,11... | collective-permute-start | bytes 202760 | tf_op jit(solution)/shard_map/ppermute | solution.py:406
  23.3 0.0 copy-start.7
  23.4 0.1 pad_add_fusion.spot
  23.4 2.4 %collective-permute-done.2.refs_3_ = f32[33,4,128]{2,1,0:T(4,128)S(1)} collective-permute-done((f32[33,4,128]{2,1,0:T(4,128)S(1)}, f32[33,4,128]{2,1,0:T(4,128)S(1)}, u32[]{:S(2)}, u32[]{:S(2)}) %collective-permute-start.2) | collective-permute-done | bytes 67616 | tf_op jit(solution)/shard_map/ppermute | solution.py:406
  25.8 0.0 collective-permute-done.1.refs_2_
  25.8 0.6 collective-permute-done.refs_1_
  26.4 0.0 collective-permute-done.6.refs_6_
  26.4 0.0 collective-permute-done.5.refs_4_
  26.4 2.1 %pair_forces.1 = (f32[32,4,128]{2,1,0:T(4,128)S(1)}, f32[32,4,128]{2,1,0:T(4,128)S(1)}, f32[32,4,128]{2,1,0:T(4,128)S(1)}, f32[32,4,128]{2,1,0:T(4,128)S(1)}, f3...) custom-call(s32[1,64]{1,0:T(1,128)S(1)} %copy-done.4, ...), custom_call_target="tpu_custom_call" | custom-call | flops 41943040 | bytes 2097152 | tf_op jit(solution)/shard_map/pair_forces/pallas_call | solution.py:279
  28.6 0.6 collective-permute-start.10
  29.1 5.6 %collective-permute-start.11 = (f32[3,32,4,128]{3,2,1,0:T(4,128)S(1)}, f32[3,32,4,128]{3,2,1,0:T(4,128)S(1)}, u32[]{:S(2)}, u32[]{:S(2)}) collective-permute-start(f32[3,32,4,128]{3,2,1,0:T(4,128)S(1)} %get-tuple-element.21), channel_id=1, source_target_pairs={{4,8},{12,16},{20,24},{28,32},{36,40},{44,48},{52,56},{60,0},{8,4}... | collective-permute-start | bytes 589832 | tf_op jit(solution)/shard_map/ppermute | solution.py:30
  34.7 0.0 collective-permute-start.7
  34.7 0.0 collective-permute-start.8
  34.7 4.7 %collective-permute-start.9 = (f32[32,4,128]{2,1,0:T(4,128)S(1)}, f32[32,4,128]{2,1,0:T(4,128)S(1)}, u32[]{:S(2)}, u32[]{:S(2)}) collective-permute-start(f32[32,4,128]{2,1,0:T(4,128)S(1)} %get-tuple-element.18), channel_id=1, source_target_pairs={{0,3},{1,2},{2,1},{3,0},{4,7},{5,6},{6,5},{7,4},{8,11},{9,10},{10,... | collective-permute-start | bytes 196616 | tf_op jit(solution)/shard_map/ppermute | solution.py:406
  39.4 0.0 collective-permute-done.10
  39.4 0.9 %collective-permute-done.11 = f32[3,32,4,128]{3,2,1,0:T(4,128)S(1)} collective-permute-done((f32[3,32,4,128]{3,2,1,0:T(4,128)S(1)}, f32[3,32,4,128]{3,2,1,0:T(4,128)S(1)}, u32[]{:S(2)}, u32[]{:S(2)}) %collective-permute-start.11) | collective-permute-done | bytes 196640 | tf_op jit(solution)/shard_map/ppermute | solution.py:30
  40.4 0.0 copy-start
  40.4 9.1 %collective-permute-start.13 = (f32[32,4,128]{2,1,0:T(4,128)S(1)}, f32[32,4,128]{2,1,0:T(4,128)S(1)}, u32[]{:S(2)}, u32[]{:S(2)}) collective-permute-start(f32[32,4,128]{2,1,0:T(4,128)S(1)} %get-tuple-element.30), channel_id=1, source_target_pairs={{64,128},{192,0},{128,64},{0,192},{65,129},{193,1},{129,65},{1,193... | collective-permute-start | bytes 196616 | tf_op jit(solution)/shard_map/ppermute | solution.py:30
  49.5 0.0 collective-permute-start.12
  49.5 0.0 collective-permute-done.7.refs_1_
  49.5 0.0 collective-permute-done.8.refs_2_
  49.5 0.0 collective-permute-done.9.refs_3_
  49.5 2.2 %collective-permute-done.13.refs_6_ = f32[32,4,128]{2,1,0:T(4,128)S(1)} collective-permute-done((f32[32,4,128]{2,1,0:T(4,128)S(1)}, f32[32,4,128]{2,1,0:T(4,128)S(1)}, u32[]{:S(2)}, u32[]{:S(2)}) %collective-permute-start.13) | collective-permute-done | bytes 65568 | tf_op jit(solution)/shard_map/ppermute | solution.py:30
  51.7 2.2 %collective-permute-done.12.refs_5_ = f32[32,4,128]{2,1,0:T(4,128)S(1)} collective-permute-done((f32[32,4,128]{2,1,0:T(4,128)S(1)}, f32[32,4,128]{2,1,0:T(4,128)S(1)}, u32[]{:S(2)}, u32[]{:S(2)}) %collective-permute-start.12) | collective-permute-done | bytes 65568 | tf_op jit(solution)/shard_map/ppermute | solution.py:30
  53.9 0.6 copy-done.1
  54.6 0.0 copy-done.2
  54.6 1.3 %kick.1 = (f32[32,3,128]{2,1,0:T(4,128)}, f32[32,3,128]{2,1,0:T(4,128)}, f32[32,3,128]{2,1,0:T(4,128)}, f32[4,8,128]{2,1,0:T(8,128)S(1)}) custom-call(s32[1,4]{1,0:T(1,128)S(1)} %copy-done.1, s32[1,4]{1,0:T(1,128)S(1)} %copy-done.2, f32[33,4,128]{2,1,0:T(4,128)S(1)} %get-tuple-element.36.refs_0_.features, f32[32,3,128]{2,1,0:T(4,128)S(1)} %get-tuple-element.33.half_kick, ...), custom_call_target="tpu_custom_call" | custom-call | tf_op jit(solution)/shard_map/kick/pallas_call | solution.py:364
  55.9 2.0 %collective-permute-start.15 = (f32[4,8,128]{2,1,0:T(8,128)S(1)}, f32[4,8,128]{2,1,0:T(8,128)S(1)}, u32[]{:S(2)}, u32[]{:S(2)}) collective-permute-start(f32[4,8,128]{2,1,0:T(8,128)S(1)} %get-tuple-element.25), channel_id=1, source_target_pairs={{64,128},{192,0},{128,64},{0,192},{65,129},{193,1},{129,65},{1,193... | collective-permute-start | bytes 49160 | tf_op jit(solution)/shard_map/ppermute | solution.py:30
  57.9 0.0 collective-permute-start.14
  57.9 3.6 %collective-permute-done.15 = f32[4,8,128]{2,1,0:T(8,128)S(1)} collective-permute-done((f32[4,8,128]{2,1,0:T(8,128)S(1)}, f32[4,8,128]{2,1,0:T(8,128)S(1)}, u32[]{:S(2)}, u32[]{:S(2)}) %collective-permute-start.15) | collective-permute-done | bytes 16416 | tf_op jit(solution)/shard_map/ppermute | solution.py:30
  61.4 0.2 collective-permute-done.14
  61.6 0.0 collective-permute-start.17
  61.6 0.1 collective-permute-start.16
  61.7 9.4 %collective-permute-done.17.refs_2_ = f32[3,4,8,128]{3,2,1,0:T(8,128)S(1)} collective-permute-done((f32[3,4,8,128]{3,2,1,0:T(8,128)S(1)}, f32[3,4,8,128]{3,2,1,0:T(8,128)S(1)}, u32[]{:S(2)}, u32[]{:S(2)}) %collective-permute-start.17) | collective-permute-done | bytes 49184 | tf_op jit(solution)/shard_map/ppermute | solution.py:30
  71.2 0.0 collective-permute-done.16.refs_0_
  71.2 1.3 %arrivals.1 = f32[6,8,512]{2,1,0:T(8,128)} custom-call(s32[3]{0:T(128)S(1)} %pad_add_fusion.spot, f32[3,4,8,128]{3,2,1,0:T(8,128)S(1)} %collective-permute-done.16.refs_0_, f32[3,4,8,128]{3,2,1,0:T(8,128)S(1)} %pad_maximum_fusion.2.refs_1_, f32[3,4,8,128]{3,2,1,0:T(8,128)S(1)} %collective-permute-done.17.refs_2_), custom_call_target="tpu_custom_call" | custom-call | tf_op jit(solution)/shard_map/arrivals/pallas_call | solution.py:321
  (20 shorter events, 0.2 us)
Async XLA Ops:
  1.3 1.7 %copy-start.8 = (f32[4096]{0:T(1024)S(1)}, f32[4096]{0:T(1024)}, u32[]{:S(2)}) copy-start(f32[4096]{0:T(1024)} %param.18) | copy-start | bytes 49156
  2.0 24.4 %copy-start.3 = (s32[1,64,16,128]{3,2,1,0:T(8,128)S(1)}, s32[1,64,16,128]{3,2,1,0:T(8,128)}, u32[]{:S(2)}) copy-start(s32[1,64,16,128]{3,2,1,0:T(8,128)} %param.25) | copy-start | bytes 1572868
  3.1 7.7 %collective-permute-start.4 = (f32[33,4,128]{2,1,0:T(4,128)S(1)}, f32[33,4,128]{2,1,0:T(4,128)S(1)}, u32[]{:S(2)}, u32[]{:S(2)}) collective-permute-start(f32[33,4,128]{2,1,0:T(4,128)S(1)} %get-tuple-element.36.refs_0_.features), channel_id=1, source_target_pairs={{64,128},{192,0},{128,64},{0,192},{65,129},{193,1},{129,65},{1,193... | collective-permute-start | bytes 202760 | tf_op jit(solution)/shard_map/ppermute | solution.py:30
  7.8 4.3 %collective-permute-start.3 = (f32[33,4,128]{2,1,0:T(4,128)S(1)}, f32[33,4,128]{2,1,0:T(4,128)S(1)}, u32[]{:S(2)}, u32[]{:S(2)}) collective-permute-start(f32[33,4,128]{2,1,0:T(4,128)S(1)} %get-tuple-element.36.refs_0_.features), channel_id=1, source_target_pairs={{0,64},{128,192},{64,0},{192,128},{1,65},{129,193},{65,1},{193,129... | collective-permute-start | bytes 202760 | tf_op jit(solution)/shard_map/ppermute | solution.py:30
  12.2 14.2 %collective-permute-start.6 = (f32[3,33,4,128]{3,2,1,0:T(4,128)S(1)}, f32[3,33,4,128]{3,2,1,0:T(4,128)S(1)}, u32[]{:S(2)}, u32[]{:S(2)}) collective-permute-start(f32[3,33,4,128]{3,2,1,0:T(4,128)S(1)} %pad_maximum_fusion.refs_5_), channel_id=1, source_target_pairs={{4,8},{12,16},{20,24},{28,32},{36,40},{44,48},{52,56},{60,0},{8,4}... | collective-permute-start | bytes 608264 | tf_op jit(solution)/shard_map/ppermute | solution.py:30
  18.6 7.8 %collective-permute-start.5 = (f32[3,33,4,128]{3,2,1,0:T(4,128)S(1)}, f32[3,33,4,128]{3,2,1,0:T(4,128)S(1)}, u32[]{:S(2)}, u32[]{:S(2)}) collective-permute-start(f32[3,33,4,128]{3,2,1,0:T(4,128)S(1)} %pad_maximum_fusion.refs_5_), channel_id=1, source_target_pairs={{0,4},{8,12},{16,20},{24,28},{32,36},{40,44},{48,52},{56,60},{4,0}... | collective-permute-start | bytes 608264 | tf_op jit(solution)/shard_map/ppermute | solution.py:30
  18.6 7.2 %collective-permute-start.2 = (f32[33,4,128]{2,1,0:T(4,128)S(1)}, f32[33,4,128]{2,1,0:T(4,128)S(1)}, u32[]{:S(2)}, u32[]{:S(2)}) collective-permute-start(f32[33,4,128]{2,1,0:T(4,128)S(1)} %get-tuple-element.36.refs_0_.features), channel_id=1, source_target_pairs={{0,3},{1,2},{2,1},{3,0},{4,7},{5,6},{6,5},{7,4},{8,11},{9,10},{10,... | collective-permute-start | bytes 202760 | tf_op jit(solution)/shard_map/ppermute | solution.py:406
  19.1 6.7 %collective-permute-start.1 = (f32[33,4,128]{2,1,0:T(4,128)S(1)}, f32[33,4,128]{2,1,0:T(4,128)S(1)}, u32[]{:S(2)}, u32[]{:S(2)}) collective-permute-start(f32[33,4,128]{2,1,0:T(4,128)S(1)} %get-tuple-element.36.refs_0_.features), channel_id=1, source_target_pairs={{0,2},{1,3},{2,0},{3,1},{4,6},{5,7},{6,4},{7,5},{8,10},{9,11},{10,... | collective-permute-start | bytes 202760 | tf_op jit(solution)/shard_map/ppermute | solution.py:406
  21.5 4.9 %collective-permute-start = (f32[33,4,128]{2,1,0:T(4,128)S(1)}, f32[33,4,128]{2,1,0:T(4,128)S(1)}, u32[]{:S(2)}, u32[]{:S(2)}) collective-permute-start(f32[33,4,128]{2,1,0:T(4,128)S(1)} %get-tuple-element.36.refs_0_.features), channel_id=1, source_target_pairs={{0,1},{1,0},{2,3},{3,2},{4,5},{5,4},{6,7},{7,6},{8,9},{9,8},{10,11... | collective-permute-start | bytes 202760 | tf_op jit(solution)/shard_map/ppermute | solution.py:406
  23.3 3.0 %copy-start.7 = (f32[4]{0:T(128)S(1)}, f32[4]{0:T(128)}, u32[]{:S(2)}) copy-start(f32[4]{0:T(128)} %epsilon_table.1) | copy-start | bytes 52
  23.4 3.0 %copy-start.4 = (s32[1,64]{1,0:T(1,128)S(1)}, s32[1,64]{1,0:T(1,128)}, u32[]{:S(2)}) copy-start(s32[1,64]{1,0:T(1,128)} %tower_list.1) | copy-start | bytes 772
  23.4 3.0 %copy-start.5 = (s32[1,64]{1,0:T(1,128)S(1)}, s32[1,64]{1,0:T(1,128)}, u32[]{:S(2)}) copy-start(s32[1,64]{1,0:T(1,128)} %plate_list.1) | copy-start | bytes 772
  23.4 3.0 %copy-start.6 = (f32[4]{0:T(128)S(1)}, f32[4]{0:T(128)}, u32[]{:S(2)}) copy-start(f32[4]{0:T(128)} %sigma_table.1) | copy-start | bytes 52
  28.6 10.8 %collective-permute-start.10 = (f32[3,32,4,128]{3,2,1,0:T(4,128)S(1)}, f32[3,32,4,128]{3,2,1,0:T(4,128)S(1)}, u32[]{:S(2)}, u32[]{:S(2)}) collective-permute-start(f32[3,32,4,128]{3,2,1,0:T(4,128)S(1)} %get-tuple-element.20), channel_id=1, source_target_pairs={{0,4},{8,12},{16,20},{24,28},{32,36},{40,44},{48,52},{56,60},{4,0}... | collective-permute-start | bytes 589832 | tf_op jit(solution)/shard_map/ppermute | solution.py:30
  29.1 11.2 %collective-permute-start.11 = (f32[3,32,4,128]{3,2,1,0:T(4,128)S(1)}, f32[3,32,4,128]{3,2,1,0:T(4,128)S(1)}, u32[]{:S(2)}, u32[]{:S(2)}) collective-permute-start(f32[3,32,4,128]{3,2,1,0:T(4,128)S(1)} %get-tuple-element.21), channel_id=1, source_target_pairs={{4,8},{12,16},{20,24},{28,32},{36,40},{44,48},{52,56},{60,0},{8,4}... | collective-permute-start | bytes 589832 | tf_op jit(solution)/shard_map/ppermute | solution.py:30
  34.7 14.8 %collective-permute-start.7 = (f32[32,4,128]{2,1,0:T(4,128)S(1)}, f32[32,4,128]{2,1,0:T(4,128)S(1)}, u32[]{:S(2)}, u32[]{:S(2)}) collective-permute-start(f32[32,4,128]{2,1,0:T(4,128)S(1)} %get-tuple-element.16), channel_id=1, source_target_pairs={{0,1},{1,0},{2,3},{3,2},{4,5},{5,4},{6,7},{7,6},{8,9},{9,8},{10,11... | collective-permute-start | bytes 196616 | tf_op jit(solution)/shard_map/ppermute | solution.py:406
  34.7 14.8 %collective-permute-start.8 = (f32[32,4,128]{2,1,0:T(4,128)S(1)}, f32[32,4,128]{2,1,0:T(4,128)S(1)}, u32[]{:S(2)}, u32[]{:S(2)}) collective-permute-start(f32[32,4,128]{2,1,0:T(4,128)S(1)} %get-tuple-element.17), channel_id=1, source_target_pairs={{0,2},{1,3},{2,0},{3,1},{4,6},{5,7},{6,4},{7,5},{8,10},{9,11},{10,... | collective-permute-start | bytes 196616 | tf_op jit(solution)/shard_map/ppermute | solution.py:406
  34.7 14.8 %collective-permute-start.9 = (f32[32,4,128]{2,1,0:T(4,128)S(1)}, f32[32,4,128]{2,1,0:T(4,128)S(1)}, u32[]{:S(2)}, u32[]{:S(2)}) collective-permute-start(f32[32,4,128]{2,1,0:T(4,128)S(1)} %get-tuple-element.18), channel_id=1, source_target_pairs={{0,3},{1,2},{2,1},{3,0},{4,7},{5,6},{6,5},{7,4},{8,11},{9,10},{10,... | collective-permute-start | bytes 196616 | tf_op jit(solution)/shard_map/ppermute | solution.py:406
  40.4 13.6 %copy-start = (f32[4096]{0:T(1024)S(1)}, f32[4096]{0:T(1024)}, u32[]{:S(2)}) copy-start(f32[4096]{0:T(1024)} %param.17) | copy-start | bytes 49156
  40.4 11.3 %collective-permute-start.13 = (f32[32,4,128]{2,1,0:T(4,128)S(1)}, f32[32,4,128]{2,1,0:T(4,128)S(1)}, u32[]{:S(2)}, u32[]{:S(2)}) collective-permute-start(f32[32,4,128]{2,1,0:T(4,128)S(1)} %get-tuple-element.30), channel_id=1, source_target_pairs={{64,128},{192,0},{128,64},{0,192},{65,129},{193,1},{129,65},{1,193... | collective-permute-start | bytes 196616 | tf_op jit(solution)/shard_map/ppermute | solution.py:30
  49.5 4.4 %collective-permute-start.12 = (f32[32,4,128]{2,1,0:T(4,128)S(1)}, f32[32,4,128]{2,1,0:T(4,128)S(1)}, u32[]{:S(2)}, u32[]{:S(2)}) collective-permute-start(f32[32,4,128]{2,1,0:T(4,128)S(1)} %get-tuple-element.31), channel_id=1, source_target_pairs={{0,64},{128,192},{64,0},{192,128},{1,65},{129,193},{65,1},{193,129... | collective-permute-start | bytes 196616 | tf_op jit(solution)/shard_map/ppermute | solution.py:30
  53.9 0.7 copy-start.1
  53.9 0.7 copy-start.2
  55.9 5.5 %collective-permute-start.15 = (f32[4,8,128]{2,1,0:T(8,128)S(1)}, f32[4,8,128]{2,1,0:T(8,128)S(1)}, u32[]{:S(2)}, u32[]{:S(2)}) collective-permute-start(f32[4,8,128]{2,1,0:T(8,128)S(1)} %get-tuple-element.25), channel_id=1, source_target_pairs={{64,128},{192,0},{128,64},{0,192},{65,129},{193,1},{129,65},{1,193... | collective-permute-start | bytes 49160 | tf_op jit(solution)/shard_map/ppermute | solution.py:30
  57.9 3.7 %collective-permute-start.14 = (f32[4,8,128]{2,1,0:T(8,128)S(1)}, f32[4,8,128]{2,1,0:T(8,128)S(1)}, u32[]{:S(2)}, u32[]{:S(2)}) collective-permute-start(f32[4,8,128]{2,1,0:T(8,128)S(1)} %get-tuple-element.25), channel_id=1, source_target_pairs={{0,64},{128,192},{64,0},{192,128},{1,65},{129,193},{65,1},{193,129... | collective-permute-start | bytes 49160 | tf_op jit(solution)/shard_map/ppermute | solution.py:30
  61.6 9.5 %collective-permute-start.17 = (f32[3,4,8,128]{3,2,1,0:T(8,128)S(1)}, f32[3,4,8,128]{3,2,1,0:T(8,128)S(1)}, u32[]{:S(2)}, u32[]{:S(2)}) collective-permute-start(f32[3,4,8,128]{3,2,1,0:T(8,128)S(1)} %pad_maximum_fusion.2.refs_1_), channel_id=1, source_target_pairs={{4,8},{12,16},{20,24},{28,32},{36,40},{44,48},{52,56},{60,0},{8,4}... | collective-permute-start | bytes 147464 | tf_op jit(solution)/shard_map/ppermute | solution.py:30
  61.6 9.5 %collective-permute-start.16 = (f32[3,4,8,128]{3,2,1,0:T(8,128)S(1)}, f32[3,4,8,128]{3,2,1,0:T(8,128)S(1)}, u32[]{:S(2)}, u32[]{:S(2)}) collective-permute-start(f32[3,4,8,128]{3,2,1,0:T(8,128)S(1)} %pad_maximum_fusion.2.refs_1_), channel_id=1, source_target_pairs={{0,4},{8,12},{16,20},{24,28},{32,36},{40,44},{48,52},{56,60},{4,0}... | collective-permute-start | bytes 147464 | tf_op jit(solution)/shard_map/ppermute | solution.py:30

commit v3 on v2

--- a/solution.py
+++ b/solution.py
@@ -73,6 +73,7 @@
     length_x,
     length_y,
     unroll,
+    late,
     tower_list,
     plate_list,
     count,
@@ -81,10 +82,17 @@
     epsilon_table,
     *refs,
 ):
-    tower_refs, (first_row, own_row, second_row) = refs[0:4], refs[4:7]
-    masks, tower_outs, row_outs, held = refs[7], refs[8:12], refs[12:15], refs[15:]
+    count_rows = 1 if late else 2
+    tower_refs, plate_rows_held, refs = refs[0:4], refs[4 : 4 + count_rows], refs[4 + count_rows :]
+    masks, refs = refs[0], refs[1:]
+    if late:
+        earlier, refs = refs[0:4], refs[4:]
+    tower_outs, row_outs, held = refs[0:4], refs[4 : 4 + count_rows], refs[4 + count_rows : -1]
+    listed_slots = refs[-1]
     blocks = tower_outs[0].shape[0]
-    for ref in (*tower_outs, *row_outs):
+    for z, ref in enumerate(tower_outs):
+        ref[...] = earlier[z][...] if late else jnp.zeros_like(ref)
+    for ref in row_outs:
         ref[...] = jnp.zeros_like(ref)
     odd_x, odd_y, me_z = (spot[n] for n in range(3))
     f32 = jnp.float32
@@ -124,7 +132,7 @@
         ],
         axis=1,
     ).astype(jnp.bfloat16)
-    total = count[0]
+    all_slots = count[0]
     sigmas = [jnp.full((1, 1), sigma_table[n]) for n in range(sigma_table.shape[0])]
     depths = [jnp.sqrt(jnp.full((1, 1), epsilon_table[n])) for n in range(sigma_table.shape[0])]
 
@@ -155,19 +163,33 @@
             layer < 2, near, jnp.where(layer == 2, tower_refs[2][row], tower_refs[3][row])
         )
 
-    last = tower_list.shape[1] - 1
+    spare = listed_slots.shape[0]
+    late_row = 2 * odd_y
+
+    def gather(step, found):
+        for u in range(8):
+            slot = 8 * step + u
+            cell = jnp.right_shift(plate_list[0, slot], shift)
+            is_late = (cell - 3 * jnp.right_shift(cell * 11, 5) == late_row).astype(jnp.int32)
+            listed_slots[found] = slot
+            found = found + jnp.where(slot < all_slots, is_late if late else 1 - is_late, 0)
+        return found
+
+    total = lax.fori_loop(0, tower_list.shape[1] // 8, gather, 0)
+
+    def slot_at(number):
+        slot = listed_slots[jnp.minimum(number, spare - 1)]
+        return jnp.where(number < total, slot, 0)
+
 
     def prepare(slot, buffer, u):
         spread_ref, terms_ref = buffer
-        layer, tower_block, cell_x, cell_y, plate_block = place(jnp.minimum(slot, last))
+        layer, tower_block, cell_x, cell_y, plate_block = place(slot_at(slot))
         tower_kind = tower_tile(layer, blocks)
 
         def chosen(row):
-            return jnp.where(
-                cell_y == 0,
-                first_row[cell_x, row],
-                jnp.where(cell_y == 1, own_row[cell_x, row], second_row[cell_x, row]),
-            )
+            found = [ref[cell_x, row] for ref in plate_rows_held]
+            return found[0] if late else jnp.where(cell_y == 0, found[0], found[1])
 
         plate_rows = chosen(plate_block) * scale
         plate_kind = chosen(blocks)
@@ -196,11 +218,11 @@
 
     def evaluate(slot, buffer, u):
         spread_ref, terms_ref = buffer
-        layer, tower_block, cell_x, cell_y, plate_block = place(slot)
+        layer, tower_block, cell_x, cell_y, plate_block = place(slot_at(slot))
         tower_rows = tower_tile(layer, tower_block) * tower_scale
         low, high = terms_ref[u, 0], terms_ref[u, 1]
         rows = [jnp.broadcast_to(tower_rows[c : c + 1], (8, lanes)) for c in range(4)]
-        words = masks[slot]
+        words = masks[slot_at(slot)]
         on_tower = [jnp.zeros((8, lanes), f32) for _ in range(3)]
         on_plate = [jnp.zeros((8, lanes), f32) for _ in range(3)]
         for w in range(lanes // 8):
@@ -253,7 +275,9 @@
             for z, ref in enumerate(tower_outs):
                 ref[tower_block] += jnp.where(layer == z, on_tower, 0.0)
             for y, ref in enumerate(row_outs):
-                ref[cell_x, plate_block] += jnp.where(cell_y == y, on_plate, 0.0)
+                ref[cell_x, plate_block] += (
+                    on_plate if late else jnp.where(cell_y == y, on_plate, 0.0)
+                )
 
     buffers = (held[0:2], held[2:4])
 
@@ -272,26 +296,31 @@
     lax.fori_loop(0, (total + 2 * unroll - 1) // (2 * unroll), step, 0)
 
 
-def pair_forces(tower_list, plate_list, count, spot, tables, towers, rows, masks, lengths):
+def pair_forces(lists, spot, tables, towers, rows, masks, lengths, earlier=()):
+    late = len(earlier) > 0
     blocks = towers[0].shape[0] - 1
+    slots = lists[0].shape[1]
     shape_one = jax.ShapeDtypeStruct((blocks, 4, lanes), jnp.float32)
     shape_row = jax.ShapeDtypeStruct((3, blocks, 4, lanes), jnp.float32)
+    flops = 20 * slots * lanes * lanes
+    size = 2 if late else group
     return pl.pallas_call(
-        functools.partial(pair_kernel, *lengths, group),
-        out_shape=[shape_one] * 4 + [shape_row] * 3,
-        in_specs=[smem()] * 6 + [vmem()] * 8,
-        out_specs=[vmem()] * 7,
+        functools.partial(pair_kernel, *lengths, size, late),
+        out_shape=[shape_one] * 4 + [shape_row] * len(rows),
+        in_specs=[smem()] * 6 + [vmem()] * (5 + len(rows) + len(earlier)),
+        out_specs=[vmem()] * (4 + len(rows)),
         scratch_shapes=[
-            pltpu.VMEM((group, lanes, 4 * lanes), jnp.float32),
-            pltpu.VMEM((group, 2, 8, lanes), jnp.float32),
+            pltpu.VMEM((size, lanes, 4 * lanes), jnp.float32),
+            pltpu.VMEM((size, 2, 8, lanes), jnp.float32),
         ]
-        * 2,
+        * 2
+        + [pltpu.SMEM((slots + 1,), jnp.int32)],
         compiler_params=pltpu.CompilerParams(vmem_limit_bytes=VMEM_LIMIT),
         cost_estimate=pl.CostEstimate(
-            flops=40 * 64 * lanes * lanes, bytes_accessed=2**21, transcendentals=64 * lanes * lanes
+            flops=flops, bytes_accessed=2**20, transcendentals=flops // 40
         ),
-        name="pair_forces",
-    )(tower_list, plate_list, count, spot, *tables, *towers, *rows, masks)
+        name="pairs_late" if late else "pairs_early",
+    )(*lists, spot, *tables, *towers, *rows, masks, *earlier)
 
 
 def arrival_kernel(spot, *refs):
@@ -336,8 +365,11 @@
     return tiles.transpose(1, 0, 2).reshape(tiles.shape[1], -1)
 
 
-def kick_kernel(leaving, heading, features, half_kick, inv_mass, *refs):
+def kick_kernel(spot, features, half_kick, inv_mass, *refs):
     parts, (positions, velocities, forces, state) = refs[:-4], refs[-4:]
+    count = state.shape[0]
+    leaving = [spot[3 + q] for q in range(count)]
+    heading = [spot[3 + count + q] for q in range(count)]
     blocks = half_kick.shape[0]
     for b in range(blocks):
         total = parts[0][b]
@@ -347,29 +379,29 @@
         forces[b] = force
         velocities[b] = half_kick[b] + 0.5 * time_step * force * inv_mass[b : b + 1]
         positions[b] = features[b, 0:3]
-    for q in range(leaving.shape[1]):
-        block = leaving[0, q]
+    for q in range(count):
+        block = leaving[q]
         state[q, 0:3] = features[block, 0:3]
         state[q, 3:6] = velocities[block]
-        state[q, 6:8] = jnp.full((2, lanes), heading[0, q].astype(jnp.float32))
+        state[q, 6:8] = jnp.full((2, lanes), heading[q].astype(jnp.float32))
     nothing = jnp.zeros((3, lanes), jnp.float32)
-    for q in range(leaving.shape[1]):
-        positions[leaving[0, q]] = nothing
-        velocities[leaving[0, q]] = nothing
-
-
-def kick(leaving, heading, features, half_kick, inv_mass, parts):
+    for q in range(count):
+        positions[leaving[q]] = nothing
+        velocities[leaving[q]] = nothing
+
+
+def kick(spot, count, features, half_kick, inv_mass, parts):
     blocks = half_kick.shape[0]
     shape = jax.ShapeDtypeStruct((blocks, 3, lanes), jnp.float32)
     return pl.pallas_call(
         kick_kernel,
         out_shape=[shape] * 3
-        + [jax.ShapeDtypeStruct((leaving.shape[1], 8, lanes), jnp.float32)],
-        in_specs=[smem()] * 2 + [vmem()] * (3 + len(parts)),
+        + [jax.ShapeDtypeStruct((count, 8, lanes), jnp.float32)],
+        in_specs=[smem()] + [vmem()] * (3 + len(parts)),
         out_specs=[vmem()] * 4,
         compiler_params=pltpu.CompilerParams(vmem_limit_bytes=VMEM_LIMIT),
         name="kick",
-    )(leaving, heading, features, half_kick, inv_mass.reshape(blocks, lanes), *parts)
+    )(spot, features, half_kick, inv_mass.reshape(blocks, lanes), *parts)
 
 
 def local(
@@ -400,27 +432,33 @@
     )
     me_x, me_y, me_z = (lax.axis_index(axis) for axis in ("gx", "gy", "gz"))
     spot = jnp.stack([me_x % 2, me_y % 2, me_z]).astype(jnp.int32)
+    spot = jnp.concatenate([spot, mig_block[0], mig_dest[0]])
     rows = halo(features)
 
     def from_layer(value, step):
         return lax.ppermute(value, "gz", [(i, i ^ step) for i in range(layers)])
 
     towers = [features] + [from_layer(features, step) for step in range(1, layers)]
-    sums = pair_forces(
-        tower_index,
-        plate_index,
-        tile_counts,
-        spot,
-        (sigma_table, epsilon_table),
-        towers,
-        rows,
-        exclusions[0],
-        (length_x, length_y),
-    )
+    first, own, second = rows
+
+    def pairs(rows, earlier=()):
+        return pair_forces(
+            (tower_index, plate_index, tile_counts),
+            spot,
+            (sigma_table, epsilon_table),
+            towers,
+            rows,
+            exclusions[0],
+            (length_x, length_y),
+            earlier,
+        )
+
+    *early, on_first, on_own = pairs((first, own))
+    *sums, on_second = pairs((second,), early)
     parts = [sums[0]] + [from_layer(sums[step], step) for step in range(1, layers)]
-    parts += sent_home(*sums[layers:])
+    parts += sent_home(on_first, on_own, on_second)
     positions_new, velocities_new, forces_new, state = kick(
-        mig_block, mig_dest, features, by_block(half_kick), inv_mass, parts
+        spot, mig_block.shape[1], features, by_block(half_kick), inv_mass, parts
     )
     arrivals = arrivals_of(spot, halo(state))[:, None]
     return (by_atom(positions_new), by_atom(velocities_new), by_atom(forces_new), arrivals)

time: 72.6 us -> 73.3 us (level)
  starting transfers between devices: 37.2 us -> 35.9 us
  waiting for transfers between devices: 25.8 us -> 26.8 us
  Pallas kernels: 4.69 us -> 5.62 us
    ppermute x12, waiting for transfers between devices: 22.8 us -> 25.1 us  [swap(): return lax.ppermute(value, axis, [*pairs, *((j, i) for i, j in pairs)])]
    ppermute x12, starting transfers between devices: 28.4 us -> 27.1 us  [swap(): return lax.ppermute(value, axis, [*pairs, *((j, i) for i, j in pairs)])]
    ppermute x6, waiting for transfers between devices: 2.94 us -> 1.67 us  [from_layer(): return lax.ppermute(value, 'gz', [(i, i ^ step) for i in range(layers)])]
    pallas_call x1 -> x2, Pallas kernels: 2.13 us -> 3.06 us  [pair_forces(): pl.pallas_call(functools.partial(pair_kernel, *lengths, size, late), out_...]
  transfers between devices with their start and end apart: 18 -> 18, of which waited for: 10 -> 10; matrix products, arithmetic and copies ran while one was open for 0% -> 0% of each run, Pallas kernels for 0% -> 2%
where the time goes in v3:
time: 73.3 us; the launch traced here: 73.1 us
  starting transfers between devices  35.9 us (49%)
  waiting for transfers between devices  26.8 us (37%)
  Pallas kernels  5.62 us (8%)
  other arithmetic  2.55 us (3%)
  between operations  1.46 us (2%)
  local copies, waits for them, and re-layouts  0.78 us (1%)
    ppermute x12, starting transfers between devices, swap(): return lax.ppermute(value, axis, [*pairs, *((j, i) for i, j in pairs)])  27.1 us
    ppermute x12, waiting for transfers between devices, swap(): return lax.ppermute(value, axis, [*pairs, *((j, i) for i, j in pairs)])  25.1 us
    ppermute x6, starting transfers between devices, from_layer(): return lax.ppermute(value, 'gz', [(i, i ^ step) for i in range(layers)])  8.79 us
    pallas_call x2, Pallas kernels, pair_forces(): pl.pallas_call(functools.partial(pair_kernel, *lengths, size, late), out_...  3.06 us
    ppermute x6, waiting for transfers between devices, from_layer(): return lax.ppermute(value, 'gz', [(i, i ^ step) for i in range(layers)])  1.67 us
  transfers between devices with their start and end apart: 18, of which 10 were waited for; matrix products, arithmetic and copies ran while one was open for 0% of the time, Pallas kernels for 2%

profile of v3, /device:TPU:6, one launch (start us, length us, event | category | flops | bytes accessed | tf_op | source)
XLA Modules:
  0.0 73.1 jit_solution(9756118377286956886)
XLA Ops:
  0.6 0.7 convert_bitcast_fusion
  1.3 0.7 %broadcast_multiply_fusion = f32[4096]{0:T(1024)S(1)} fusion(f32[4096]{0:T(1024)} %param.17), kind=kLoop, calls=%fused_computation.11 | loop fusion | flops 4096 | bytes 32768 | tf_op jit(solution)/shard_map/mul | solution.py:426
  2.0 1.0 %fusion = (f32[32,3,128]{2,1,0:T(4,128)S(1)}, f32[3,32,128]{2,0,1:T(4,128)S(1)}) fusion(f32[3,4096]{1,0:T(4,128)} %param.15, f32[3,4096]{1,0:T(4,128)} %param.16, f32[4096]{0:T(1024)S(1)} %broadcast_multiply_fusion, f32[3,4096]{1,0:T(4,128)} %param.14), kind=kLoop, calls=%fused_computation.10 | loop fusion | flops 49152 | bytes 262144 | tf_op jit(solution)/shard_map/transpose | solution.py:361
  3.1 4.7 %collective-permute-start.4 = (f32[33,4,128]{2,1,0:T(4,128)S(1)}, f32[33,4,128]{2,1,0:T(4,128)S(1)}, u32[]{:S(2)}, u32[]{:S(2)}) collective-permute-start(f32[33,4,128]{2,1,0:T(4,128)S(1)} %get-tuple-element.44.refs_0_.features), channel_id=1, source_target_pairs={{64,128},{192,0},{128,64},{0,192},{65,129},{193,1},{129,65},{1,193... | collective-permute-start | bytes 202760 | tf_op jit(solution)/shard_map/ppermute | solution.py:30
  7.8 0.0 collective-permute-start.3
  7.8 3.0 %collective-permute-done.4 = f32[33,4,128]{2,1,0:T(4,128)S(1)} collective-permute-done((f32[33,4,128]{2,1,0:T(4,128)S(1)}, f32[33,4,128]{2,1,0:T(4,128)S(1)}, u32[]{:S(2)}, u32[]{:S(2)}) %collective-permute-start.4) | collective-permute-done | bytes 67616 | tf_op jit(solution)/shard_map/ppermute | solution.py:30
  10.8 1.3 %collective-permute-done.3 = f32[33,4,128]{2,1,0:T(4,128)S(1)} collective-permute-done((f32[33,4,128]{2,1,0:T(4,128)S(1)}, f32[33,4,128]{2,1,0:T(4,128)S(1)}, u32[]{:S(2)}, u32[]{:S(2)}) %collective-permute-start.3) | collective-permute-done | bytes 67616 | tf_op jit(solution)/shard_map/ppermute | solution.py:30
  12.2 0.1 collective-permute-start.6
  12.3 7.8 %collective-permute-start.5 = (f32[3,33,4,128]{3,2,1,0:T(4,128)S(1)}, f32[3,33,4,128]{3,2,1,0:T(4,128)S(1)}, u32[]{:S(2)}, u32[]{:S(2)}) collective-permute-start(f32[3,33,4,128]{3,2,1,0:T(4,128)S(1)} %pad_maximum_fusion.refs_5_), channel_id=1, source_target_pairs={{4,8},{12,16},{20,24},{28,32},{36,40},{44,48},{52,56},{60,0},{8,4}... | collective-permute-start | bytes 608264 | tf_op jit(solution)/shard_map/ppermute | solution.py:30
  20.1 0.5 collective-permute-start.2
  20.6 2.4 %collective-permute-start.1 = (f32[33,4,128]{2,1,0:T(4,128)S(1)}, f32[33,4,128]{2,1,0:T(4,128)S(1)}, u32[]{:S(2)}, u32[]{:S(2)}) collective-permute-start(f32[33,4,128]{2,1,0:T(4,128)S(1)} %get-tuple-element.44.refs_0_.features), channel_id=1, source_target_pairs={{0,2},{1,3},{2,0},{3,1},{4,6},{5,7},{6,4},{7,5},{8,10},{9,11},{10,... | collective-permute-start | bytes 202760 | tf_op jit(solution)/shard_map/ppermute | solution.py:439
  23.0 1.2 %collective-permute-start = (f32[33,4,128]{2,1,0:T(4,128)S(1)}, f32[33,4,128]{2,1,0:T(4,128)S(1)}, u32[]{:S(2)}, u32[]{:S(2)}) collective-permute-start(f32[33,4,128]{2,1,0:T(4,128)S(1)} %get-tuple-element.44.refs_0_.features), channel_id=1, source_target_pairs={{0,1},{1,0},{2,3},{3,2},{4,5},{5,4},{6,7},{7,6},{8,9},{9,8},{10,11... | collective-permute-start | bytes 202760 | tf_op jit(solution)/shard_map/ppermute | solution.py:439
  24.8 0.0 copy-start.7
  24.8 0.0 copy-start.8
  24.9 0.6 copy-done.7
  25.5 0.0 copy-done.8
  25.5 0.1 concatenate.14.spot
  25.6 0.0 collective-permute-done.2.refs_3_
  25.6 0.7 %collective-permute-done.1.refs_2_ = f32[33,4,128]{2,1,0:T(4,128)S(1)} collective-permute-done((f32[33,4,128]{2,1,0:T(4,128)S(1)}, f32[33,4,128]{2,1,0:T(4,128)S(1)}, u32[]{:S(2)}, u32[]{:S(2)}) %collective-permute-start.1) | collective-permute-done | bytes 67616 | tf_op jit(solution)/shard_map/ppermute | solution.py:439
  26.3 0.9 %collective-permute-done.refs_1_ = f32[33,4,128]{2,1,0:T(4,128)S(1)} collective-permute-done((f32[33,4,128]{2,1,0:T(4,128)S(1)}, f32[33,4,128]{2,1,0:T(4,128)S(1)}, u32[]{:S(2)}, u32[]{:S(2)}) %collective-permute-start) | collective-permute-done | bytes 67616 | tf_op jit(solution)/shard_map/ppermute | solution.py:439
  27.3 0.0 collective-permute-done.6.refs_4_
  27.3 1.3 %pairs_early.1 = (f32[32,4,128]{2,1,0:T(4,128)S(1)}, f32[32,4,128]{2,1,0:T(4,128)S(1)}, f32[32,4,128]{2,1,0:T(4,128)S(1)}, f32[32,4,128]{2,1,0:T(4,128)S(1)}, f3...) custom-call(s32[1,64]{1,0:T(1,128)S(1)} %copy-done.2, s32[1,64]{1,0:T(1,128)S(1)} %copy-done.3, ...), custom_call_target="tpu_custom_call" | custom-call | flops 20971520 | bytes 1048576 | tf_op jit(solution)/shard_map/pairs_early/pallas_call | solution.py:307
  28.6 0.0 collective-permute-done.5.refs_4_
  28.6 1.8 %pairs_late.1 = (f32[32,4,128]{2,1,0:T(4,128)S(1)}, f32[32,4,128]{2,1,0:T(4,128)S(1)}, f32[32,4,128]{2,1,0:T(4,128)S(1)}, f32[32,4,128]{2,1,0:T(4,128)S(1)}, f32[3,32,4,128]{3,2,1,0:T(4,128)S(1)}) custom-call(s32[1,64]{1,0:T(1,128)S(1)} %copy-done.2, s32[1,64]{1,0:T(1,128)S(1)} %copy-done.3, s32[1]{0:T(128)S(6)} %copy.19.count, s32[11]{0:T(128)S(1)} %concatenate.14.spot, ...), custom_call_target="tpu_custom_call" | custom-call | flops 20971520 | bytes 1048576 | tf_op jit(solution)/shard_map/pairs_late/pallas_call | solution.py:307
  30.4 2.8 %collective-permute-start.11 = (f32[3,32,4,128]{3,2,1,0:T(4,128)S(1)}, f32[3,32,4,128]{3,2,1,0:T(4,128)S(1)}, u32[]{:S(2)}, u32[]{:S(2)}) collective-permute-start(f32[3,32,4,128]{3,2,1,0:T(4,128)S(1)} %get-tuple-element.29), channel_id=1, source_target_pairs={{4,8},{12,16},{20,24},{28,32},{36,40},{44,48},{52,56},{60,0},{8,4}... | collective-permute-start | bytes 589832 | tf_op jit(solution)/shard_map/ppermute | solution.py:30
  33.2 0.0 collective-permute-start.10
  33.2 0.2 collective-permute-start.7
  33.4 1.7 %collective-permute-start.8 = (f32[32,4,128]{2,1,0:T(4,128)S(1)}, f32[32,4,128]{2,1,0:T(4,128)S(1)}, u32[]{:S(2)}, u32[]{:S(2)}) collective-permute-start(f32[32,4,128]{2,1,0:T(4,128)S(1)} %get-tuple-element.25), channel_id=1, source_target_pairs={{0,2},{1,3},{2,0},{3,1},{4,6},{5,7},{6,4},{7,5},{8,10},{9,11},{10,... | collective-permute-start | bytes 196616 | tf_op jit(solution)/shard_map/ppermute | solution.py:439
  35.1 2.8 %collective-permute-start.9 = (f32[32,4,128]{2,1,0:T(4,128)S(1)}, f32[32,4,128]{2,1,0:T(4,128)S(1)}, u32[]{:S(2)}, u32[]{:S(2)}) collective-permute-start(f32[32,4,128]{2,1,0:T(4,128)S(1)} %get-tuple-element.26), channel_id=1, source_target_pairs={{0,3},{1,2},{2,1},{3,0},{4,7},{5,6},{6,5},{7,4},{8,11},{9,10},{10,... | collective-permute-start | bytes 196616 | tf_op jit(solution)/shard_map/ppermute | solution.py:439
  37.9 3.8 %collective-permute-done.11 = f32[3,32,4,128]{3,2,1,0:T(4,128)S(1)} collective-permute-done((f32[3,32,4,128]{3,2,1,0:T(4,128)S(1)}, f32[3,32,4,128]{3,2,1,0:T(4,128)S(1)}, u32[]{:S(2)}, u32[]{:S(2)}) %collective-permute-start.11) | collective-permute-done | bytes 196640 | tf_op jit(solution)/shard_map/ppermute | solution.py:30
  41.6 0.0 collective-permute-done.10
  41.7 0.0 copy-start.1
  41.7 9.3 %collective-permute-start.13 = (f32[32,4,128]{2,1,0:T(4,128)S(1)}, f32[32,4,128]{2,1,0:T(4,128)S(1)}, u32[]{:S(2)}, u32[]{:S(2)}) collective-permute-start(f32[32,4,128]{2,1,0:T(4,128)S(1)} %get-tuple-element.38), channel_id=1, source_target_pairs={{64,128},{192,0},{128,64},{0,192},{65,129},{193,1},{129,65},{1,193... | collective-permute-start | bytes 196616 | tf_op jit(solution)/shard_map/ppermute | solution.py:30
  51.0 0.0 collective-permute-start.12
  51.0 0.0 collective-permute-done.7.refs_1_
  51.0 0.0 collective-permute-done.9.refs_3_
  51.0 2.6 %collective-permute-done.13.refs_6_ = f32[32,4,128]{2,1,0:T(4,128)S(1)} collective-permute-done((f32[32,4,128]{2,1,0:T(4,128)S(1)}, f32[32,4,128]{2,1,0:T(4,128)S(1)}, u32[]{:S(2)}, u32[]{:S(2)}) %collective-permute-start.13) | collective-permute-done | bytes 65568 | tf_op jit(solution)/shard_map/ppermute | solution.py:30
  53.6 1.7 %collective-permute-done.12.refs_5_ = f32[32,4,128]{2,1,0:T(4,128)S(1)} collective-permute-done((f32[32,4,128]{2,1,0:T(4,128)S(1)}, f32[32,4,128]{2,1,0:T(4,128)S(1)}, u32[]{:S(2)}, u32[]{:S(2)}) %collective-permute-start.12) | collective-permute-done | bytes 65568 | tf_op jit(solution)/shard_map/ppermute | solution.py:30
  55.3 1.3 %kick.1 = (f32[32,3,128]{2,1,0:T(4,128)}, f32[32,3,128]{2,1,0:T(4,128)}, f32[32,3,128]{2,1,0:T(4,128)}, f32[4,8,128]{2,1,0:T(8,128)S(1)}) custom-call(s32[11]{0:T(128)S(1)} %concatenate.14.spot, f32[33,4,128]{2,1,0:T(4,128)S(1)} %get-tuple-element.44.refs_0_.features, f32[32,3,128]{2,1,0:T(4,128)S(1)} %get-tuple-element.41.half_kick, ...), custom_call_target="tpu_custom_call" | custom-call | tf_op jit(solution)/shard_map/kick/pallas_call | solution.py:396
  56.6 1.8 %collective-permute-start.15 = (f32[4,8,128]{2,1,0:T(8,128)S(1)}, f32[4,8,128]{2,1,0:T(8,128)S(1)}, u32[]{:S(2)}, u32[]{:S(2)}) collective-permute-start(f32[4,8,128]{2,1,0:T(8,128)S(1)} %get-tuple-element.33), channel_id=1, source_target_pairs={{64,128},{192,0},{128,64},{0,192},{65,129},{193,1},{129,65},{1,193... | collective-permute-start | bytes 49160 | tf_op jit(solution)/shard_map/ppermute | solution.py:30
  58.4 0.0 collective-permute-start.14
  58.4 3.7 %collective-permute-done.15 = f32[4,8,128]{2,1,0:T(8,128)S(1)} collective-permute-done((f32[4,8,128]{2,1,0:T(8,128)S(1)}, f32[4,8,128]{2,1,0:T(8,128)S(1)}, u32[]{:S(2)}, u32[]{:S(2)}) %collective-permute-start.15) | collective-permute-done | bytes 16416 | tf_op jit(solution)/shard_map/ppermute | solution.py:30
  62.1 0.2 collective-permute-done.14
  62.3 0.6 collective-permute-start.17
  62.9 0.0 collective-permute-start.16
  62.9 8.9 %collective-permute-done.17.refs_2_ = f32[3,4,8,128]{3,2,1,0:T(8,128)S(1)} collective-permute-done((f32[3,4,8,128]{3,2,1,0:T(8,128)S(1)}, f32[3,4,8,128]{3,2,1,0:T(8,128)S(1)}, u32[]{:S(2)}, u32[]{:S(2)}) %collective-permute-start.17) | collective-permute-done | bytes 49184 | tf_op jit(solution)/shard_map/ppermute | solution.py:30
  71.8 0.0 collective-permute-done.16.refs_0_
  71.8 1.3 %arrivals.1 = f32[6,8,512]{2,1,0:T(8,128)} custom-call(s32[11]{0:T(128)S(1)} %concatenate.14.spot, f32[3,4,8,128]{3,2,1,0:T(8,128)S(1)} %collective-permute-done.16.refs_0_, f32[3,4,8,128]{3,2,1,0:T(8,128)S(1)} %pad_maximum_fusion.2.refs_1_, f32[3,4,8,128]{3,2,1,0:T(8,128)S(1)} %collective-permute-done.17.refs_2_), custom_call_target="tpu_custom_call" | custom-call | tf_op jit(solution)/shard_map/arrivals/pallas_call | solution.py:350
  (21 shorter events, 0.2 us)
Async XLA Ops:
  1.3 1.7 %copy-start.6 = (f32[4096]{0:T(1024)S(1)}, f32[4096]{0:T(1024)}, u32[]{:S(2)}) copy-start(f32[4096]{0:T(1024)} %param.18) | copy-start | bytes 49156
  2.0 25.2 %copy-start = (s32[1,64,16,128]{3,2,1,0:T(8,128)S(1)}, s32[1,64,16,128]{3,2,1,0:T(8,128)}, u32[]{:S(2)}) copy-start(s32[1,64,16,128]{3,2,1,0:T(8,128)} %param.25) | copy-start | bytes 1572868
  3.1 7.7 %collective-permute-start.4 = (f32[33,4,128]{2,1,0:T(4,128)S(1)}, f32[33,4,128]{2,1,0:T(4,128)S(1)}, u32[]{:S(2)}, u32[]{:S(2)}) collective-permute-start(f32[33,4,128]{2,1,0:T(4,128)S(1)} %get-tuple-element.44.refs_0_.features), channel_id=1, source_target_pairs={{64,128},{192,0},{128,64},{0,192},{65,129},{193,1},{129,65},{1,193... | collective-permute-start | bytes 202760 | tf_op jit(solution)/shard_map/ppermute | solution.py:30
  7.8 4.3 %collective-permute-start.3 = (f32[33,4,128]{2,1,0:T(4,128)S(1)}, f32[33,4,128]{2,1,0:T(4,128)S(1)}, u32[]{:S(2)}, u32[]{:S(2)}) collective-permute-start(f32[33,4,128]{2,1,0:T(4,128)S(1)} %get-tuple-element.44.refs_0_.features), channel_id=1, source_target_pairs={{0,64},{128,192},{64,0},{192,128},{1,65},{129,193},{65,1},{193,129... | collective-permute-start | bytes 202760 | tf_op jit(solution)/shard_map/ppermute | solution.py:30
  12.2 15.1 %collective-permute-start.6 = (f32[3,33,4,128]{3,2,1,0:T(4,128)S(1)}, f32[3,33,4,128]{3,2,1,0:T(4,128)S(1)}, u32[]{:S(2)}, u32[]{:S(2)}) collective-permute-start(f32[3,33,4,128]{3,2,1,0:T(4,128)S(1)} %pad_maximum_fusion.refs_5_), channel_id=1, source_target_pairs={{0,4},{8,12},{16,20},{24,28},{32,36},{40,44},{48,52},{56,60},{4,0}... | collective-permute-start | bytes 608264 | tf_op jit(solution)/shard_map/ppermute | solution.py:30
  12.3 16.3 %collective-permute-start.5 = (f32[3,33,4,128]{3,2,1,0:T(4,128)S(1)}, f32[3,33,4,128]{3,2,1,0:T(4,128)S(1)}, u32[]{:S(2)}, u32[]{:S(2)}) collective-permute-start(f32[3,33,4,128]{3,2,1,0:T(4,128)S(1)} %pad_maximum_fusion.refs_5_), channel_id=1, source_target_pairs={{4,8},{12,16},{20,24},{28,32},{36,40},{44,48},{52,56},{60,0},{8,4}... | collective-permute-start | bytes 608264 | tf_op jit(solution)/shard_map/ppermute | solution.py:30
  20.1 5.5 %collective-permute-start.2 = (f32[33,4,128]{2,1,0:T(4,128)S(1)}, f32[33,4,128]{2,1,0:T(4,128)S(1)}, u32[]{:S(2)}, u32[]{:S(2)}) collective-permute-start(f32[33,4,128]{2,1,0:T(4,128)S(1)} %get-tuple-element.44.refs_0_.features), channel_id=1, source_target_pairs={{0,3},{1,2},{2,1},{3,0},{4,7},{5,6},{6,5},{7,4},{8,11},{9,10},{10,... | collective-permute-start | bytes 202760 | tf_op jit(solution)/shard_map/ppermute | solution.py:439
  20.6 5.8 %collective-permute-start.1 = (f32[33,4,128]{2,1,0:T(4,128)S(1)}, f32[33,4,128]{2,1,0:T(4,128)S(1)}, u32[]{:S(2)}, u32[]{:S(2)}) collective-permute-start(f32[33,4,128]{2,1,0:T(4,128)S(1)} %get-tuple-element.44.refs_0_.features), channel_id=1, source_target_pairs={{0,2},{1,3},{2,0},{3,1},{4,6},{5,7},{6,4},{7,5},{8,10},{9,11},{10,... | collective-permute-start | bytes 202760 | tf_op jit(solution)/shard_map/ppermute | solution.py:439
  23.0 4.3 %collective-permute-start = (f32[33,4,128]{2,1,0:T(4,128)S(1)}, f32[33,4,128]{2,1,0:T(4,128)S(1)}, u32[]{:S(2)}, u32[]{:S(2)}) collective-permute-start(f32[33,4,128]{2,1,0:T(4,128)S(1)} %get-tuple-element.44.refs_0_.features), channel_id=1, source_target_pairs={{0,1},{1,0},{2,3},{3,2},{4,5},{5,4},{6,7},{7,6},{8,9},{9,8},{10,11... | collective-permute-start | bytes 202760 | tf_op jit(solution)/shard_map/ppermute | solution.py:439
  24.8 0.7 copy-start.7
  24.8 0.7 copy-start.8
  25.5 1.8 %copy-start.5 = (f32[4]{0:T(128)S(1)}, f32[4]{0:T(128)}, u32[]{:S(2)}) copy-start(f32[4]{0:T(128)} %epsilon_table.3) | copy-start | bytes 52
  25.6 1.7 %copy-start.2 = (s32[1,64]{1,0:T(1,128)S(1)}, s32[1,64]{1,0:T(1,128)}, u32[]{:S(2)}) copy-start(s32[1,64]{1,0:T(1,128)} %tower_list.3) | copy-start | bytes 772
  25.6 1.7 %copy-start.3 = (s32[1,64]{1,0:T(1,128)S(1)}, s32[1,64]{1,0:T(1,128)}, u32[]{:S(2)}) copy-start(s32[1,64]{1,0:T(1,128)} %plate_list.3) | copy-start | bytes 772
  25.6 1.7 %copy-start.4 = (f32[4]{0:T(128)S(1)}, f32[4]{0:T(128)}, u32[]{:S(2)}) copy-start(f32[4]{0:T(128)} %sigma_table.3) | copy-start | bytes 52
  30.4 11.3 %collective-permute-start.11 = (f32[3,32,4,128]{3,2,1,0:T(4,128)S(1)}, f32[3,32,4,128]{3,2,1,0:T(4,128)S(1)}, u32[]{:S(2)}, u32[]{:S(2)}) collective-permute-start(f32[3,32,4,128]{3,2,1,0:T(4,128)S(1)} %get-tuple-element.29), channel_id=1, source_target_pairs={{4,8},{12,16},{20,24},{28,32},{36,40},{44,48},{52,56},{60,0},{8,4}... | collective-permute-start | bytes 589832 | tf_op jit(solution)/shard_map/ppermute | solution.py:30
  33.2 8.5 %collective-permute-start.10 = (f32[3,32,4,128]{3,2,1,0:T(4,128)S(1)}, f32[3,32,4,128]{3,2,1,0:T(4,128)S(1)}, u32[]{:S(2)}, u32[]{:S(2)}) collective-permute-start(f32[3,32,4,128]{3,2,1,0:T(4,128)S(1)} %get-tuple-element.28), channel_id=1, source_target_pairs={{0,4},{8,12},{16,20},{24,28},{32,36},{40,44},{48,52},{56,60},{4,0}... | collective-permute-start | bytes 589832 | tf_op jit(solution)/shard_map/ppermute | solution.py:30
  33.2 17.8 %collective-permute-start.7 = (f32[32,4,128]{2,1,0:T(4,128)S(1)}, f32[32,4,128]{2,1,0:T(4,128)S(1)}, u32[]{:S(2)}, u32[]{:S(2)}) collective-permute-start(f32[32,4,128]{2,1,0:T(4,128)S(1)} %get-tuple-element.24), channel_id=1, source_target_pairs={{0,1},{1,0},{2,3},{3,2},{4,5},{5,4},{6,7},{7,6},{8,9},{9,8},{10,11... | collective-permute-start | bytes 196616 | tf_op jit(solution)/shard_map/ppermute | solution.py:439
  33.4 17.6 %collective-permute-start.8 = (f32[32,4,128]{2,1,0:T(4,128)S(1)}, f32[32,4,128]{2,1,0:T(4,128)S(1)}, u32[]{:S(2)}, u32[]{:S(2)}) collective-permute-start(f32[32,4,128]{2,1,0:T(4,128)S(1)} %get-tuple-element.25), channel_id=1, source_target_pairs={{0,2},{1,3},{2,0},{3,1},{4,6},{5,7},{6,4},{7,5},{8,10},{9,11},{10,... | collective-permute-start | bytes 196616 | tf_op jit(solution)/shard_map/ppermute | solution.py:439
  35.1 15.9 %collective-permute-start.9 = (f32[32,4,128]{2,1,0:T(4,128)S(1)}, f32[32,4,128]{2,1,0:T(4,128)S(1)}, u32[]{:S(2)}, u32[]{:S(2)}) collective-permute-start(f32[32,4,128]{2,1,0:T(4,128)S(1)} %get-tuple-element.26), channel_id=1, source_target_pairs={{0,3},{1,2},{2,1},{3,0},{4,7},{5,6},{6,5},{7,4},{8,11},{9,10},{10,... | collective-permute-start | bytes 196616 | tf_op jit(solution)/shard_map/ppermute | solution.py:439
  41.7 13.6 %copy-start.1 = (f32[4096]{0:T(1024)S(1)}, f32[4096]{0:T(1024)}, u32[]{:S(2)}) copy-start(f32[4096]{0:T(1024)} %param.17) | copy-start | bytes 49156
  41.7 11.9 %collective-permute-start.13 = (f32[32,4,128]{2,1,0:T(4,128)S(1)}, f32[32,4,128]{2,1,0:T(4,128)S(1)}, u32[]{:S(2)}, u32[]{:S(2)}) collective-permute-start(f32[32,4,128]{2,1,0:T(4,128)S(1)} %get-tuple-element.38), channel_id=1, source_target_pairs={{64,128},{192,0},{128,64},{0,192},{65,129},{193,1},{129,65},{1,193... | collective-permute-start | bytes 196616 | tf_op jit(solution)/shard_map/ppermute | solution.py:30
  51.0 4.3 %collective-permute-start.12 = (f32[32,4,128]{2,1,0:T(4,128)S(1)}, f32[32,4,128]{2,1,0:T(4,128)S(1)}, u32[]{:S(2)}, u32[]{:S(2)}) collective-permute-start(f32[32,4,128]{2,1,0:T(4,128)S(1)} %get-tuple-element.39), channel_id=1, source_target_pairs={{0,64},{128,192},{64,0},{192,128},{1,65},{129,193},{65,1},{193,129... | collective-permute-start | bytes 196616 | tf_op jit(solution)/shard_map/ppermute | solution.py:30
  56.6 5.6 %collective-permute-start.15 = (f32[4,8,128]{2,1,0:T(8,128)S(1)}, f32[4,8,128]{2,1,0:T(8,128)S(1)}, u32[]{:S(2)}, u32[]{:S(2)}) collective-permute-start(f32[4,8,128]{2,1,0:T(8,128)S(1)} %get-tuple-element.33), channel_id=1, source_target_pairs={{64,128},{192,0},{128,64},{0,192},{65,129},{193,1},{129,65},{1,193... | collective-permute-start | bytes 49160 | tf_op jit(solution)/shard_map/ppermute | solution.py:30
  58.4 3.9 %collective-permute-start.14 = (f32[4,8,128]{2,1,0:T(8,128)S(1)}, f32[4,8,128]{2,1,0:T(8,128)S(1)}, u32[]{:S(2)}, u32[]{:S(2)}) collective-permute-start(f32[4,8,128]{2,1,0:T(8,128)S(1)} %get-tuple-element.33), channel_id=1, source_target_pairs={{0,64},{128,192},{64,0},{192,128},{1,65},{129,193},{65,1},{193,129... | collective-permute-start | bytes 49160 | tf_op jit(solution)/shard_map/ppermute | solution.py:30
  62.3 9.5 %collective-permute-start.17 = (f32[3,4,8,128]{3,2,1,0:T(8,128)S(1)}, f32[3,4,8,128]{3,2,1,0:T(8,128)S(1)}, u32[]{:S(2)}, u32[]{:S(2)}) collective-permute-start(f32[3,4,8,128]{3,2,1,0:T(8,128)S(1)} %pad_maximum_fusion.2.refs_1_), channel_id=1, source_target_pairs={{4,8},{12,16},{20,24},{28,32},{36,40},{44,48},{52,56},{60,0},{8,4}... | collective-permute-start | bytes 147464 | tf_op jit(solution)/shard_map/ppermute | solution.py:30
  62.9 8.9 %collective-permute-start.16 = (f32[3,4,8,128]{3,2,1,0:T(8,128)S(1)}, f32[3,4,8,128]{3,2,1,0:T(8,128)S(1)}, u32[]{:S(2)}, u32[]{:S(2)}) collective-permute-start(f32[3,4,8,128]{3,2,1,0:T(8,128)S(1)} %pad_maximum_fusion.2.refs_1_), channel_id=1, source_target_pairs={{0,4},{8,12},{16,20},{24,28},{32,36},{40,44},{48,52},{56,60},{4,0}... | collective-permute-start | bytes 147464 | tf_op jit(solution)/shard_map/ppermute | solution.py:30

commit v4 on v3

--- a/solution.py
+++ b/solution.py
@@ -38,12 +38,30 @@
     return (swap(own, "gy", pairs_first(count_y)), own, swap(own, "gy", pairs_second(count_y)))
 
 
+def sum_kernel(own, first, second, *outs):
+    for x, out in enumerate(outs):
+        for b in range(out.shape[0]):
+            out[b] = own[x, b] + first[x, b]
+        for c in range(3):
+            for b in range(out.shape[0]):
+                out[b, c : c + 1] += second[x, c, b : b + 1]
+
+
+def row_sums(own, first, second):
+    return pl.pallas_call(
+        sum_kernel,
+        out_shape=[jax.ShapeDtypeStruct(own.shape[1:], jnp.float32)] * 3,
+        in_specs=[vmem()] * 3,
+        out_specs=[vmem()] * 3,
+        compiler_params=pltpu.CompilerParams(vmem_limit_bytes=VMEM_LIMIT),
+        name="row_sums",
+    )(own, first, second)
+
+
 def sent_home(first, own, second):
     count_x, count_y = lax.axis_size("gx"), lax.axis_size("gy")
-    row = (
-        own
-        + swap(first, "gy", pairs_first(count_y))
-        + swap(second, "gy", pairs_second(count_y))
+    row = row_sums(
+        own, swap(first, "gy", pairs_first(count_y)), swap(second, "gy", pairs_second(count_y))
     )
     return [
         row[1], swap(row[0], "gx", pairs_first(count_x)), swap(row[2], "gx", pairs_second(count_x))
@@ -275,9 +293,12 @@
             for z, ref in enumerate(tower_outs):
                 ref[tower_block] += jnp.where(layer == z, on_tower, 0.0)
             for y, ref in enumerate(row_outs):
-                ref[cell_x, plate_block] += (
-                    on_plate if late else jnp.where(cell_y == y, on_plate, 0.0)
-                )
+                if late:
+                    place_in = pl.ds(plate_block, 1)
+                    for c in range(3):
+                        ref[cell_x, c, place_in, :] += on_plate[c : c + 1]
+                else:
+                    ref[cell_x, plate_block] += jnp.where(cell_y == y, on_plate, 0.0)
 
     buffers = (held[0:2], held[2:4])
 
@@ -301,7 +322,8 @@
     blocks = towers[0].shape[0] - 1
     slots = lists[0].shape[1]
     shape_one = jax.ShapeDtypeStruct((blocks, 4, lanes), jnp.float32)
-    shape_row = jax.ShapeDtypeStruct((3, blocks, 4, lanes), jnp.float32)
+    dims_row = (3, 3, blocks, lanes) if late else (3, blocks, 4, lanes)
+    shape_row = jax.ShapeDtypeStruct(dims_row, jnp.float32)
     flops = 20 * slots * lanes * lanes
     size = 2 if late else group
     return pl.pallas_call(

time: 73.3 us -> 73.7 us (level)
  starting transfers between devices: 35.9 us -> 39.9 us
  waiting for transfers between devices: 26.8 us -> 23 us
    ppermute x12, starting transfers between devices: 27.1 us -> 31.1 us  [swap(): return lax.ppermute(value, axis, [*pairs, *((j, i) for i, j in pairs)])]
    ppermute x12, waiting for transfers between devices: 25.1 us -> 21.4 us  [swap(): return lax.ppermute(value, axis, [*pairs, *((j, i) for i, j in pairs)])]
  transfers between devices with their start and end apart: 18 -> 18, of which waited for: 10 -> 9; matrix products, arithmetic and copies ran while one was open for 0% -> 0% of each run, Pallas kernels for 2% -> 4%
where the time goes in v4:
time: 73.7 us; the launch traced here: 73.4 us
  starting transfers between devices  39.9 us (54%)
  waiting for transfers between devices  23 us (31%)
  Pallas kernels  5.83 us (8%)
  other arithmetic  2.5 us (3%)
  between operations  1.46 us (2%)
  local copies, waits for them, and re-layouts  0.77 us (1%)
    ppermute x12, starting transfers between devices, swap(): return lax.ppermute(value, axis, [*pairs, *((j, i) for i, j in pairs)])  31.1 us
    ppermute x12, waiting for transfers between devices, swap(): return lax.ppermute(value, axis, [*pairs, *((j, i) for i, j in pairs)])  21.4 us
    ppermute x6, starting transfers between devices, from_layer(): return lax.ppermute(value, 'gz', [(i, i ^ step) for i in range(layers)])  8.79 us
    pallas_call x2, Pallas kernels, pair_forces(): pl.pallas_call(functools.partial(pair_kernel, *lengths, size, late), out_...  3.06 us
    ppermute x6, waiting for transfers between devices, from_layer(): return lax.ppermute(value, 'gz', [(i, i ^ step) for i in range(layers)])  1.67 us
  transfers between devices with their start and end apart: 18, of which 9 were waited for; matrix products, arithmetic and copies ran while one was open for 0% of the time, Pallas kernels for 4%

profile of v4, /device:TPU:6, one launch (start us, length us, event | category | flops | bytes accessed | tf_op | source)
XLA Modules:
  0.0 73.4 jit_solution(16902091227846612485)
XLA Ops:
  0.6 0.7 convert_bitcast_fusion
  1.3 0.7 broadcast_multiply_fusion
  2.0 1.0 %fusion = (f32[32,3,128]{2,1,0:T(4,128)S(1)}, f32[3,32,128]{2,0,1:T(4,128)S(1)}) fusion(f32[3,4096]{1,0:T(4,128)} %param.15, f32[3,4096]{1,0:T(4,128)} %param.16, f32[4096]{0:T(1024)S(1)} %broadcast_multiply_fusion, f32[3,4096]{1,0:T(4,128)} %param.14), kind=kLoop, calls=%fused_computation.6 | loop fusion | flops 49152 | bytes 262144 | tf_op jit(solution)/shard_map/transpose | solution.py:383
  3.1 4.7 %collective-permute-start.4 = (f32[33,4,128]{2,1,0:T(4,128)S(1)}, f32[33,4,128]{2,1,0:T(4,128)S(1)}, u32[]{:S(2)}, u32[]{:S(2)}) collective-permute-start(f32[33,4,128]{2,1,0:T(4,128)S(1)} %get-tuple-element.47.refs_0_.features), channel_id=1, source_target_pairs={{64,128},{192,0},{128,64},{0,192},{65,129},{193,1},{129,65},{1,193... | collective-permute-start | bytes 202760 | tf_op jit(solution)/shard_map/ppermute | solution.py:30
  7.8 0.0 collective-permute-start.3
  7.8 3.0 %collective-permute-done.4 = f32[33,4,128]{2,1,0:T(4,128)S(1)} collective-permute-done((f32[33,4,128]{2,1,0:T(4,128)S(1)}, f32[33,4,128]{2,1,0:T(4,128)S(1)}, u32[]{:S(2)}, u32[]{:S(2)}) %collective-permute-start.4) | collective-permute-done | bytes 67616 | tf_op jit(solution)/shard_map/ppermute | solution.py:30
  10.8 1.3 %collective-permute-done.3 = f32[33,4,128]{2,1,0:T(4,128)S(1)} collective-permute-done((f32[33,4,128]{2,1,0:T(4,128)S(1)}, f32[33,4,128]{2,1,0:T(4,128)S(1)}, u32[]{:S(2)}, u32[]{:S(2)}) %collective-permute-start.3) | collective-permute-done | bytes 67616 | tf_op jit(solution)/shard_map/ppermute | solution.py:30
  12.2 0.1 collective-permute-start.6
  12.3 7.8 %collective-permute-start.5 = (f32[3,33,4,128]{3,2,1,0:T(4,128)S(1)}, f32[3,33,4,128]{3,2,1,0:T(4,128)S(1)}, u32[]{:S(2)}, u32[]{:S(2)}) collective-permute-start(f32[3,33,4,128]{3,2,1,0:T(4,128)S(1)} %pad_maximum_fusion.refs_5_), channel_id=1, source_target_pairs={{4,8},{12,16},{20,24},{28,32},{36,40},{44,48},{52,56},{60,0},{8,4}... | collective-permute-start | bytes 608264 | tf_op jit(solution)/shard_map/ppermute | solution.py:30
  20.1 0.5 collective-permute-start.2
  20.6 2.4 %collective-permute-start.1 = (f32[33,4,128]{2,1,0:T(4,128)S(1)}, f32[33,4,128]{2,1,0:T(4,128)S(1)}, u32[]{:S(2)}, u32[]{:S(2)}) collective-permute-start(f32[33,4,128]{2,1,0:T(4,128)S(1)} %get-tuple-element.47.refs_0_.features), channel_id=1, source_target_pairs={{0,2},{1,3},{2,0},{3,1},{4,6},{5,7},{6,4},{7,5},{8,10},{9,11},{10,... | collective-permute-start | bytes 202760 | tf_op jit(solution)/shard_map/ppermute | solution.py:461
  23.0 1.2 %collective-permute-start = (f32[33,4,128]{2,1,0:T(4,128)S(1)}, f32[33,4,128]{2,1,0:T(4,128)S(1)}, u32[]{:S(2)}, u32[]{:S(2)}) collective-permute-start(f32[33,4,128]{2,1,0:T(4,128)S(1)} %get-tuple-element.47.refs_0_.features), channel_id=1, source_target_pairs={{0,1},{1,0},{2,3},{3,2},{4,5},{5,4},{6,7},{7,6},{8,9},{9,8},{10,11... | collective-permute-start | bytes 202760 | tf_op jit(solution)/shard_map/ppermute | solution.py:461
  24.8 0.0 copy-start.7
  24.8 0.0 copy-start.8
  24.9 0.6 copy-done.7
  25.5 0.0 copy-done.8
  25.5 0.1 concatenate.14.spot
  25.6 0.0 collective-permute-done.2.refs_3_
  25.6 0.7 %collective-permute-done.1.refs_2_ = f32[33,4,128]{2,1,0:T(4,128)S(1)} collective-permute-done((f32[33,4,128]{2,1,0:T(4,128)S(1)}, f32[33,4,128]{2,1,0:T(4,128)S(1)}, u32[]{:S(2)}, u32[]{:S(2)}) %collective-permute-start.1) | collective-permute-done | bytes 67616 | tf_op jit(solution)/shard_map/ppermute | solution.py:461
  26.3 0.9 %collective-permute-done.refs_1_ = f32[33,4,128]{2,1,0:T(4,128)S(1)} collective-permute-done((f32[33,4,128]{2,1,0:T(4,128)S(1)}, f32[33,4,128]{2,1,0:T(4,128)S(1)}, u32[]{:S(2)}, u32[]{:S(2)}) %collective-permute-start) | collective-permute-done | bytes 67616 | tf_op jit(solution)/shard_map/ppermute | solution.py:461
  27.3 0.0 collective-permute-done.6.refs_4_
  27.3 1.3 %pairs_early.1 = (f32[32,4,128]{2,1,0:T(4,128)S(1)}, f32[32,4,128]{2,1,0:T(4,128)S(1)}, f32[32,4,128]{2,1,0:T(4,128)S(1)}, f32[32,4,128]{2,1,0:T(4,128)S(1)}, f3...) custom-call(s32[1,64]{1,0:T(1,128)S(1)} %copy-done.2, s32[1,64]{1,0:T(1,128)S(1)} %copy-done.3, ...), custom_call_target="tpu_custom_call" | custom-call | flops 20971520 | bytes 1048576 | tf_op jit(solution)/shard_map/pairs_early/pallas_call | solution.py:329
  28.6 0.1 collective-permute-start.10
  28.7 0.0 collective-permute-done.5.refs_4_
  28.7 1.7 %pairs_late.1 = (f32[32,4,128]{2,1,0:T(4,128)S(1)}, f32[32,4,128]{2,1,0:T(4,128)S(1)}, f32[32,4,128]{2,1,0:T(4,128)S(1)}, f32[32,4,128]{2,1,0:T(4,128)S(1)}, f32[3,3,32,128]{3,2,1,0:T(8,128)S(1)}) custom-call(s32[1,64]{1,0:T(1,128)S(1)} %copy-done.2, s32[1,64]{1,0:T(1,128)S(1)} %copy-done.3, s32[1]{0:T(128)S(6)} %copy.19.count, s32[11]{0:T(128)S(1)} %concatenate.14.spot, ...), custom_call_target="tpu_custom_call" | custom-call | flops 20971520 | bytes 1048576 | tf_op jit(solution)/shard_map/pairs_late/pallas_call | solution.py:329
  30.5 5.3 %collective-permute-start.11 = (f32[3,3,32,128]{3,2,1,0:T(8,128)S(1)}, f32[3,3,32,128]{3,2,1,0:T(8,128)S(1)}, u32[]{:S(2)}, u32[]{:S(2)}) collective-permute-start(f32[3,3,32,128]{3,2,1,0:T(8,128)S(1)} %get-tuple-element.32), channel_id=1, source_target_pairs={{4,8},{12,16},{20,24},{28,32},{36,40},{44,48},{52,56},{60,0},{8,4}... | collective-permute-start | bytes 442376 | tf_op jit(solution)/shard_map/ppermute | solution.py:30
  35.8 0.0 collective-permute-start.7
  35.8 0.0 collective-permute-start.8
  35.8 4.7 %collective-permute-start.9 = (f32[32,4,128]{2,1,0:T(4,128)S(1)}, f32[32,4,128]{2,1,0:T(4,128)S(1)}, u32[]{:S(2)}, u32[]{:S(2)}) collective-permute-start(f32[32,4,128]{2,1,0:T(4,128)S(1)} %get-tuple-element.29), channel_id=1, source_target_pairs={{0,3},{1,2},{2,1},{3,0},{4,7},{5,6},{6,5},{7,4},{8,11},{9,10},{10,... | collective-permute-start | bytes 196616 | tf_op jit(solution)/shard_map/ppermute | solution.py:461
  40.5 0.6 collective-permute-done.11.second
  41.2 0.0 collective-permute-done.10.first
  41.2 0.2 row_sums.1
  41.4 2.1 %collective-permute-start.12 = (f32[32,4,128]{2,1,0:T(4,128)S(1)}, f32[32,4,128]{2,1,0:T(4,128)S(1)}, u32[]{:S(2)}, u32[]{:S(2)}) collective-permute-start(f32[32,4,128]{2,1,0:T(4,128)S(1)} %get-tuple-element.34), channel_id=1, source_target_pairs={{0,64},{128,192},{64,0},{192,128},{1,65},{129,193},{65,1},{193,129... | collective-permute-start | bytes 196616 | tf_op jit(solution)/shard_map/ppermute | solution.py:30
  43.5 8.1 %collective-permute-start.13 = (f32[32,4,128]{2,1,0:T(4,128)S(1)}, f32[32,4,128]{2,1,0:T(4,128)S(1)}, u32[]{:S(2)}, u32[]{:S(2)}) collective-permute-start(f32[32,4,128]{2,1,0:T(4,128)S(1)} %get-tuple-element.35), channel_id=1, source_target_pairs={{64,128},{192,0},{128,64},{0,192},{65,129},{193,1},{129,65},{1,193... | collective-permute-start | bytes 196616 | tf_op jit(solution)/shard_map/ppermute | solution.py:30
  51.5 0.0 collective-permute-done.7.refs_1_
  51.5 0.0 collective-permute-done.8.refs_2_
  51.5 0.0 collective-permute-done.9.refs_3_
  51.5 0.0 collective-permute-done.12.refs_5_
  51.6 3.3 %collective-permute-done.13.refs_6_ = f32[32,4,128]{2,1,0:T(4,128)S(1)} collective-permute-done((f32[32,4,128]{2,1,0:T(4,128)S(1)}, f32[32,4,128]{2,1,0:T(4,128)S(1)}, u32[]{:S(2)}, u32[]{:S(2)}) %collective-permute-start.13) | collective-permute-done | bytes 65568 | tf_op jit(solution)/shard_map/ppermute | solution.py:30
  54.9 1.3 %kick.1 = (f32[32,3,128]{2,1,0:T(4,128)}, f32[32,3,128]{2,1,0:T(4,128)}, f32[32,3,128]{2,1,0:T(4,128)}, f32[4,8,128]{2,1,0:T(8,128)S(1)}) custom-call(s32[11]{0:T(128)S(1)} %concatenate.14.spot, f32[33,4,128]{2,1,0:T(4,128)S(1)} %get-tuple-element.47.refs_0_.features, f32[32,3,128]{2,1,0:T(4,128)S(1)} %get-tuple-element.44.half_kick, ...), custom_call_target="tpu_custom_call" | custom-call | tf_op jit(solution)/shard_map/kick/pallas_call | solution.py:418
  56.2 2.7 %collective-permute-start.15 = (f32[4,8,128]{2,1,0:T(8,128)S(1)}, f32[4,8,128]{2,1,0:T(8,128)S(1)}, u32[]{:S(2)}, u32[]{:S(2)}) collective-permute-start(f32[4,8,128]{2,1,0:T(8,128)S(1)} %get-tuple-element.39), channel_id=1, source_target_pairs={{64,128},{192,0},{128,64},{0,192},{65,129},{193,1},{129,65},{1,193... | collective-permute-start | bytes 49160 | tf_op jit(solution)/shard_map/ppermute | solution.py:30
  58.9 0.1 collective-permute-start.14
  59.0 2.8 %collective-permute-done.15 = f32[4,8,128]{2,1,0:T(8,128)S(1)} collective-permute-done((f32[4,8,128]{2,1,0:T(8,128)S(1)}, f32[4,8,128]{2,1,0:T(8,128)S(1)}, u32[]{:S(2)}, u32[]{:S(2)}) %collective-permute-start.15) | collective-permute-done | bytes 16416 | tf_op jit(solution)/shard_map/ppermute | solution.py:30
  61.7 0.9 %collective-permute-done.14 = f32[4,8,128]{2,1,0:T(8,128)S(1)} collective-permute-done((f32[4,8,128]{2,1,0:T(8,128)S(1)}, f32[4,8,128]{2,1,0:T(8,128)S(1)}, u32[]{:S(2)}, u32[]{:S(2)}) %collective-permute-start.14) | collective-permute-done | bytes 16416 | tf_op jit(solution)/shard_map/ppermute | solution.py:30
  62.6 0.0 collective-permute-start.17
  62.7 0.1 collective-permute-start.16
  62.8 9.4 %collective-permute-done.17.refs_2_ = f32[3,4,8,128]{3,2,1,0:T(8,128)S(1)} collective-permute-done((f32[3,4,8,128]{3,2,1,0:T(8,128)S(1)}, f32[3,4,8,128]{3,2,1,0:T(8,128)S(1)}, u32[]{:S(2)}, u32[]{:S(2)}) %collective-permute-start.17) | collective-permute-done | bytes 49184 | tf_op jit(solution)/shard_map/ppermute | solution.py:30
  72.2 1.3 %arrivals.1 = f32[6,8,512]{2,1,0:T(8,128)} custom-call(s32[11]{0:T(128)S(1)} %concatenate.14.spot, f32[3,4,8,128]{3,2,1,0:T(8,128)S(1)} %collective-permute-done.16.refs_0_, f32[3,4,8,128]{3,2,1,0:T(8,128)S(1)} %pad_maximum_fusion.2.refs_1_, f32[3,4,8,128]{3,2,1,0:T(8,128)S(1)} %collective-permute-done.17.refs_2_), custom_call_target="tpu_custom_call" | custom-call | tf_op jit(solution)/shard_map/arrivals/pallas_call | solution.py:372
  (20 shorter events, 0.1 us)
Async XLA Ops:
  1.3 1.7 %copy-start.6 = (f32[4096]{0:T(1024)S(1)}, f32[4096]{0:T(1024)}, u32[]{:S(2)}) copy-start(f32[4096]{0:T(1024)} %param.18) | copy-start | bytes 49156
  2.0 25.2 %copy-start = (s32[1,64,16,128]{3,2,1,0:T(8,128)S(1)}, s32[1,64,16,128]{3,2,1,0:T(8,128)}, u32[]{:S(2)}) copy-start(s32[1,64,16,128]{3,2,1,0:T(8,128)} %param.25) | copy-start | bytes 1572868
  3.1 7.7 %collective-permute-start.4 = (f32[33,4,128]{2,1,0:T(4,128)S(1)}, f32[33,4,128]{2,1,0:T(4,128)S(1)}, u32[]{:S(2)}, u32[]{:S(2)}) collective-permute-start(f32[33,4,128]{2,1,0:T(4,128)S(1)} %get-tuple-element.47.refs_0_.features), channel_id=1, source_target_pairs={{64,128},{192,0},{128,64},{0,192},{65,129},{193,1},{129,65},{1,193... | collective-permute-start | bytes 202760 | tf_op jit(solution)/shard_map/ppermute | solution.py:30
  7.8 4.3 %collective-permute-start.3 = (f32[33,4,128]{2,1,0:T(4,128)S(1)}, f32[33,4,128]{2,1,0:T(4,128)S(1)}, u32[]{:S(2)}, u32[]{:S(2)}) collective-permute-start(f32[33,4,128]{2,1,0:T(4,128)S(1)} %get-tuple-element.47.refs_0_.features), channel_id=1, source_target_pairs={{0,64},{128,192},{64,0},{192,128},{1,65},{129,193},{65,1},{193,129... | collective-permute-start | bytes 202760 | tf_op jit(solution)/shard_map/ppermute | solution.py:30
  12.2 15.1 %collective-permute-start.6 = (f32[3,33,4,128]{3,2,1,0:T(4,128)S(1)}, f32[3,33,4,128]{3,2,1,0:T(4,128)S(1)}, u32[]{:S(2)}, u32[]{:S(2)}) collective-permute-start(f32[3,33,4,128]{3,2,1,0:T(4,128)S(1)} %pad_maximum_fusion.refs_5_), channel_id=1, source_target_pairs={{0,4},{8,12},{16,20},{24,28},{32,36},{40,44},{48,52},{56,60},{4,0}... | collective-permute-start | bytes 608264 | tf_op jit(solution)/shard_map/ppermute | solution.py:30
  12.3 16.4 %collective-permute-start.5 = (f32[3,33,4,128]{3,2,1,0:T(4,128)S(1)}, f32[3,33,4,128]{3,2,1,0:T(4,128)S(1)}, u32[]{:S(2)}, u32[]{:S(2)}) collective-permute-start(f32[3,33,4,128]{3,2,1,0:T(4,128)S(1)} %pad_maximum_fusion.refs_5_), channel_id=1, source_target_pairs={{4,8},{12,16},{20,24},{28,32},{36,40},{44,48},{52,56},{60,0},{8,4}... | collective-permute-start | bytes 608264 | tf_op jit(solution)/shard_map/ppermute | solution.py:30
  20.1 5.5 %collective-permute-start.2 = (f32[33,4,128]{2,1,0:T(4,128)S(1)}, f32[33,4,128]{2,1,0:T(4,128)S(1)}, u32[]{:S(2)}, u32[]{:S(2)}) collective-permute-start(f32[33,4,128]{2,1,0:T(4,128)S(1)} %get-tuple-element.47.refs_0_.features), channel_id=1, source_target_pairs={{0,3},{1,2},{2,1},{3,0},{4,7},{5,6},{6,5},{7,4},{8,11},{9,10},{10,... | collective-permute-start | bytes 202760 | tf_op jit(solution)/shard_map/ppermute | solution.py:461
  20.6 5.8 %collective-permute-start.1 = (f32[33,4,128]{2,1,0:T(4,128)S(1)}, f32[33,4,128]{2,1,0:T(4,128)S(1)}, u32[]{:S(2)}, u32[]{:S(2)}) collective-permute-start(f32[33,4,128]{2,1,0:T(4,128)S(1)} %get-tuple-element.47.refs_0_.features), channel_id=1, source_target_pairs={{0,2},{1,3},{2,0},{3,1},{4,6},{5,7},{6,4},{7,5},{8,10},{9,11},{10,... | collective-permute-start | bytes 202760 | tf_op jit(solution)/shard_map/ppermute | solution.py:461
  23.0 4.3 %collective-permute-start = (f32[33,4,128]{2,1,0:T(4,128)S(1)}, f32[33,4,128]{2,1,0:T(4,128)S(1)}, u32[]{:S(2)}, u32[]{:S(2)}) collective-permute-start(f32[33,4,128]{2,1,0:T(4,128)S(1)} %get-tuple-element.47.refs_0_.features), channel_id=1, source_target_pairs={{0,1},{1,0},{2,3},{3,2},{4,5},{5,4},{6,7},{7,6},{8,9},{9,8},{10,11... | collective-permute-start | bytes 202760 | tf_op jit(solution)/shard_map/ppermute | solution.py:461
  24.8 0.7 copy-start.7
  24.8 0.7 copy-start.8
  25.5 1.8 %copy-start.5 = (f32[4]{0:T(128)S(1)}, f32[4]{0:T(128)}, u32[]{:S(2)}) copy-start(f32[4]{0:T(128)} %epsilon_table.3) | copy-start | bytes 52
  25.6 1.7 %copy-start.2 = (s32[1,64]{1,0:T(1,128)S(1)}, s32[1,64]{1,0:T(1,128)}, u32[]{:S(2)}) copy-start(s32[1,64]{1,0:T(1,128)} %tower_list.3) | copy-start | bytes 772
  25.6 1.7 %copy-start.3 = (s32[1,64]{1,0:T(1,128)S(1)}, s32[1,64]{1,0:T(1,128)}, u32[]{:S(2)}) copy-start(s32[1,64]{1,0:T(1,128)} %plate_list.3) | copy-start | bytes 772
  25.6 1.7 %copy-start.4 = (f32[4]{0:T(128)S(1)}, f32[4]{0:T(128)}, u32[]{:S(2)}) copy-start(f32[4]{0:T(128)} %sigma_table.3) | copy-start | bytes 52
  28.6 12.5 %collective-permute-start.10 = (f32[3,32,4,128]{3,2,1,0:T(4,128)S(1)}, f32[3,32,4,128]{3,2,1,0:T(4,128)S(1)}, u32[]{:S(2)}, u32[]{:S(2)}) collective-permute-start(f32[3,32,4,128]{3,2,1,0:T(4,128)S(1)} %get-tuple-element.31), channel_id=1, source_target_pairs={{0,4},{8,12},{16,20},{24,28},{32,36},{40,44},{48,52},{56,60},{4,0}... | collective-permute-start | bytes 589832 | tf_op jit(solution)/shard_map/ppermute | solution.py:30
  30.5 10.7 %collective-permute-start.11 = (f32[3,3,32,128]{3,2,1,0:T(8,128)S(1)}, f32[3,3,32,128]{3,2,1,0:T(8,128)S(1)}, u32[]{:S(2)}, u32[]{:S(2)}) collective-permute-start(f32[3,3,32,128]{3,2,1,0:T(8,128)S(1)} %get-tuple-element.32), channel_id=1, source_target_pairs={{4,8},{12,16},{20,24},{28,32},{36,40},{44,48},{52,56},{60,0},{8,4}... | collective-permute-start | bytes 442376 | tf_op jit(solution)/shard_map/ppermute | solution.py:30
  35.8 15.7 %collective-permute-start.7 = (f32[32,4,128]{2,1,0:T(4,128)S(1)}, f32[32,4,128]{2,1,0:T(4,128)S(1)}, u32[]{:S(2)}, u32[]{:S(2)}) collective-permute-start(f32[32,4,128]{2,1,0:T(4,128)S(1)} %get-tuple-element.27), channel_id=1, source_target_pairs={{0,1},{1,0},{2,3},{3,2},{4,5},{5,4},{6,7},{7,6},{8,9},{9,8},{10,11... | collective-permute-start | bytes 196616 | tf_op jit(solution)/shard_map/ppermute | solution.py:461
  35.8 15.7 %collective-permute-start.8 = (f32[32,4,128]{2,1,0:T(4,128)S(1)}, f32[32,4,128]{2,1,0:T(4,128)S(1)}, u32[]{:S(2)}, u32[]{:S(2)}) collective-permute-start(f32[32,4,128]{2,1,0:T(4,128)S(1)} %get-tuple-element.28), channel_id=1, source_target_pairs={{0,2},{1,3},{2,0},{3,1},{4,6},{5,7},{6,4},{7,5},{8,10},{9,11},{10,... | collective-permute-start | bytes 196616 | tf_op jit(solution)/shard_map/ppermute | solution.py:461
  35.8 15.7 %collective-permute-start.9 = (f32[32,4,128]{2,1,0:T(4,128)S(1)}, f32[32,4,128]{2,1,0:T(4,128)S(1)}, u32[]{:S(2)}, u32[]{:S(2)}) collective-permute-start(f32[32,4,128]{2,1,0:T(4,128)S(1)} %get-tuple-element.29), channel_id=1, source_target_pairs={{0,3},{1,2},{2,1},{3,0},{4,7},{5,6},{6,5},{7,4},{8,11},{9,10},{10,... | collective-permute-start | bytes 196616 | tf_op jit(solution)/shard_map/ppermute | solution.py:461
  41.2 13.7 %copy-start.1 = (f32[4096]{0:T(1024)S(1)}, f32[4096]{0:T(1024)}, u32[]{:S(2)}) copy-start(f32[4096]{0:T(1024)} %param.17) | copy-start | bytes 49156
  41.4 10.2 %collective-permute-start.12 = (f32[32,4,128]{2,1,0:T(4,128)S(1)}, f32[32,4,128]{2,1,0:T(4,128)S(1)}, u32[]{:S(2)}, u32[]{:S(2)}) collective-permute-start(f32[32,4,128]{2,1,0:T(4,128)S(1)} %get-tuple-element.34), channel_id=1, source_target_pairs={{0,64},{128,192},{64,0},{192,128},{1,65},{129,193},{65,1},{193,129... | collective-permute-start | bytes 196616 | tf_op jit(solution)/shard_map/ppermute | solution.py:30
  43.5 11.4 %collective-permute-start.13 = (f32[32,4,128]{2,1,0:T(4,128)S(1)}, f32[32,4,128]{2,1,0:T(4,128)S(1)}, u32[]{:S(2)}, u32[]{:S(2)}) collective-permute-start(f32[32,4,128]{2,1,0:T(4,128)S(1)} %get-tuple-element.35), channel_id=1, source_target_pairs={{64,128},{192,0},{128,64},{0,192},{65,129},{193,1},{129,65},{1,193... | collective-permute-start | bytes 196616 | tf_op jit(solution)/shard_map/ppermute | solution.py:30
  56.2 5.5 %collective-permute-start.15 = (f32[4,8,128]{2,1,0:T(8,128)S(1)}, f32[4,8,128]{2,1,0:T(8,128)S(1)}, u32[]{:S(2)}, u32[]{:S(2)}) collective-permute-start(f32[4,8,128]{2,1,0:T(8,128)S(1)} %get-tuple-element.39), channel_id=1, source_target_pairs={{64,128},{192,0},{128,64},{0,192},{65,129},{193,1},{129,65},{1,193... | collective-permute-start | bytes 49160 | tf_op jit(solution)/shard_map/ppermute | solution.py:30
  58.9 3.7 %collective-permute-start.14 = (f32[4,8,128]{2,1,0:T(8,128)S(1)}, f32[4,8,128]{2,1,0:T(8,128)S(1)}, u32[]{:S(2)}, u32[]{:S(2)}) collective-permute-start(f32[4,8,128]{2,1,0:T(8,128)S(1)} %get-tuple-element.39), channel_id=1, source_target_pairs={{0,64},{128,192},{64,0},{192,128},{1,65},{129,193},{65,1},{193,129... | collective-permute-start | bytes 49160 | tf_op jit(solution)/shard_map/ppermute | solution.py:30
  62.6 9.5 %collective-permute-start.17 = (f32[3,4,8,128]{3,2,1,0:T(8,128)S(1)}, f32[3,4,8,128]{3,2,1,0:T(8,128)S(1)}, u32[]{:S(2)}, u32[]{:S(2)}) collective-permute-start(f32[3,4,8,128]{3,2,1,0:T(8,128)S(1)} %pad_maximum_fusion.2.refs_1_), channel_id=1, source_target_pairs={{4,8},{12,16},{20,24},{28,32},{36,40},{44,48},{52,56},{60,0},{8,4}... | collective-permute-start | bytes 147464 | tf_op jit(solution)/shard_map/ppermute | solution.py:30
  62.7 9.5 %collective-permute-start.16 = (f32[3,4,8,128]{3,2,1,0:T(8,128)S(1)}, f32[3,4,8,128]{3,2,1,0:T(8,128)S(1)}, u32[]{:S(2)}, u32[]{:S(2)}) collective-permute-start(f32[3,4,8,128]{3,2,1,0:T(8,128)S(1)} %pad_maximum_fusion.2.refs_1_), channel_id=1, source_target_pairs={{0,4},{8,12},{16,20},{24,28},{32,36},{40,44},{48,52},{56,60},{4,0}... | collective-permute-start | bytes 147464 | tf_op jit(solution)/shard_map/ppermute | solution.py:30

commit v5 on v4

--- a/solution.py
+++ b/solution.py
@@ -445,13 +445,13 @@
     layers = lax.axis_size("gz")
     length_x = float(lax.axis_size("gx"))
     length_y = float(lax.axis_size("gy"))
-    half_kick = velocities + 0.5 * time_step * forces_old * inv_mass[None, :]
-    moved = positions + time_step * half_kick
+    inverse = inv_mass.reshape(-1, 1, lanes)
+    half_kick = by_block(velocities) + 0.5 * time_step * by_block(forces_old) * inverse
+    moved = by_block(positions) + time_step * half_kick
     kinds = block_species.astype(jnp.float32)
     kind_tile = jnp.pad(kinds[None, :], ((0, 3), (0, lanes - kinds.shape[0])))
-    features = jnp.concatenate(
-        [by_block(jnp.concatenate([moved, charges[None, :]])), kind_tile[None]]
-    )
+    tiles = jnp.concatenate([moved, charges.reshape(-1, 1, lanes)], axis=1)
+    features = jnp.concatenate([tiles, kind_tile[None]])
     me_x, me_y, me_z = (lax.axis_index(axis) for axis in ("gx", "gy", "gz"))
     spot = jnp.stack([me_x % 2, me_y % 2, me_z]).astype(jnp.int32)
     spot = jnp.concatenate([spot, mig_block[0], mig_dest[0]])
@@ -480,7 +480,7 @@
     parts = [sums[0]] + [from_layer(sums[step], step) for step in range(1, layers)]
     parts += sent_home(on_first, on_own, on_second)
     positions_new, velocities_new, forces_new, state = kick(
-        spot, mig_block.shape[1], features, by_block(half_kick), inv_mass, parts
+        spot, mig_block.shape[1], features, half_kick, inv_mass, parts
     )
     arrivals = arrivals_of(spot, halo(state))[:, None]
     return (by_atom(positions_new), by_atom(velocities_new), by_atom(forces_new), arrivals)

time: 73.7 us -> 73.6 us (level)
    transpose x2 -> x0, other arithmetic: 1.04 us -> none  [by_block(): return rows.reshape(rows.shape[0], -1, lanes).transpose(1, 0, 2)]
    add x0 -> x1, other arithmetic: none -> 1 us  [local(): moved = by_block(positions) + time_step * half_kick]
where the time goes in v5:
time: 73.6 us; the launch traced here: 73.4 us
  starting transfers between devices  39.9 us (54%)
  waiting for transfers between devices  23 us (31%)
  Pallas kernels  5.82 us (8%)
  other arithmetic  2.51 us (3%)
  between operations  1.46 us (2%)
  local copies, waits for them, and re-layouts  0.77 us (1%)
    ppermute x12, starting transfers between devices, swap(): return lax.ppermute(value, axis, [*pairs, *((j, i) for i, j in pairs)])  31.1 us
    ppermute x12, waiting for transfers between devices, swap(): return lax.ppermute(value, axis, [*pairs, *((j, i) for i, j in pairs)])  21.3 us
    ppermute x6, starting transfers between devices, from_layer(): return lax.ppermute(value, 'gz', [(i, i ^ step) for i in range(layers)])  8.79 us
    pallas_call x2, Pallas kernels, pair_forces(): pl.pallas_call(functools.partial(pair_kernel, *lengths, size, late), out_...  3.05 us
    ppermute x6, waiting for transfers between devices, from_layer(): return lax.ppermute(value, 'gz', [(i, i ^ step) for i in range(layers)])  1.67 us
  transfers between devices with their start and end apart: 18, of which 9 were waited for; matrix products, arithmetic and copies ran while one was open for 0% of the time, Pallas kernels for 4%

profile of v5, /device:TPU:6, one launch (start us, length us, event | category | flops | bytes accessed | tf_op | source)
XLA Modules:
  0.0 73.4 jit_solution(10646737742557530022)
XLA Ops:
  0.6 0.7 convert_bitcast_fusion
  1.3 0.7 broadcast_multiply_fusion
  2.0 1.0 %bitcast_add_fusion = (f32[32,3,128]{2,1,0:T(4,128)S(1)}, f32[32,3,128]{2,1,0:T(4,128)S(1)}) fusion(f32[3,4096]{1,0:T(4,128)} %param.14, f32[32,128]{1,0:T(8,128)S(1)} %broadcast_multiply_fusion, f32[3,4096]{1,0:T(4,128)} %param.16, f32[3,4096]{1,0:T(4,128)} %param.15), kind=kLoop, calls=%fused_computation.2 | loop fusion | flops 49152 | bytes 262144 | tf_op jit(solution)/shard_map/add | solution.py:450
  3.1 4.7 %collective-permute-start.4 = (f32[33,4,128]{2,1,0:T(4,128)S(1)}, f32[33,4,128]{2,1,0:T(4,128)S(1)}, u32[]{:S(2)}, u32[]{:S(2)}) collective-permute-start(f32[33,4,128]{2,1,0:T(4,128)S(1)} %pad_maximum_fusion.1.refs_0_.features), channel_id=1, source_target_pairs={{64,128},{192,0},{128,64},{0,192},{65,129},{193,1},{129,65},{1,193... | collective-permute-start | bytes 202760 | tf_op jit(solution)/shard_map/ppermute | solution.py:30
  7.8 0.0 collective-permute-start.3
  7.8 2.9 %collective-permute-done.4 = f32[33,4,128]{2,1,0:T(4,128)S(1)} collective-permute-done((f32[33,4,128]{2,1,0:T(4,128)S(1)}, f32[33,4,128]{2,1,0:T(4,128)S(1)}, u32[]{:S(2)}, u32[]{:S(2)}) %collective-permute-start.4) | collective-permute-done | bytes 67616 | tf_op jit(solution)/shard_map/ppermute | solution.py:30
  10.8 1.3 %collective-permute-done.3 = f32[33,4,128]{2,1,0:T(4,128)S(1)} collective-permute-done((f32[33,4,128]{2,1,0:T(4,128)S(1)}, f32[33,4,128]{2,1,0:T(4,128)S(1)}, u32[]{:S(2)}, u32[]{:S(2)}) %collective-permute-start.3) | collective-permute-done | bytes 67616 | tf_op jit(solution)/shard_map/ppermute | solution.py:30
  12.1 0.1 collective-permute-start.6
  12.2 7.8 %collective-permute-start.5 = (f32[3,33,4,128]{3,2,1,0:T(4,128)S(1)}, f32[3,33,4,128]{3,2,1,0:T(4,128)S(1)}, u32[]{:S(2)}, u32[]{:S(2)}) collective-permute-start(f32[3,33,4,128]{3,2,1,0:T(4,128)S(1)} %pad_maximum_fusion.refs_5_), channel_id=1, source_target_pairs={{4,8},{12,16},{20,24},{28,32},{36,40},{44,48},{52,56},{60,0},{8,4}... | collective-permute-start | bytes 608264 | tf_op jit(solution)/shard_map/ppermute | solution.py:30
  20.0 0.5 collective-permute-start.2
  20.5 2.4 %collective-permute-start.1 = (f32[33,4,128]{2,1,0:T(4,128)S(1)}, f32[33,4,128]{2,1,0:T(4,128)S(1)}, u32[]{:S(2)}, u32[]{:S(2)}) collective-permute-start(f32[33,4,128]{2,1,0:T(4,128)S(1)} %pad_maximum_fusion.1.refs_0_.features), channel_id=1, source_target_pairs={{0,2},{1,3},{2,0},{3,1},{4,6},{5,7},{6,4},{7,5},{8,10},{9,11},{10,... | collective-permute-start | bytes 202760 | tf_op jit(solution)/shard_map/ppermute | solution.py:461
  22.9 1.2 %collective-permute-start = (f32[33,4,128]{2,1,0:T(4,128)S(1)}, f32[33,4,128]{2,1,0:T(4,128)S(1)}, u32[]{:S(2)}, u32[]{:S(2)}) collective-permute-start(f32[33,4,128]{2,1,0:T(4,128)S(1)} %pad_maximum_fusion.1.refs_0_.features), channel_id=1, source_target_pairs={{0,1},{1,0},{2,3},{3,2},{4,5},{5,4},{6,7},{7,6},{8,9},{9,8},{10,11... | collective-permute-start | bytes 202760 | tf_op jit(solution)/shard_map/ppermute | solution.py:461
  24.8 0.0 copy-start.7
  24.8 0.0 copy-start.8
  24.8 0.6 copy-done.7
  25.5 0.0 copy-done.8
  25.5 0.1 concatenate.9.spot
  25.6 0.0 collective-permute-done.2.refs_3_
  25.6 0.7 %collective-permute-done.1.refs_2_ = f32[33,4,128]{2,1,0:T(4,128)S(1)} collective-permute-done((f32[33,4,128]{2,1,0:T(4,128)S(1)}, f32[33,4,128]{2,1,0:T(4,128)S(1)}, u32[]{:S(2)}, u32[]{:S(2)}) %collective-permute-start.1) | collective-permute-done | bytes 67616 | tf_op jit(solution)/shard_map/ppermute | solution.py:461
  26.3 0.9 %collective-permute-done.refs_1_ = f32[33,4,128]{2,1,0:T(4,128)S(1)} collective-permute-done((f32[33,4,128]{2,1,0:T(4,128)S(1)}, f32[33,4,128]{2,1,0:T(4,128)S(1)}, u32[]{:S(2)}, u32[]{:S(2)}) %collective-permute-start) | collective-permute-done | bytes 67616 | tf_op jit(solution)/shard_map/ppermute | solution.py:461
  27.2 0.0 collective-permute-done.6.refs_4_
  27.3 1.3 %pairs_early.1 = (f32[32,4,128]{2,1,0:T(4,128)S(1)}, f32[32,4,128]{2,1,0:T(4,128)S(1)}, f32[32,4,128]{2,1,0:T(4,128)S(1)}, f32[32,4,128]{2,1,0:T(4,128)S(1)}, f3...) custom-call(s32[1,64]{1,0:T(1,128)S(1)} %copy-done.2, s32[1,64]{1,0:T(1,128)S(1)} %copy-done.3, ...), custom_call_target="tpu_custom_call" | custom-call | flops 20971520 | bytes 1048576 | tf_op jit(solution)/shard_map/pairs_early/pallas_call | solution.py:329
  28.6 0.1 collective-permute-start.10
  28.7 0.0 collective-permute-done.5.refs_4_
  28.7 1.7 %pairs_late.1 = (f32[32,4,128]{2,1,0:T(4,128)S(1)}, f32[32,4,128]{2,1,0:T(4,128)S(1)}, f32[32,4,128]{2,1,0:T(4,128)S(1)}, f32[32,4,128]{2,1,0:T(4,128)S(1)}, f32[3,3,32,128]{3,2,1,0:T(8,128)S(1)}) custom-call(s32[1,64]{1,0:T(1,128)S(1)} %copy-done.2, s32[1,64]{1,0:T(1,128)S(1)} %copy-done.3, s32[1]{0:T(128)S(6)} %copy.19.count, s32[11]{0:T(128)S(1)} %concatenate.9.spot, ...), custom_call_target="tpu_custom_call" | custom-call | flops 20971520 | bytes 1048576 | tf_op jit(solution)/shard_map/pairs_late/pallas_call | solution.py:329
  30.4 5.3 %collective-permute-start.11 = (f32[3,3,32,128]{3,2,1,0:T(8,128)S(1)}, f32[3,3,32,128]{3,2,1,0:T(8,128)S(1)}, u32[]{:S(2)}, u32[]{:S(2)}) collective-permute-start(f32[3,3,32,128]{3,2,1,0:T(8,128)S(1)} %get-tuple-element.32), channel_id=1, source_target_pairs={{4,8},{12,16},{20,24},{28,32},{36,40},{44,48},{52,56},{60,0},{8,4}... | collective-permute-start | bytes 442376 | tf_op jit(solution)/shard_map/ppermute | solution.py:30
  35.8 0.0 collective-permute-start.7
  35.8 0.0 collective-permute-start.8
  35.8 4.7 %collective-permute-start.9 = (f32[32,4,128]{2,1,0:T(4,128)S(1)}, f32[32,4,128]{2,1,0:T(4,128)S(1)}, u32[]{:S(2)}, u32[]{:S(2)}) collective-permute-start(f32[32,4,128]{2,1,0:T(4,128)S(1)} %get-tuple-element.29), channel_id=1, source_target_pairs={{0,3},{1,2},{2,1},{3,0},{4,7},{5,6},{6,5},{7,4},{8,11},{9,10},{10,... | collective-permute-start | bytes 196616 | tf_op jit(solution)/shard_map/ppermute | solution.py:461
  40.5 0.6 collective-permute-done.11.second
  41.1 0.0 collective-permute-done.10.first
  41.1 0.2 row_sums.1
  41.3 2.1 %collective-permute-start.12 = (f32[32,4,128]{2,1,0:T(4,128)S(1)}, f32[32,4,128]{2,1,0:T(4,128)S(1)}, u32[]{:S(2)}, u32[]{:S(2)}) collective-permute-start(f32[32,4,128]{2,1,0:T(4,128)S(1)} %get-tuple-element.34), channel_id=1, source_target_pairs={{0,64},{128,192},{64,0},{192,128},{1,65},{129,193},{65,1},{193,129... | collective-permute-start | bytes 196616 | tf_op jit(solution)/shard_map/ppermute | solution.py:30
  43.4 8.1 %collective-permute-start.13 = (f32[32,4,128]{2,1,0:T(4,128)S(1)}, f32[32,4,128]{2,1,0:T(4,128)S(1)}, u32[]{:S(2)}, u32[]{:S(2)}) collective-permute-start(f32[32,4,128]{2,1,0:T(4,128)S(1)} %get-tuple-element.35), channel_id=1, source_target_pairs={{64,128},{192,0},{128,64},{0,192},{65,129},{193,1},{129,65},{1,193... | collective-permute-start | bytes 196616 | tf_op jit(solution)/shard_map/ppermute | solution.py:30
  51.5 0.0 collective-permute-done.7.refs_1_
  51.5 0.0 collective-permute-done.8.refs_2_
  51.5 0.0 collective-permute-done.9.refs_3_
  51.5 0.0 collective-permute-done.12.refs_5_
  51.5 3.3 %collective-permute-done.13.refs_6_ = f32[32,4,128]{2,1,0:T(4,128)S(1)} collective-permute-done((f32[32,4,128]{2,1,0:T(4,128)S(1)}, f32[32,4,128]{2,1,0:T(4,128)S(1)}, u32[]{:S(2)}, u32[]{:S(2)}) %collective-permute-start.13) | collective-permute-done | bytes 65568 | tf_op jit(solution)/shard_map/ppermute | solution.py:30
  54.9 1.3 %kick.1 = (f32[32,3,128]{2,1,0:T(4,128)}, f32[32,3,128]{2,1,0:T(4,128)}, f32[32,3,128]{2,1,0:T(4,128)}, f32[4,8,128]{2,1,0:T(8,128)S(1)}) custom-call(s32[11]{0:T(128)S(1)} %concatenate.9.spot, f32[33,4,128]{2,1,0:T(4,128)S(1)} %pad_maximum_fusion.1.refs_0_.features, f32[32,3,128]{2,1,0:T(4,128)S(1)} %get-tuple-element.45.half_kick, f32[32,128]{1,0:T(8,128)S(1)} %bitcast.51, ...), custom_call_target="tpu_custom_call" | custom-call | tf_op jit(solution)/shard_map/kick/pallas_call | solution.py:418
  56.2 2.7 %collective-permute-start.15 = (f32[4,8,128]{2,1,0:T(8,128)S(1)}, f32[4,8,128]{2,1,0:T(8,128)S(1)}, u32[]{:S(2)}, u32[]{:S(2)}) collective-permute-start(f32[4,8,128]{2,1,0:T(8,128)S(1)} %get-tuple-element.39), channel_id=1, source_target_pairs={{64,128},{192,0},{128,64},{0,192},{65,129},{193,1},{129,65},{1,193... | collective-permute-start | bytes 49160 | tf_op jit(solution)/shard_map/ppermute | solution.py:30
  58.9 0.1 collective-permute-start.14
  58.9 2.8 %collective-permute-done.15 = f32[4,8,128]{2,1,0:T(8,128)S(1)} collective-permute-done((f32[4,8,128]{2,1,0:T(8,128)S(1)}, f32[4,8,128]{2,1,0:T(8,128)S(1)}, u32[]{:S(2)}, u32[]{:S(2)}) %collective-permute-start.15) | collective-permute-done | bytes 16416 | tf_op jit(solution)/shard_map/ppermute | solution.py:30
  61.7 0.9 %collective-permute-done.14 = f32[4,8,128]{2,1,0:T(8,128)S(1)} collective-permute-done((f32[4,8,128]{2,1,0:T(8,128)S(1)}, f32[4,8,128]{2,1,0:T(8,128)S(1)}, u32[]{:S(2)}, u32[]{:S(2)}) %collective-permute-start.14) | collective-permute-done | bytes 16416 | tf_op jit(solution)/shard_map/ppermute | solution.py:30
  62.6 0.0 collective-permute-start.17
  62.6 0.1 collective-permute-start.16
  62.7 9.4 %collective-permute-done.17.refs_2_ = f32[3,4,8,128]{3,2,1,0:T(8,128)S(1)} collective-permute-done((f32[3,4,8,128]{3,2,1,0:T(8,128)S(1)}, f32[3,4,8,128]{3,2,1,0:T(8,128)S(1)}, u32[]{:S(2)}, u32[]{:S(2)}) %collective-permute-start.17) | collective-permute-done | bytes 49184 | tf_op jit(solution)/shard_map/ppermute | solution.py:30
  72.2 1.3 %arrivals.1 = f32[6,8,512]{2,1,0:T(8,128)} custom-call(s32[11]{0:T(128)S(1)} %concatenate.9.spot, f32[3,4,8,128]{3,2,1,0:T(8,128)S(1)} %collective-permute-done.16.refs_0_, f32[3,4,8,128]{3,2,1,0:T(8,128)S(1)} %pad_maximum_fusion.2.refs_1_, f32[3,4,8,128]{3,2,1,0:T(8,128)S(1)} %collective-permute-done.17.refs_2_), custom_call_target="tpu_custom_call" | custom-call | tf_op jit(solution)/shard_map/arrivals/pallas_call | solution.py:372
  (20 shorter events, 0.2 us)
Async XLA Ops:
  1.3 1.7 %copy-start.6 = (f32[4096]{0:T(1024)S(1)}, f32[4096]{0:T(1024)}, u32[]{:S(2)}) copy-start(f32[4096]{0:T(1024)} %param.18) | copy-start | bytes 49156
  2.0 25.2 %copy-start = (s32[1,64,16,128]{3,2,1,0:T(8,128)S(1)}, s32[1,64,16,128]{3,2,1,0:T(8,128)}, u32[]{:S(2)}) copy-start(s32[1,64,16,128]{3,2,1,0:T(8,128)} %param.25) | copy-start | bytes 1572868
  3.1 7.7 %collective-permute-start.4 = (f32[33,4,128]{2,1,0:T(4,128)S(1)}, f32[33,4,128]{2,1,0:T(4,128)S(1)}, u32[]{:S(2)}, u32[]{:S(2)}) collective-permute-start(f32[33,4,128]{2,1,0:T(4,128)S(1)} %pad_maximum_fusion.1.refs_0_.features), channel_id=1, source_target_pairs={{64,128},{192,0},{128,64},{0,192},{65,129},{193,1},{129,65},{1,193... | collective-permute-start | bytes 202760 | tf_op jit(solution)/shard_map/ppermute | solution.py:30
  7.8 4.3 %collective-permute-start.3 = (f32[33,4,128]{2,1,0:T(4,128)S(1)}, f32[33,4,128]{2,1,0:T(4,128)S(1)}, u32[]{:S(2)}, u32[]{:S(2)}) collective-permute-start(f32[33,4,128]{2,1,0:T(4,128)S(1)} %pad_maximum_fusion.1.refs_0_.features), channel_id=1, source_target_pairs={{0,64},{128,192},{64,0},{192,128},{1,65},{129,193},{65,1},{193,129... | collective-permute-start | bytes 202760 | tf_op jit(solution)/shard_map/ppermute | solution.py:30
  12.1 15.1 %collective-permute-start.6 = (f32[3,33,4,128]{3,2,1,0:T(4,128)S(1)}, f32[3,33,4,128]{3,2,1,0:T(4,128)S(1)}, u32[]{:S(2)}, u32[]{:S(2)}) collective-permute-start(f32[3,33,4,128]{3,2,1,0:T(4,128)S(1)} %pad_maximum_fusion.refs_5_), channel_id=1, source_target_pairs={{0,4},{8,12},{16,20},{24,28},{32,36},{40,44},{48,52},{56,60},{4,0}... | collective-permute-start | bytes 608264 | tf_op jit(solution)/shard_map/ppermute | solution.py:30
  12.2 16.4 %collective-permute-start.5 = (f32[3,33,4,128]{3,2,1,0:T(4,128)S(1)}, f32[3,33,4,128]{3,2,1,0:T(4,128)S(1)}, u32[]{:S(2)}, u32[]{:S(2)}) collective-permute-start(f32[3,33,4,128]{3,2,1,0:T(4,128)S(1)} %pad_maximum_fusion.refs_5_), channel_id=1, source_target_pairs={{4,8},{12,16},{20,24},{28,32},{36,40},{44,48},{52,56},{60,0},{8,4}... | collective-permute-start | bytes 608264 | tf_op jit(solution)/shard_map/ppermute | solution.py:30
  20.0 5.5 %collective-permute-start.2 = (f32[33,4,128]{2,1,0:T(4,128)S(1)}, f32[33,4,128]{2,1,0:T(4,128)S(1)}, u32[]{:S(2)}, u32[]{:S(2)}) collective-permute-start(f32[33,4,128]{2,1,0:T(4,128)S(1)} %pad_maximum_fusion.1.refs_0_.features), channel_id=1, source_target_pairs={{0,3},{1,2},{2,1},{3,0},{4,7},{5,6},{6,5},{7,4},{8,11},{9,10},{10,... | collective-permute-start | bytes 202760 | tf_op jit(solution)/shard_map/ppermute | solution.py:461
  20.5 5.8 %collective-permute-start.1 = (f32[33,4,128]{2,1,0:T(4,128)S(1)}, f32[33,4,128]{2,1,0:T(4,128)S(1)}, u32[]{:S(2)}, u32[]{:S(2)}) collective-permute-start(f32[33,4,128]{2,1,0:T(4,128)S(1)} %pad_maximum_fusion.1.refs_0_.features), channel_id=1, source_target_pairs={{0,2},{1,3},{2,0},{3,1},{4,6},{5,7},{6,4},{7,5},{8,10},{9,11},{10,... | collective-permute-start | bytes 202760 | tf_op jit(solution)/shard_map/ppermute | solution.py:461
  22.9 4.3 %collective-permute-start = (f32[33,4,128]{2,1,0:T(4,128)S(1)}, f32[33,4,128]{2,1,0:T(4,128)S(1)}, u32[]{:S(2)}, u32[]{:S(2)}) collective-permute-start(f32[33,4,128]{2,1,0:T(4,128)S(1)} %pad_maximum_fusion.1.refs_0_.features), channel_id=1, source_target_pairs={{0,1},{1,0},{2,3},{3,2},{4,5},{5,4},{6,7},{7,6},{8,9},{9,8},{10,11... | collective-permute-start | bytes 202760 | tf_op jit(solution)/shard_map/ppermute | solution.py:461
  24.8 0.7 copy-start.7
  24.8 0.7 copy-start.8
  25.5 1.8 %copy-start.5 = (f32[4]{0:T(128)S(1)}, f32[4]{0:T(128)}, u32[]{:S(2)}) copy-start(f32[4]{0:T(128)} %epsilon_table.3) | copy-start | bytes 52
  25.6 1.7 %copy-start.2 = (s32[1,64]{1,0:T(1,128)S(1)}, s32[1,64]{1,0:T(1,128)}, u32[]{:S(2)}) copy-start(s32[1,64]{1,0:T(1,128)} %tower_list.3) | copy-start | bytes 772
  25.6 1.7 %copy-start.3 = (s32[1,64]{1,0:T(1,128)S(1)}, s32[1,64]{1,0:T(1,128)}, u32[]{:S(2)}) copy-start(s32[1,64]{1,0:T(1,128)} %plate_list.3) | copy-start | bytes 772
  25.6 1.7 %copy-start.4 = (f32[4]{0:T(128)S(1)}, f32[4]{0:T(128)}, u32[]{:S(2)}) copy-start(f32[4]{0:T(128)} %sigma_table.3) | copy-start | bytes 52
  28.6 12.5 %collective-permute-start.10 = (f32[3,32,4,128]{3,2,1,0:T(4,128)S(1)}, f32[3,32,4,128]{3,2,1,0:T(4,128)S(1)}, u32[]{:S(2)}, u32[]{:S(2)}) collective-permute-start(f32[3,32,4,128]{3,2,1,0:T(4,128)S(1)} %get-tuple-element.31), channel_id=1, source_target_pairs={{0,4},{8,12},{16,20},{24,28},{32,36},{40,44},{48,52},{56,60},{4,0}... | collective-permute-start | bytes 589832 | tf_op jit(solution)/shard_map/ppermute | solution.py:30
  30.4 10.7 %collective-permute-start.11 = (f32[3,3,32,128]{3,2,1,0:T(8,128)S(1)}, f32[3,3,32,128]{3,2,1,0:T(8,128)S(1)}, u32[]{:S(2)}, u32[]{:S(2)}) collective-permute-start(f32[3,3,32,128]{3,2,1,0:T(8,128)S(1)} %get-tuple-element.32), channel_id=1, source_target_pairs={{4,8},{12,16},{20,24},{28,32},{36,40},{44,48},{52,56},{60,0},{8,4}... | collective-permute-start | bytes 442376 | tf_op jit(solution)/shard_map/ppermute | solution.py:30
  35.8 15.7 %collective-permute-start.7 = (f32[32,4,128]{2,1,0:T(4,128)S(1)}, f32[32,4,128]{2,1,0:T(4,128)S(1)}, u32[]{:S(2)}, u32[]{:S(2)}) collective-permute-start(f32[32,4,128]{2,1,0:T(4,128)S(1)} %get-tuple-element.27), channel_id=1, source_target_pairs={{0,1},{1,0},{2,3},{3,2},{4,5},{5,4},{6,7},{7,6},{8,9},{9,8},{10,11... | collective-permute-start | bytes 196616 | tf_op jit(solution)/shard_map/ppermute | solution.py:461
  35.8 15.7 %collective-permute-start.8 = (f32[32,4,128]{2,1,0:T(4,128)S(1)}, f32[32,4,128]{2,1,0:T(4,128)S(1)}, u32[]{:S(2)}, u32[]{:S(2)}) collective-permute-start(f32[32,4,128]{2,1,0:T(4,128)S(1)} %get-tuple-element.28), channel_id=1, source_target_pairs={{0,2},{1,3},{2,0},{3,1},{4,6},{5,7},{6,4},{7,5},{8,10},{9,11},{10,... | collective-permute-start | bytes 196616 | tf_op jit(solution)/shard_map/ppermute | solution.py:461
  35.8 15.7 %collective-permute-start.9 = (f32[32,4,128]{2,1,0:T(4,128)S(1)}, f32[32,4,128]{2,1,0:T(4,128)S(1)}, u32[]{:S(2)}, u32[]{:S(2)}) collective-permute-start(f32[32,4,128]{2,1,0:T(4,128)S(1)} %get-tuple-element.29), channel_id=1, source_target_pairs={{0,3},{1,2},{2,1},{3,0},{4,7},{5,6},{6,5},{7,4},{8,11},{9,10},{10,... | collective-permute-start | bytes 196616 | tf_op jit(solution)/shard_map/ppermute | solution.py:461
  41.1 13.7 %copy-start.1 = (f32[4096]{0:T(1024)S(1)}, f32[4096]{0:T(1024)}, u32[]{:S(2)}) copy-start(f32[4096]{0:T(1024)} %param.17) | copy-start | bytes 49156
  41.3 10.2 %collective-permute-start.12 = (f32[32,4,128]{2,1,0:T(4,128)S(1)}, f32[32,4,128]{2,1,0:T(4,128)S(1)}, u32[]{:S(2)}, u32[]{:S(2)}) collective-permute-start(f32[32,4,128]{2,1,0:T(4,128)S(1)} %get-tuple-element.34), channel_id=1, source_target_pairs={{0,64},{128,192},{64,0},{192,128},{1,65},{129,193},{65,1},{193,129... | collective-permute-start | bytes 196616 | tf_op jit(solution)/shard_map/ppermute | solution.py:30
  43.4 11.4 %collective-permute-start.13 = (f32[32,4,128]{2,1,0:T(4,128)S(1)}, f32[32,4,128]{2,1,0:T(4,128)S(1)}, u32[]{:S(2)}, u32[]{:S(2)}) collective-permute-start(f32[32,4,128]{2,1,0:T(4,128)S(1)} %get-tuple-element.35), channel_id=1, source_target_pairs={{64,128},{192,0},{128,64},{0,192},{65,129},{193,1},{129,65},{1,193... | collective-permute-start | bytes 196616 | tf_op jit(solution)/shard_map/ppermute | solution.py:30
  56.2 5.5 %collective-permute-start.15 = (f32[4,8,128]{2,1,0:T(8,128)S(1)}, f32[4,8,128]{2,1,0:T(8,128)S(1)}, u32[]{:S(2)}, u32[]{:S(2)}) collective-permute-start(f32[4,8,128]{2,1,0:T(8,128)S(1)} %get-tuple-element.39), channel_id=1, source_target_pairs={{64,128},{192,0},{128,64},{0,192},{65,129},{193,1},{129,65},{1,193... | collective-permute-start | bytes 49160 | tf_op jit(solution)/shard_map/ppermute | solution.py:30
  58.9 3.7 %collective-permute-start.14 = (f32[4,8,128]{2,1,0:T(8,128)S(1)}, f32[4,8,128]{2,1,0:T(8,128)S(1)}, u32[]{:S(2)}, u32[]{:S(2)}) collective-permute-start(f32[4,8,128]{2,1,0:T(8,128)S(1)} %get-tuple-element.39), channel_id=1, source_target_pairs={{0,64},{128,192},{64,0},{192,128},{1,65},{129,193},{65,1},{193,129... | collective-permute-start | bytes 49160 | tf_op jit(solution)/shard_map/ppermute | solution.py:30
  62.6 9.5 %collective-permute-start.17 = (f32[3,4,8,128]{3,2,1,0:T(8,128)S(1)}, f32[3,4,8,128]{3,2,1,0:T(8,128)S(1)}, u32[]{:S(2)}, u32[]{:S(2)}) collective-permute-start(f32[3,4,8,128]{3,2,1,0:T(8,128)S(1)} %pad_maximum_fusion.2.refs_1_), channel_id=1, source_target_pairs={{4,8},{12,16},{20,24},{28,32},{36,40},{44,48},{52,56},{60,0},{8,4}... | collective-permute-start | bytes 147464 | tf_op jit(solution)/shard_map/ppermute | solution.py:30
  62.6 9.5 %collective-permute-start.16 = (f32[3,4,8,128]{3,2,1,0:T(8,128)S(1)}, f32[3,4,8,128]{3,2,1,0:T(8,128)S(1)}, u32[]{:S(2)}, u32[]{:S(2)}) collective-permute-start(f32[3,4,8,128]{3,2,1,0:T(8,128)S(1)} %pad_maximum_fusion.2.refs_1_), channel_id=1, source_target_pairs={{0,4},{8,12},{16,20},{24,28},{32,36},{40,44},{48,52},{56,60},{4,0}... | collective-permute-start | bytes 147464 | tf_op jit(solution)/shard_map/ppermute | solution.py:30
